TPU v7x, 8 devices: a whole 2x2x1 slice. The times are simulated.
8 devices in a mesh: inst: 1 (over z), qy: 2 (over y), qx: 4 (over x, core).
Axes of the slice: x: 2, y: 2, z: 1, core: 2. Of those that a mesh axis runs over, the one named last changes fastest.
Arguments:
- cost: float32 [2097152], P(('inst', 'qy', 'qx'))
- gamma: float32 [2, 6], P('inst')
- beta: float32 [2, 6], P('inst')
Outputs:
- output 1: float32 [2], P('inst')
- output 2: float32 [2, 12], P('inst')
All inputs are finite; a program needn't handle non-finite values.
Results may differ from a plain program's by a relative error of at most 0.001.
Values sent between devices are 32-bit elements.
A program may use at most 1 GiB of HBM per device.

v0:
```python
import jax
import jax.numpy as jnp
from jax import lax
from jax.sharding import PartitionSpec as P

LANE_BITS = 7
LANE_WIDTH = 128


def flip_grid(amplitudes, qubit):
    if qubit < LANE_BITS:
        shift = 2 ** qubit
        position = lax.broadcasted_iota(jnp.int32, (LANE_WIDTH,), 0)
        axis_pos = amplitudes.ndim - 1
    else:
        shift = 2 ** (qubit - LANE_BITS)
        position = lax.broadcasted_iota(jnp.int32, (amplitudes.shape[-2], 1), 0)
        axis_pos = amplitudes.ndim - 2
    upper = (position & shift) != 0
    return jnp.where(upper, jnp.roll(amplitudes, shift, axis=axis_pos), jnp.roll(amplitudes, -shift, axis=axis_pos))


def partner_tables(mesh):
    tables = []
    for axis_name in ('qx', 'qy'):
        width = mesh.shape[axis_name]
        for bit_pos in range(width.bit_length() - 1):
            tables.append((axis_name, [(index, index ^ (1 << bit_pos)) for index in range(width)]))
    return tables


def inverse_step(four_amps, partner, cos_b, sin_b):
    psi_re, psi_im, lam_re, lam_im = four_amps
    term = jnp.sum(lam_re * partner[1] - lam_im * partner[0], axis=(1, 2))
    updated = (cos_b * psi_re - sin_b * partner[1], cos_b * psi_im + sin_b * partner[0], cos_b * lam_re - sin_b * partner[3], cos_b * lam_im + sin_b * partner[2])
    return updated, term


def solution(mesh):
    partners = partner_tables(mesh)
    global_count = len(partners)
    group_axes = ('qy', 'qx')

    def device_fn(cost, gamma, beta):
        local_size = cost.shape[0]
        local_count = local_size.bit_length() - 1
        row_count = local_size // LANE_WIDTH
        num_sets, num_layers = gamma.shape
        start_amp = 2.0 ** (-0.5 * (local_count + global_count))
        cost_grid = cost.reshape(1, row_count, LANE_WIDTH)
        gamma_grid = gamma[:, :, None, None]
        half_cos = jnp.cos(0.5 * beta)[:, :, None, None]
        half_sin = jnp.sin(0.5 * beta)[:, :, None, None]
        psi_re = jnp.full((num_sets, row_count, LANE_WIDTH), start_amp, jnp.float32)
        psi_im = jnp.zeros_like(psi_re)
        phase_saved = []
        for layer in range(num_layers):
            phase = gamma_grid[:, layer] * cost_grid
            cos_p = jnp.cos(phase)
            sin_p = jnp.sin(phase)
            phase_saved.append((cos_p, sin_p))
            psi_re, psi_im = psi_re * cos_p + psi_im * sin_p, psi_im * cos_p - psi_re * sin_p
            cos_b = half_cos[:, layer]
            sin_b = half_sin[:, layer]
            for qubit in range(local_count):
                flip_re = flip_grid(psi_re, qubit)
                flip_im = flip_grid(psi_im, qubit)
                psi_re, psi_im = cos_b * psi_re + sin_b * flip_im, cos_b * psi_im - sin_b * flip_re
            for axis_name, pair_list in partners:
                partner = lax.ppermute(jnp.stack([psi_re, psi_im]), axis_name, pair_list)
                psi_re, psi_im = cos_b * psi_re + sin_b * partner[1], cos_b * psi_im - sin_b * partner[0]
        energy_part = jnp.sum(cost_grid * (psi_re * psi_re + psi_im * psi_im), axis=(1, 2))
        four_amps = (psi_re, psi_im, cost_grid * psi_re, cost_grid * psi_im)
        gamma_grads = [None] * num_layers
        beta_grads = [None] * num_layers
        for layer in reversed(range(num_layers)):
            cos_b = half_cos[:, layer]
            sin_b = half_sin[:, layer]
            beta_term = jnp.zeros((num_sets,), jnp.float32)
            for qubit in range(local_count):
                flips = [flip_grid(amplitudes, qubit) for amplitudes in four_amps]
                four_amps, term = inverse_step(four_amps, flips, cos_b, sin_b)
                beta_term = beta_term + term
            for axis_name, pair_list in partners:
                partner = lax.ppermute(jnp.stack(list(four_amps)), axis_name, pair_list)
                four_amps, term = inverse_step(four_amps, partner, cos_b, sin_b)
                beta_term = beta_term + term
            psi_re, psi_im, lam_re, lam_im = four_amps
            beta_grads[layer] = beta_term
            gamma_grads[layer] = 2.0 * jnp.sum(cost_grid * (lam_re * psi_im - lam_im * psi_re), axis=(1, 2))
            if layer > 0:
                cos_p, sin_p = phase_saved[layer]
                four_amps = (psi_re * cos_p - psi_im * sin_p, psi_im * cos_p + psi_re * sin_p, lam_re * cos_p - lam_im * sin_p, lam_im * cos_p + lam_re * sin_p)
        grad_rows = jnp.stack(gamma_grads + beta_grads, axis=1)
        totals = lax.psum(jnp.concatenate([energy_part[:, None], grad_rows], axis=1), group_axes)
        return totals[:, 0], totals[:, 1:]

    cost_spec = P(('inst', 'qy', 'qx'))
    angle_spec = P('inst', None)
    return jax.shard_map(device_fn, mesh=mesh, in_specs=(cost_spec, angle_spec, angle_spec), out_specs=(P('inst'), angle_spec), check_vma=False)
```

profile of v0, /device:TPU:0, one launch (start us, length us, event | category | flops | bytes accessed | tf_op | source)
XLA Modules:
  0.0 8990.7 jit_solution(9658704552780821828)
XLA Ops:
  2.3 33.0 fusion.69
  49.5 35.7 fusion.231
  95.0 41.0 fusion.237
  471.6 20.7 fusion.285
  500.8 26.9 fusion.291
  536.4 32.5 fusion.293
  627.0 203.5 %fusion.378 = f32[1,2,2048,128]{3,1,2,0:T(2,128)S(1)} fusion(f32[1,2,1536,128]{3,1,2,0:T(2,128)} %get-tuple-element.3646, f32[1,2,512,128]{3,1,2,0:T(2,128)} %get-tuple-element.3648, f32[1,2,512,128]{3,1,2,0:T(2,128)} %get-tuple-element.3649, f32[1,2,1536,128]{3,1,2,0:T(2,128)} %get-tuple-element.3644, f32[1,2,1024,128]{3,1,2,0:T(2,128)} %get-tuple-element.3521, ...), kind=kLoop, calls=%fused_computation.596 | loop fusion | flops 56623104 | bytes 74470168 | tf_op jit(solution)/shard_map/sub | solution.py:68
  830.8 191.5 %fusion.338 = f32[1,2,2048,128]{3,1,2,0:T(2,128)S(1)} fusion(f32[1,2,1536,128]{3,1,2,0:T(2,128)} %get-tuple-element.3652, f32[1,2,512,128]{3,1,2,0:T(2,128)} %get-tuple-element.3656, f32[1,2,512,128]{3,1,2,0:T(2,128)S(1)} %copy-done.538, f32[1,2,1536,128]{3,1,2,0:T(2,128)S(1)} %copy-done.361, f32[1,2,1024,128]{3,1,2,0:T(2,128)} %get-tuple-element.3517, ...), kind=kLoop, calls=%fused_computation.538 | loop fusion | flops 56623104 | bytes 74470168 | tf_op jit(solution)/shard_map/add | solution.py:68
  1039.6 90.9 %collective-permute-done.1 = f32[2,2,2048,128]{3,1,2,0:T(2,128)S(1)} collective-permute-done((f32[2,2,2048,128]{3,1,2,0:T(2,128)S(1)}, f32[2,2,2048,128]{3,1,2,0:T(2,128)S(1)}, u32[]{:S(2)}, u32[]{:S(2)}) %collective-permute-start.1) | collective-permute-done | bytes 4194336 | tf_op jit(solution)/shard_map/ppermute | solution.py:70
  1152.9 74.2 collective-permute-done.2
  1601.7 20.9 fusion.431
  1675.9 27.1 fusion.438
  1711.8 31.5 fusion.439
  1810.8 22.0 fusion.489
  1833.1 38.0 fusion.488
  1871.4 35.1 fusion.487
  1906.7 115.4 %fusion.473 = (f32[1,2,2048,128]{3,1,2,0:T(2,128)}, f32[1,2,2048,128]{3,1,2,0:T(2,128)}) fusion(f32[1,2,2032,128]{3,1,2,0:T(2,128)} %get-tuple-element.3364, f32[1,2,16,128]{3,1,2,0:T(2,128)S(1)} %copy-done.649, f32[1,2,16,128]{3,1,2,0:T(2,128)S(1)} %copy-done.648, f32[1,2,2032,128]{3,1,2,0:T(2,128)} %get-tuple-element.3363, ...), kind=kLoop, calls=%fused_computation.740 | loop fusion | flops 40894464 | bytes 59779880 | tf_op jit(solution)/shard_map/mul | solution.py:68
  2038.5 59.9 broadcast_multiply_fusion.4
  2179.5 91.2 %collective-permute-done.4 = f32[2,2,2048,128]{3,2,1,0:T(8,128)S(1)} collective-permute-done((f32[2,2,2048,128]{3,2,1,0:T(8,128)S(1)}, f32[2,2,2048,128]{3,2,1,0:T(8,128)S(1)}, u32[]{:S(2)}, u32[]{:S(2)}) %collective-permute-start.4) | collective-permute-done | bytes 4194336 | tf_op jit(solution)/shard_map/ppermute | solution.py:70
  2292.3 90.3 %collective-permute-done.5 = f32[2,2,2048,128]{3,1,2,0:T(2,128)S(1)} collective-permute-done((f32[2,2,2048,128]{3,1,2,0:T(2,128)S(1)}, f32[2,2,2048,128]{3,1,2,0:T(2,128)S(1)}, u32[]{:S(2)}, u32[]{:S(2)}) %collective-permute-start.5) | collective-permute-done | bytes 4194336 | tf_op jit(solution)/shard_map/ppermute | solution.py:70
  2838.8 20.8 broadcast_multiply_fusion.3
  2945.5 21.7 fusion.578
  2967.4 21.3 fusion.580
  2988.8 22.3 fusion.582
  3011.3 29.2 fusion.648
  3040.5 30.6 copy_multiply_fusion.1
  3075.9 34.0 fusion.612
  3126.8 91.2 %collective-permute-done.7 = f32[2,2,2048,128]{3,2,1,0:T(8,128)S(1)} collective-permute-done((f32[2,2,2048,128]{3,2,1,0:T(8,128)S(1)}, f32[2,2,2048,128]{3,2,1,0:T(8,128)S(1)}, u32[]{:S(2)}, u32[]{:S(2)}) %collective-permute-start.7) | collective-permute-done | bytes 4194336 | tf_op jit(solution)/shard_map/ppermute | solution.py:70
  3220.3 90.3 %collective-permute-done.8 = f32[2,2,2048,128]{3,2,1,0:T(8,128)S(1)} collective-permute-done((f32[2,2,2048,128]{3,2,1,0:T(8,128)S(1)}, f32[2,2,2048,128]{3,2,1,0:T(8,128)S(1)}, u32[]{:S(2)}, u32[]{:S(2)}) %collective-permute-start.8) | collective-permute-done | bytes 4194336 | tf_op jit(solution)/shard_map/ppermute | solution.py:70
  3410.1 91.2 %collective-permute-done.10 = f32[2,2,2048,128]{3,2,1,0:T(8,128)S(1)} collective-permute-done((f32[2,2,2048,128]{3,2,1,0:T(8,128)S(1)}, f32[2,2,2048,128]{3,2,1,0:T(8,128)S(1)}, u32[]{:S(2)}, u32[]{:S(2)}) %collective-permute-start.10) | collective-permute-done | bytes 4194336 | tf_op jit(solution)/shard_map/ppermute | solution.py:70
  3504.5 90.3 %collective-permute-done.11 = f32[2,2,2048,128]{3,2,1,0:T(8,128)S(1)} collective-permute-done((f32[2,2,2048,128]{3,2,1,0:T(8,128)S(1)}, f32[2,2,2048,128]{3,2,1,0:T(8,128)S(1)}, u32[]{:S(2)}, u32[]{:S(2)}) %collective-permute-start.11) | collective-permute-done | bytes 4194336 | tf_op jit(solution)/shard_map/ppermute | solution.py:70
  3694.7 91.2 %collective-permute-done.13 = f32[2,2,2048,128]{3,2,1,0:T(8,128)S(1)} collective-permute-done((f32[2,2,2048,128]{3,2,1,0:T(8,128)S(1)}, f32[2,2,2048,128]{3,2,1,0:T(8,128)S(1)}, u32[]{:S(2)}, u32[]{:S(2)}) %collective-permute-start.13) | collective-permute-done | bytes 4194336 | tf_op jit(solution)/shard_map/ppermute | solution.py:70
  3789.1 90.3 %collective-permute-done.14 = f32[2,2,2048,128]{3,2,1,0:T(8,128)S(1)} collective-permute-done((f32[2,2,2048,128]{3,2,1,0:T(8,128)S(1)}, f32[2,2,2048,128]{3,2,1,0:T(8,128)S(1)}, u32[]{:S(2)}, u32[]{:S(2)}) %collective-permute-start.14) | collective-permute-done | bytes 4194336 | tf_op jit(solution)/shard_map/ppermute | solution.py:70
  3979.4 91.2 %collective-permute-done.16 = f32[2,2,2048,128]{3,2,1,0:T(8,128)S(1)} collective-permute-done((f32[2,2,2048,128]{3,2,1,0:T(8,128)S(1)}, f32[2,2,2048,128]{3,2,1,0:T(8,128)S(1)}, u32[]{:S(2)}, u32[]{:S(2)}) %collective-permute-start.16) | collective-permute-done | bytes 4194336 | tf_op jit(solution)/shard_map/ppermute | solution.py:70
  4073.7 90.3 %collective-permute-done.17 = f32[2,2,2048,128]{3,2,1,0:T(8,128)S(1)} collective-permute-done((f32[2,2,2048,128]{3,2,1,0:T(8,128)S(1)}, f32[2,2,2048,128]{3,2,1,0:T(8,128)S(1)}, u32[]{:S(2)}, u32[]{:S(2)}) %collective-permute-start.17) | collective-permute-done | bytes 4194336 | tf_op jit(solution)/shard_map/ppermute | solution.py:70
  4566.6 181.0 %collective-permute-done.19 = f32[4,2,2048,128]{3,2,1,0:T(8,128)} collective-permute-done((f32[4,2,2048,128]{3,2,1,0:T(8,128)S(1)}, f32[4,2,2048,128]{3,2,1,0:T(8,128)}, u32[]{:S(2)}, u32[]{:S(2)}) %collective-permute-start.19) | collective-permute-done | bytes 8388640 | tf_op jit(solution)/shard_map/ppermute | solution.py:85
  4758.4 180.3 %collective-permute-done.20 = f32[4,2,2048,128]{3,2,1,0:T(8,128)S(1)} collective-permute-done((f32[4,2,2048,128]{3,2,1,0:T(8,128)S(1)}, f32[4,2,2048,128]{3,2,1,0:T(8,128)S(1)}, u32[]{:S(2)}, u32[]{:S(2)}) %collective-permute-start.20) | collective-permute-done | bytes 8388640 | tf_op jit(solution)/shard_map/ppermute | solution.py:85
  5370.7 181.0 %collective-permute-done.22 = f32[4,2,2048,128]{3,2,1,0:T(8,128)} collective-permute-done((f32[4,2,2048,128]{3,2,1,0:T(8,128)S(1)}, f32[4,2,2048,128]{3,2,1,0:T(8,128)}, u32[]{:S(2)}, u32[]{:S(2)}) %collective-permute-start.22) | collective-permute-done | bytes 8388640 | tf_op jit(solution)/shard_map/ppermute | solution.py:85
  5562.5 180.3 %collective-permute-done.23 = f32[4,2,2048,128]{3,2,1,0:T(8,128)S(1)} collective-permute-done((f32[4,2,2048,128]{3,2,1,0:T(8,128)S(1)}, f32[4,2,2048,128]{3,2,1,0:T(8,128)S(1)}, u32[]{:S(2)}, u32[]{:S(2)}) %collective-permute-start.23) | collective-permute-done | bytes 8388640 | tf_op jit(solution)/shard_map/ppermute | solution.py:85
  6173.8 181.0 %collective-permute-done.25 = f32[4,2,2048,128]{3,2,1,0:T(8,128)} collective-permute-done((f32[4,2,2048,128]{3,2,1,0:T(8,128)S(1)}, f32[4,2,2048,128]{3,2,1,0:T(8,128)}, u32[]{:S(2)}, u32[]{:S(2)}) %collective-permute-start.25) | collective-permute-done | bytes 8388640 | tf_op jit(solution)/shard_map/ppermute | solution.py:85
  6365.6 180.3 %collective-permute-done.26 = f32[4,2,2048,128]{3,2,1,0:T(8,128)S(1)} collective-permute-done((f32[4,2,2048,128]{3,2,1,0:T(8,128)S(1)}, f32[4,2,2048,128]{3,2,1,0:T(8,128)S(1)}, u32[]{:S(2)}, u32[]{:S(2)}) %collective-permute-start.26) | collective-permute-done | bytes 8388640 | tf_op jit(solution)/shard_map/ppermute | solution.py:85
  6977.1 181.0 %collective-permute-done.28 = f32[4,2,2048,128]{3,2,1,0:T(8,128)} collective-permute-done((f32[4,2,2048,128]{3,2,1,0:T(8,128)S(1)}, f32[4,2,2048,128]{3,2,1,0:T(8,128)}, u32[]{:S(2)}, u32[]{:S(2)}) %collective-permute-start.28) | collective-permute-done | bytes 8388640 | tf_op jit(solution)/shard_map/ppermute | solution.py:85
  7168.9 180.3 %collective-permute-done.29 = f32[4,2,2048,128]{3,2,1,0:T(8,128)S(1)} collective-permute-done((f32[4,2,2048,128]{3,2,1,0:T(8,128)S(1)}, f32[4,2,2048,128]{3,2,1,0:T(8,128)S(1)}, u32[]{:S(2)}, u32[]{:S(2)}) %collective-permute-start.29) | collective-permute-done | bytes 8388640 | tf_op jit(solution)/shard_map/ppermute | solution.py:85
  7779.5 181.0 %collective-permute-done.31 = f32[4,2,2048,128]{3,2,1,0:T(8,128)} collective-permute-done((f32[4,2,2048,128]{3,2,1,0:T(8,128)S(1)}, f32[4,2,2048,128]{3,2,1,0:T(8,128)}, u32[]{:S(2)}, u32[]{:S(2)}) %collective-permute-start.31) | collective-permute-done | bytes 8388640 | tf_op jit(solution)/shard_map/ppermute | solution.py:85
  7971.3 180.3 %collective-permute-done.32 = f32[4,2,2048,128]{3,2,1,0:T(8,128)S(1)} collective-permute-done((f32[4,2,2048,128]{3,2,1,0:T(8,128)S(1)}, f32[4,2,2048,128]{3,2,1,0:T(8,128)S(1)}, u32[]{:S(2)}, u32[]{:S(2)}) %collective-permute-start.32) | collective-permute-done | bytes 8388640 | tf_op jit(solution)/shard_map/ppermute | solution.py:85
  8580.1 181.0 %collective-permute-done.34 = f32[4,2,2048,128]{3,2,1,0:T(8,128)} collective-permute-done((f32[4,2,2048,128]{3,2,1,0:T(8,128)S(1)}, f32[4,2,2048,128]{3,2,1,0:T(8,128)}, u32[]{:S(2)}, u32[]{:S(2)}) %collective-permute-start.34) | collective-permute-done | bytes 8388640 | tf_op jit(solution)/shard_map/ppermute | solution.py:85
  8791.5 163.6 %collective-permute-done.35 = f32[4,2,2048,128]{3,2,1,0:T(8,128)} collective-permute-done((f32[4,2,2048,128]{3,2,1,0:T(8,128)}, f32[4,2,2048,128]{3,2,1,0:T(8,128)}, u32[]{:S(2)}, u32[]{:S(2)}) %collective-permute-start.35) | collective-permute-done | bytes 8388640 | tf_op jit(solution)/shard_map/ppermute | solution.py:85
  8966.0 23.2 psum.7
  (3293 shorter events, 4613.7 us)
Async XLA Ops:
  49.5 1177.6 %copy-start.521 = (f32[2]{0:T(128)}, f32[2]{0:T(128)S(1)}, u32[]{:S(2)}) copy-start(f32[2]{0:T(128)S(1)} %get-tuple-element.37) | copy-start | bytes 28
  49.5 1177.6 %copy-start.524 = (f32[2]{0:T(128)}, f32[2]{0:T(128)S(1)}, u32[]{:S(2)}) copy-start(f32[2]{0:T(128)S(1)} %get-tuple-element.3973) | copy-start | bytes 28
  214.9 1183.6 %copy-start.584 = (pred[128]{0:T(512)(128)(4,1)}, pred[128]{0:T(512)(128)(4,1)S(1)}, u32[]{:S(2)}) copy-start(pred[128]{0:T(512)(128)(4,1)S(1)} %get-tuple-element.3986) | copy-start | bytes 388
  214.9 1208.8 %copy-start.571 = (pred[128]{0:T(512)(128)(4,1)}, pred[128]{0:T(512)(128)(4,1)S(1)}, u32[]{:S(2)}) copy-start(pred[128]{0:T(512)(128)(4,1)S(1)} %get-tuple-element.3985) | copy-start | bytes 388
  282.1 548.4 %copy-start.405 = (pred[2048]{0:T(1024)(128)(4,1)}, pred[2048]{0:T(1024)(128)(4,1)S(1)}, u32[]{:S(2)}) copy-start(pred[2048]{0:T(1024)(128)(4,1)S(1)} %get-tuple-element.3987) | copy-start | bytes 6148
  282.1 548.4 %copy-start.416 = (pred[2048]{0:T(1024)(128)(4,1)}, pred[2048]{0:T(1024)(128)(4,1)S(1)}, u32[]{:S(2)}) copy-start(pred[2048]{0:T(1024)(128)(4,1)S(1)} %get-tuple-element.3988) | copy-start | bytes 6148
  329.0 501.6 %copy-start.463 = (pred[2048]{0:T(1024)(128)(4,1)}, pred[2048]{0:T(1024)(128)(4,1)S(1)}, u32[]{:S(2)}) copy-start(pred[2048]{0:T(1024)(128)(4,1)S(1)} %get-tuple-element.3989) | copy-start | bytes 6148
  329.0 501.6 %copy-start.475 = (pred[2048]{0:T(1024)(128)(4,1)}, pred[2048]{0:T(1024)(128)(4,1)S(1)}, u32[]{:S(2)}) copy-start(pred[2048]{0:T(1024)(128)(4,1)S(1)} %get-tuple-element.3990) | copy-start | bytes 6148
  384.6 445.9 %copy-start.393 = (pred[2048]{0:T(1024)(128)(4,1)}, pred[2048]{0:T(1024)(128)(4,1)S(1)}, u32[]{:S(2)}) copy-start(pred[2048]{0:T(1024)(128)(4,1)S(1)} %get-tuple-element.3992) | copy-start | bytes 6148
  384.6 445.9 %copy-start.439 = (pred[2048]{0:T(1024)(128)(4,1)}, pred[2048]{0:T(1024)(128)(4,1)S(1)}, u32[]{:S(2)}) copy-start(pred[2048]{0:T(1024)(128)(4,1)S(1)} %get-tuple-element.3991) | copy-start | bytes 6148
  442.2 388.3 %copy-start.451 = (pred[2048]{0:T(1024)(128)(4,1)}, pred[2048]{0:T(1024)(128)(4,1)S(1)}, u32[]{:S(2)}) copy-start(pred[2048]{0:T(1024)(128)(4,1)S(1)} %get-tuple-element.3994) | copy-start | bytes 6148
  442.2 388.3 %copy-start.487 = (pred[2048]{0:T(1024)(128)(4,1)}, pred[2048]{0:T(1024)(128)(4,1)S(1)}, u32[]{:S(2)}) copy-start(pred[2048]{0:T(1024)(128)(4,1)S(1)} %get-tuple-element.3993) | copy-start | bytes 6148
  1024.5 7.7 collective-permute-start
  1036.7 93.8 %collective-permute-start.1 = (f32[2,2,2048,128]{3,1,2,0:T(2,128)S(1)}, f32[2,2,2048,128]{3,1,2,0:T(2,128)S(1)}, u32[]{:S(2)}, u32[]{:S(2)}) collective-permute-start(f32[2,2,2048,128]{3,1,2,0:T(2,128)S(1)} %pad_maximum_fusion.19), channel_id=1, source_target_pairs={{0,2},{1,3},{2,0},{3,1},{4,6},{5,7},{6,4},{7,5}} | collective-permute-start | bytes 12582920 | tf_op jit(solution)/shard_map/ppermute | solution.py:70
  1135.1 92.1 %collective-permute-start.2 = (f32[2,2,2048,128]{3,1,2,0:T(2,128)S(1)}, f32[2,2,2048,128]{3,1,2,0:T(2,128)S(1)}, u32[]{:S(2)}, u32[]{:S(2)}) collective-permute-start(f32[2,2,2048,128]{3,1,2,0:T(2,128)S(1)} %pad_maximum_fusion.20), channel_id=1, source_target_pairs={{0,4},{4,0},{1,5},{5,1},{2,6},{6,2},{3,7},{7,3}} | collective-permute-start | bytes 12582920 | tf_op jit(solution)/shard_map/ppermute | solution.py:70
  2168.3 7.2 collective-permute-start.3
  2178.0 92.6 %collective-permute-start.4 = (f32[2,2,2048,128]{3,2,1,0:T(8,128)S(1)}, f32[2,2,2048,128]{3,2,1,0:T(8,128)S(1)}, u32[]{:S(2)}, u32[]{:S(2)}) collective-permute-start(f32[2,2,2048,128]{3,2,1,0:T(8,128)S(1)} %pad_maximum_fusion.22), channel_id=1, source_target_pairs={{0,2},{1,3},{2,0},{3,1},{4,6},{5,7},{6,4},{7,5}} | collective-permute-start | bytes 12582920 | tf_op jit(solution)/shard_map/ppermute | solution.py:70
  2290.8 91.8 %collective-permute-start.5 = (f32[2,2,2048,128]{3,1,2,0:T(2,128)S(1)}, f32[2,2,2048,128]{3,1,2,0:T(2,128)S(1)}, u32[]{:S(2)}, u32[]{:S(2)}) collective-permute-start(f32[2,2,2048,128]{3,1,2,0:T(2,128)S(1)} %pad_maximum_fusion.23), channel_id=1, source_target_pairs={{0,4},{4,0},{1,5},{5,1},{2,6},{6,2},{3,7},{7,3}} | collective-permute-start | bytes 12582920 | tf_op jit(solution)/shard_map/ppermute | solution.py:70
  3112.7 7.2 collective-permute-start.6
  3125.3 92.6 %collective-permute-start.7 = (f32[2,2,2048,128]{3,2,1,0:T(8,128)S(1)}, f32[2,2,2048,128]{3,2,1,0:T(8,128)S(1)}, u32[]{:S(2)}, u32[]{:S(2)}) collective-permute-start(f32[2,2,2048,128]{3,2,1,0:T(8,128)S(1)} %pad_maximum_fusion.25), channel_id=1, source_target_pairs={{0,2},{1,3},{2,0},{3,1},{4,6},{5,7},{6,4},{7,5}} | collective-permute-start | bytes 12582920 | tf_op jit(solution)/shard_map/ppermute | solution.py:70
  3218.7 91.8 %collective-permute-start.8 = (f32[2,2,2048,128]{3,2,1,0:T(8,128)S(1)}, f32[2,2,2048,128]{3,2,1,0:T(8,128)S(1)}, u32[]{:S(2)}, u32[]{:S(2)}) collective-permute-start(f32[2,2,2048,128]{3,2,1,0:T(8,128)S(1)} %pad_maximum_fusion.26), channel_id=1, source_target_pairs={{0,4},{4,0},{1,5},{5,1},{2,6},{6,2},{3,7},{7,3}} | collective-permute-start | bytes 12582920 | tf_op jit(solution)/shard_map/ppermute | solution.py:70
  3400.3 7.2 collective-permute-start.9
  3408.6 92.6 %collective-permute-start.10 = (f32[2,2,2048,128]{3,2,1,0:T(8,128)S(1)}, f32[2,2,2048,128]{3,2,1,0:T(8,128)S(1)}, u32[]{:S(2)}, u32[]{:S(2)}) collective-permute-start(f32[2,2,2048,128]{3,2,1,0:T(8,128)S(1)} %pad_maximum_fusion.28), channel_id=1, source_target_pairs={{0,2},{1,3},{2,0},{3,1},{4,6},{5,7},{6,4},{7,5}} | collective-permute-start | bytes 12582920 | tf_op jit(solution)/shard_map/ppermute | solution.py:70
  3503.0 91.8 %collective-permute-start.11 = (f32[2,2,2048,128]{3,2,1,0:T(8,128)S(1)}, f32[2,2,2048,128]{3,2,1,0:T(8,128)S(1)}, u32[]{:S(2)}, u32[]{:S(2)}) collective-permute-start(f32[2,2,2048,128]{3,2,1,0:T(8,128)S(1)} %pad_maximum_fusion.29), channel_id=1, source_target_pairs={{0,4},{4,0},{1,5},{5,1},{2,6},{6,2},{3,7},{7,3}} | collective-permute-start | bytes 12582920 | tf_op jit(solution)/shard_map/ppermute | solution.py:70
  3684.9 7.2 collective-permute-start.12
  3693.3 92.6 %collective-permute-start.13 = (f32[2,2,2048,128]{3,2,1,0:T(8,128)S(1)}, f32[2,2,2048,128]{3,2,1,0:T(8,128)S(1)}, u32[]{:S(2)}, u32[]{:S(2)}) collective-permute-start(f32[2,2,2048,128]{3,2,1,0:T(8,128)S(1)} %pad_maximum_fusion.31), channel_id=1, source_target_pairs={{0,2},{1,3},{2,0},{3,1},{4,6},{5,7},{6,4},{7,5}} | collective-permute-start | bytes 12582920 | tf_op jit(solution)/shard_map/ppermute | solution.py:70
  3787.6 91.8 %collective-permute-start.14 = (f32[2,2,2048,128]{3,2,1,0:T(8,128)S(1)}, f32[2,2,2048,128]{3,2,1,0:T(8,128)S(1)}, u32[]{:S(2)}, u32[]{:S(2)}) collective-permute-start(f32[2,2,2048,128]{3,2,1,0:T(8,128)S(1)} %pad_maximum_fusion.32), channel_id=1, source_target_pairs={{0,4},{4,0},{1,5},{5,1},{2,6},{6,2},{3,7},{7,3}} | collective-permute-start | bytes 12582920 | tf_op jit(solution)/shard_map/ppermute | solution.py:70
  3969.6 7.2 collective-permute-start.15
  3977.9 92.6 %collective-permute-start.16 = (f32[2,2,2048,128]{3,2,1,0:T(8,128)S(1)}, f32[2,2,2048,128]{3,2,1,0:T(8,128)S(1)}, u32[]{:S(2)}, u32[]{:S(2)}) collective-permute-start(f32[2,2,2048,128]{3,2,1,0:T(8,128)S(1)} %pad_maximum_fusion.34), channel_id=1, source_target_pairs={{0,2},{1,3},{2,0},{3,1},{4,6},{5,7},{6,4},{7,5}} | collective-permute-start | bytes 12582920 | tf_op jit(solution)/shard_map/ppermute | solution.py:70
  4072.2 91.8 %collective-permute-start.17 = (f32[2,2,2048,128]{3,2,1,0:T(8,128)S(1)}, f32[2,2,2048,128]{3,2,1,0:T(8,128)S(1)}, u32[]{:S(2)}, u32[]{:S(2)}) collective-permute-start(f32[2,2,2048,128]{3,2,1,0:T(8,128)S(1)} %pad_maximum_fusion.35), channel_id=1, source_target_pairs={{0,4},{4,0},{1,5},{5,1},{2,6},{6,2},{3,7},{7,3}} | collective-permute-start | bytes 12582920 | tf_op jit(solution)/shard_map/ppermute | solution.py:70
  4544.9 13.2 collective-permute-start.18
  4565.1 182.5 %collective-permute-start.19 = (f32[4,2,2048,128]{3,2,1,0:T(8,128)S(1)}, f32[4,2,2048,128]{3,2,1,0:T(8,128)}, u32[]{:S(2)}, u32[]{:S(2)}) collective-permute-start(f32[4,2,2048,128]{3,2,1,0:T(8,128)S(1)} %pad_maximum_fusion.1), channel_id=1, source_target_pairs={{0,2},{1,3},{2,0},{3,1},{4,6},{5,7},{6,4},{7,5}} | collective-permute-start | bytes 25165832 | tf_op jit(solution)/shard_map/ppermute | solution.py:85
  4756.9 181.8 %collective-permute-start.20 = (f32[4,2,2048,128]{3,2,1,0:T(8,128)S(1)}, f32[4,2,2048,128]{3,2,1,0:T(8,128)S(1)}, u32[]{:S(2)}, u32[]{:S(2)}) collective-permute-start(f32[4,2,2048,128]{3,2,1,0:T(8,128)S(1)} %pad_maximum_fusion.2), channel_id=1, source_target_pairs={{0,4},{4,0},{1,5},{5,1},{2,6},{6,2},{3,7},{7,3}} | collective-permute-start | bytes 25165832 | tf_op jit(solution)/shard_map/ppermute | solution.py:85
  5349.0 13.2 collective-permute-start.21
  5369.2 182.5 %collective-permute-start.22 = (f32[4,2,2048,128]{3,2,1,0:T(8,128)S(1)}, f32[4,2,2048,128]{3,2,1,0:T(8,128)}, u32[]{:S(2)}, u32[]{:S(2)}) collective-permute-start(f32[4,2,2048,128]{3,2,1,0:T(8,128)S(1)} %pad_maximum_fusion.4), channel_id=1, source_target_pairs={{0,2},{1,3},{2,0},{3,1},{4,6},{5,7},{6,4},{7,5}} | collective-permute-start | bytes 25165832 | tf_op jit(solution)/shard_map/ppermute | solution.py:85
  5560.9 181.8 %collective-permute-start.23 = (f32[4,2,2048,128]{3,2,1,0:T(8,128)S(1)}, f32[4,2,2048,128]{3,2,1,0:T(8,128)S(1)}, u32[]{:S(2)}, u32[]{:S(2)}) collective-permute-start(f32[4,2,2048,128]{3,2,1,0:T(8,128)S(1)} %pad_maximum_fusion.5), channel_id=1, source_target_pairs={{0,4},{4,0},{1,5},{5,1},{2,6},{6,2},{3,7},{7,3}} | collective-permute-start | bytes 25165832 | tf_op jit(solution)/shard_map/ppermute | solution.py:85
  6152.1 13.2 collective-permute-start.24
  6172.3 182.5 %collective-permute-start.25 = (f32[4,2,2048,128]{3,2,1,0:T(8,128)S(1)}, f32[4,2,2048,128]{3,2,1,0:T(8,128)}, u32[]{:S(2)}, u32[]{:S(2)}) collective-permute-start(f32[4,2,2048,128]{3,2,1,0:T(8,128)S(1)} %pad_maximum_fusion.7), channel_id=1, source_target_pairs={{0,2},{1,3},{2,0},{3,1},{4,6},{5,7},{6,4},{7,5}} | collective-permute-start | bytes 25165832 | tf_op jit(solution)/shard_map/ppermute | solution.py:85
  6364.1 181.8 %collective-permute-start.26 = (f32[4,2,2048,128]{3,2,1,0:T(8,128)S(1)}, f32[4,2,2048,128]{3,2,1,0:T(8,128)S(1)}, u32[]{:S(2)}, u32[]{:S(2)}) collective-permute-start(f32[4,2,2048,128]{3,2,1,0:T(8,128)S(1)} %pad_maximum_fusion.8), channel_id=1, source_target_pairs={{0,4},{4,0},{1,5},{5,1},{2,6},{6,2},{3,7},{7,3}} | collective-permute-start | bytes 25165832 | tf_op jit(solution)/shard_map/ppermute | solution.py:85
  6955.5 13.2 collective-permute-start.27
  6975.7 182.5 %collective-permute-start.28 = (f32[4,2,2048,128]{3,2,1,0:T(8,128)S(1)}, f32[4,2,2048,128]{3,2,1,0:T(8,128)}, u32[]{:S(2)}, u32[]{:S(2)}) collective-permute-start(f32[4,2,2048,128]{3,2,1,0:T(8,128)S(1)} %pad_maximum_fusion.10), channel_id=1, source_target_pairs={{0,2},{1,3},{2,0},{3,1},{4,6},{5,7},{6,4},{7,5}} | collective-permute-start | bytes 25165832 | tf_op jit(solution)/shard_map/ppermute | solution.py:85
  7167.4 181.8 %collective-permute-start.29 = (f32[4,2,2048,128]{3,2,1,0:T(8,128)S(1)}, f32[4,2,2048,128]{3,2,1,0:T(8,128)S(1)}, u32[]{:S(2)}, u32[]{:S(2)}) collective-permute-start(f32[4,2,2048,128]{3,2,1,0:T(8,128)S(1)} %pad_maximum_fusion.11), channel_id=1, source_target_pairs={{0,4},{4,0},{1,5},{5,1},{2,6},{6,2},{3,7},{7,3}} | collective-permute-start | bytes 25165832 | tf_op jit(solution)/shard_map/ppermute | solution.py:85
  7757.8 13.2 collective-permute-start.30
  7778.0 182.5 %collective-permute-start.31 = (f32[4,2,2048,128]{3,2,1,0:T(8,128)S(1)}, f32[4,2,2048,128]{3,2,1,0:T(8,128)}, u32[]{:S(2)}, u32[]{:S(2)}) collective-permute-start(f32[4,2,2048,128]{3,2,1,0:T(8,128)S(1)} %pad_maximum_fusion.13), channel_id=1, source_target_pairs={{0,2},{1,3},{2,0},{3,1},{4,6},{5,7},{6,4},{7,5}} | collective-permute-start | bytes 25165832 | tf_op jit(solution)/shard_map/ppermute | solution.py:85
  7969.7 181.8 %collective-permute-start.32 = (f32[4,2,2048,128]{3,2,1,0:T(8,128)S(1)}, f32[4,2,2048,128]{3,2,1,0:T(8,128)S(1)}, u32[]{:S(2)}, u32[]{:S(2)}) collective-permute-start(f32[4,2,2048,128]{3,2,1,0:T(8,128)S(1)} %pad_maximum_fusion.14), channel_id=1, source_target_pairs={{0,4},{4,0},{1,5},{5,1},{2,6},{6,2},{3,7},{7,3}} | collective-permute-start | bytes 25165832 | tf_op jit(solution)/shard_map/ppermute | solution.py:85
  8557.7 13.2 collective-permute-start.33
  8578.6 182.5 %collective-permute-start.34 = (f32[4,2,2048,128]{3,2,1,0:T(8,128)S(1)}, f32[4,2,2048,128]{3,2,1,0:T(8,128)}, u32[]{:S(2)}, u32[]{:S(2)}) collective-permute-start(f32[4,2,2048,128]{3,2,1,0:T(8,128)S(1)} %pad_maximum_fusion.16), channel_id=1, source_target_pairs={{0,2},{1,3},{2,0},{3,1},{4,6},{5,7},{6,4},{7,5}} | collective-permute-start | bytes 25165832 | tf_op jit(solution)/shard_map/ppermute | solution.py:85
  8773.3 181.7 %collective-permute-start.35 = (f32[4,2,2048,128]{3,2,1,0:T(8,128)}, f32[4,2,2048,128]{3,2,1,0:T(8,128)}, u32[]{:S(2)}, u32[]{:S(2)}) collective-permute-start(f32[4,2,2048,128]{3,2,1,0:T(8,128)} %pad_maximum_fusion.17), channel_id=1, source_target_pairs={{0,4},{4,0},{1,5},{5,1},{2,6},{6,2},{3,7},{7,3}} | collective-permute-start | bytes 25165832 | tf_op jit(solution)/shard_map/ppermute | solution.py:85
  (727 other events, 15991.7 us)
where the time goes:
time: 9000 us; the launch traced here: 8990 us
  other arithmetic  3540 us (39%)
  waiting for transfers between devices  3340 us (37%)
  local copies, waits for them, and re-layouts  2030 us (23%)
    ppermute x18, waiting for transfers between devices, device_fn(): partner = lax.ppermute(jnp.stack(list(four_amps)), axis_name, pair_list)  2230 us
    ppermute x18, waiting for transfers between devices, device_fn(): partner = lax.ppermute(jnp.stack([psi_re, psi_im]), axis_name, pair_list)  1110 us
    reduce_sum x121, other arithmetic, inverse_step(): term = jnp.sum(lam_re * partner[1] - lam_im * partner[0], axis=(1, 2))  1070 us
    slice x955, local copies, waits for them, and re-layouts, flip_grid(): jnp.roll(amplitudes, shift, axis=axis_pos)  1020 us
    add x54, other arithmetic, device_fn(): cos_b * psi_re + sin_b * flip_im  623 us
    sub x56, other arithmetic, device_fn(): cos_b * psi_im - sin_b * flip_re  602 us
    concatenate x139, local copies, waits for them, and re-layouts, flip_grid(): jnp.roll(amplitudes, shift, axis=axis_pos)  471 us
    concatenate x74, local copies, waits for them, and re-layouts, flip_grid(): jnp.roll(amplitudes, -shift, axis=axis_pos)  286 us
  transfers between devices with their start and end apart: 36, of which 36 were waited for; matrix products, arithmetic and copies ran while one was open for 0% of the time, Pallas kernels for 0%

commit v1 on v0

v1 whole, which is shorter than its diff:
```python
import functools
import jax
import jax.numpy as jnp
from jax import lax
from jax.experimental import pallas as pl
from jax.experimental.pallas import tpu as pltpu
from jax.sharding import PartitionSpec as P

F32 = jnp.float32
MESH = pl.DeviceIdType.MESH
STATE = (4, 2, 2, 512, 128)
PIECES = 8


def rot_pair(v, bit_a, bit_b, c, s):
    v = list(v)
    for i in range(len(v)):
        if i & bit_a or i & bit_b:
            continue
        a00, a01, a10, a11 = v[i], v[i | bit_b], v[i | bit_a], v[i | bit_a | bit_b]
        w = c * (a11 - a00) + s * (a01 + a10)
        cw = c * w
        sw = s * w
        v[i], v[i | bit_b], v[i | bit_a], v[i | bit_a | bit_b] = a11 - cw, a01 - sw, a10 - sw, a00 + cw
    return v


def rot_one(v, bit, c, s):
    v = list(v)
    for i in range(len(v)):
        if not i & bit:
            a0, a1 = v[i], v[i | bit]
            v[i], v[i | bit] = c * a0 - s * a1, s * a0 + c * a1
    return v


def rot16(v, c, s):
    return rot_pair(rot_pair(v, 1, 2, c, s), 4, 8, c, s)


def gen16(v):
    sum_lo = [v[4 * h + 1] + v[4 * h + 2] for h in range(4)]
    dif_lo = [v[4 * h] - v[4 * h + 3] for h in range(4)]
    sum_hi = [v[4 + k] + v[8 + k] for k in range(4)]
    dif_hi = [v[k] - v[12 + k] for k in range(4)]
    out = []
    for h in range(4):
        for k in range(4):
            lo = (sum_lo[h], -1) if k == 0 else (sum_lo[h], 1) if k == 3 else (dif_lo[h], 1)
            hi = (sum_hi[k], -1) if h == 0 else (sum_hi[k], 1) if h == 3 else (dif_hi[k], 1)
            if lo[1] > 0:
                out.append(lo[0] + hi[0] if hi[1] > 0 else lo[0] - hi[0])
            else:
                out.append(hi[0] - lo[0] if hi[1] > 0 else -(hi[0] + lo[0]))
    return out


def tree_sum(terms):
    terms = list(terms)
    while len(terms) > 1:
        terms = [terms[i] + terms[i + 1] if i + 1 < len(terms) else terms[i] for i in range(0, len(terms), 2)]
    return terms[0]


def dot_lists(a, b):
    return tree_sum([x * y for x, y in zip(a, b)])


def strided(start):
    return pl.ds(start, 8, stride=8)


def main_kernel(ang, start_ref, trig_ref, cost_ref, out_ref, save_ref, S, R, TB, PB, CB, GB, send_sem, recv_sem, loc_sem):
    inst = lax.axis_index("inst")
    role = lax.axis_index("qy")
    qx = lax.axis_index("qx")
    core = lax.rem(qx, 2)
    partner = (inst, role, qx + 1 - 2 * core)
    other = 1 - core

    barrier = pltpu.get_barrier_semaphore()
    pl.semaphore_signal(barrier, inc=1, device_id=partner, device_id_type=MESH)
    pl.semaphore_wait(barrier, 1)

    def piece(par, j):
        rows = pl.ds(pl.multiple_of(j * 64, 64), 64)
        return pltpu.make_async_remote_copy(
            src_ref=S.at[:, :, other, :, rows, :], dst_ref=R.at[par, :, :, :, rows, :],
            send_sem=send_sem.at[j], recv_sem=recv_sem.at[par, j], device_id=partner, device_id_type=MESH)

    def trig_copy(k):
        return pltpu.make_async_copy(trig_ref.at[lax.rem(k, 2), lax.div(k, 2)], TB, loc_sem.at[0])

    def cost_copy(k):
        return pltpu.make_async_copy(cost_ref.at[lax.rem(k, 2)], CB, loc_sem.at[1])

    def save_copy(k):
        return pltpu.make_async_copy(PB, save_ref.at[k], loc_sem.at[2])

    def load_copy(k):
        return pltpu.make_async_copy(save_ref.at[k], PB, loc_sem.at[3])

    def get16(ref, ri, row):
        return [ref[ri, i >> 2, (i >> 1) & 1, i & 1, pl.ds(row, 8), :] for i in range(16)]

    def put16(ref, ri, row, v):
        for i in range(16):
            ref[ri, i >> 2, (i >> 1) & 1, i & 1, pl.ds(row, 8), :] = v[i]

    def post(v, c, s):
        return rot_pair(v, 2, 4, c, s)

    def pre(v, c, s):
        return rot_one(rot_pair(v, 2, 1, c, s), 8, c, s)

    def block(src, src_idx, idx, c, s):
        ri, nh, u, n0 = idx
        for n4 in range(2):
            for j in range(2):
                pos = [(n4 * 2 + n3) * 128 + j * 64 + k for n3 in range(2) for k in range(8)]
                v = rot16([src[src_idx + (strided(p), slice(None))] for p in pos], c, s)
                for p, x in zip(pos, v):
                    S[ri, nh, u, n0, strided(p), :] = x
        for q in range(4):
            v = rot16([S[ri, nh, u, n0, pl.ds(q * 128 + 8 * k, 8), :] for k in range(16)], c, s)
            t = jnp.transpose(jnp.concatenate(v, axis=0))
            v = rot16([t[8 * k:8 * k + 8, :] for k in range(16)], c, s)
            for k in range(16):
                S[ri, nh, u, n0, pl.ds(q * 128 + 8 * k, 8), :] = v[k]
        for n3 in range(2):
            for j in range(2):
                pos = [(n4 * 2 + n3) * 128 + j * 64 + k for n4 in range(2) for k in range(8)]
                v = rot16([S[ri, nh, u, n0, strided(p), :] for p in pos], c, s)
                for p, x in zip(pos, v):
                    S[ri, nh, u, n0, strided(p), :] = x

    def half(u, par, from_r, c, s):
        def body(b, carry):
            nh = lax.div(b, 2)
            n0 = lax.rem(b, 2)
            ri = lax.rem(lax.div(b, 2), 2)
            nh = lax.div(b, 4)
            if from_r:
                block(R, (par, ri, nh, n0), (ri, nh, u, n0), c, s)
            else:
                block(S, (ri, nh, u, n0), (ri, nh, u, n0), c, s)
            return carry
        lax.fori_loop(0, 16, body, 0)

    def mixer_body(step):
        c, s = ang[0, step], ang[1, step]
        par = lax.rem(step, 2)
        half(core, par, False, c, s)

        def wait(j, carry):
            piece(par, j).wait()
            return carry
        lax.fori_loop(0, PIECES, wait, 0)
        half(other, par, True, c, s)

    def sweep(step, unit, init, send):
        par = lax.rem(step, 2)

        def body(j, carry):
            carry = lax.fori_loop(0, 8, lambda t, cr: unit(pl.multiple_of(j * 64 + t * 8, 8), cr), carry)
            if send:
                @pl.when(j > 0)
                def _():
                    piece(par, j - 1).start()
            return carry
        carry = lax.fori_loop(0, PIECES, body, init)
        if send:
            piece(par, PIECES - 1).start()
        return carry

    def get_trig(which, i, row):
        return TB[which, i >> 2, (i >> 1) & 1, i & 1, pl.ds(row, 8), :]

    def get_cost(i, row):
        return CB[i >> 2, (i >> 1) & 1, i & 1, pl.ds(row, 8), :]

    zero = jnp.zeros((8, 128), F32)

    def forward(step):
        k = step
        c0, s0 = ang[2, step], ang[3, step]
        c1, s1 = ang[0, step], ang[1, step]
        trig_copy(k).wait()

        @pl.when(k > 0)
        def _():
            save_copy(k - 1).wait()

        def unit(keep_before):
            def f(row, carry):
                re = post(get16(S, 0, row), c0, s0)
                im = post(get16(S, 1, row), c0, s0)
                if keep_before:
                    put16(PB, 0, row, re)
                    put16(PB, 1, row, im)
                nre, nim = [], []
                for i in range(16):
                    cs, sn = get_trig(0, i, row), get_trig(1, i, row)
                    nre.append(re[i] * cs + im[i] * sn)
                    nim.append(im[i] * cs - re[i] * sn)
                if not keep_before:
                    put16(PB, 0, row, nre)
                    put16(PB, 1, row, nim)
                put16(S, 0, row, pre(nre, c1, s1))
                put16(S, 1, row, pre(nim, c1, s1))
                return carry
            return f

        @pl.when(role == 0)
        def _():
            sweep(step, unit(False), 0, True)

        @pl.when(role == 1)
        def _():
            sweep(step, unit(True), 0, True)
        save_copy(k).start()

        @pl.when(k < 5)
        def _():
            trig_copy(k + 1).start()

    def generator(bit):
        def row_of(b, held, j, k):
            n4, n3 = (held, b) if bit == 3 else (b, held)
            return (n4 * 2 + n3) * 128 + j * 64 + k

        def body(b, carry):
            nh, u, n0 = lax.div(b, 4), lax.rem(lax.div(b, 2), 2), lax.rem(b, 2)
            for ri in range(2):
                for held in range(2):
                    for j in range(2):
                        pos = [row_of(b, held, j, k) for b in range(2) for k in range(8)]
                        g = gen16([PB[ri, nh, u, n0, strided(p), :] for p in pos])
                        for p, x in zip(pos, g):
                            GB[ri, nh, u, n0, strided(p), :] = x
                for q in range(4):
                    g = gen16([PB[ri, nh, u, n0, pl.ds(q * 128 + 8 * k, 8), :] for k in range(16)])
                    for k in range(16):
                        rows = pl.ds(q * 128 + 8 * k, 8)
                        GB[ri, nh, u, n0, rows, :] = GB[ri, nh, u, n0, rows, :] + g[k]
            return carry
        lax.fori_loop(0, 16, body, 0)

    def add_u(g, v):
        return [g[i] + v[i ^ 2] if i & 2 else g[i] - v[i ^ 2] for i in range(16)]

    def turn(step):
        c0, s0 = ang[2, step], ang[3, step]
        c1, s1 = ang[0, step], ang[1, step]
        save_copy(5).wait()
        cost_copy(0).wait()

        def first(row, carry):
            for ri in range(2):
                put16(PB, ri, row, post(get16(S, ri, row), c0, s0))
            return carry
        sweep(step, first, 0, False)

        @pl.when(role == 1)
        def _():
            generator(4)

        def second(with_beta):
            def f(row, carry):
                acc_e, acc_b = carry
                cst = [get_cost(i, row) for i in range(16)]
                e = []
                for ri in range(2):
                    psi = get16(PB, ri, row)
                    lam = [x * y for x, y in zip(cst, psi)]
                    if with_beta:
                        acc_b = acc_b + dot_lists(lam, add_u(get16(GB, ri, row), psi))
                    else:
                        e.append(dot_lists(lam, psi))
                    put16(S, ri, row, pre(lam, c1, s1))
                if not with_beta:
                    acc_e = acc_e + (e[0] + e[1])
                return acc_e, acc_b
            return f

        @pl.when(role == 0)
        def _():
            acc_e, acc_b = sweep(step, second(False), (zero, zero), True)
            out_ref[0] = acc_e

        @pl.when(role == 1)
        def _():
            acc_e, acc_b = sweep(step, second(True), (zero, zero), True)
            out_ref[12] = acc_b
        load_copy(5).start()
        trig_copy(5).start()
        cost_copy(5).start()

    def backward(step, layer, last):
        c0, s0 = ang[2, step], ang[3, step]
        c1, s1 = (None, None) if last else (ang[0, step], ang[1, step])
        trig_copy(layer).wait()
        cost_copy(layer).wait()
        load_copy(layer).wait()

        def unit(is_role0):
            def f(row, carry):
                acc_g, acc_b = carry
                lre = post(get16(S, 0, row), c0, s0)
                lim = post(get16(S, 1, row), c0, s0)
                if is_role0:
                    for ri, lam in ((0, lre), (1, lim)):
                        psi = get16(PB, ri, row)
                        g = [x + y for x, y in zip(get16(GB, ri, row), gen16(psi))]
                        acc_b = acc_b + dot_lists(lam, g)
                if not (is_role0 and last):
                    nre, nim = [], []
                    for i in range(16):
                        cs, sn = get_trig(0, i, row), get_trig(1, i, row)
                        nre.append(lre[i] * cs - lim[i] * sn)
                        nim.append(lim[i] * cs + lre[i] * sn)
                    if not is_role0:
                        pre_, pim = get16(PB, 0, row), get16(PB, 1, row)
                        cst = [get_cost(i, row) for i in range(16)]
                        acc_g = acc_g + tree_sum(
                            [cst[i] * (nre[i] * pim[i] - nim[i] * pre_[i]) for i in range(16)])
                        if not last:
                            acc_b = acc_b + dot_lists(nre, add_u(get16(GB, 0, row), pre_))
                            acc_b = acc_b + dot_lists(nim, add_u(get16(GB, 1, row), pim))
                    if not last:
                        put16(S, 0, row, pre(nre, c1, s1))
                        put16(S, 1, row, pre(nim, c1, s1))
                return acc_g, acc_b
            return f

        @pl.when(role == 0)
        def _():
            generator(3)
            acc_g, acc_b = sweep(step, unit(True), (zero, zero), not last)
            out_ref[7 + layer] = acc_b

        @pl.when(role == 1)
        def _():
            if not last:
                generator(4)
            acc_g, acc_b = sweep(step, unit(False), (zero, zero), not last)
            out_ref[1 + layer] = acc_g
            if not last:
                out_ref[6 + layer] = acc_b
        if not last:
            load_copy(layer - 1).start()
            trig_copy(layer - 1).start()
            cost_copy(layer - 1).start()

    out_ref[...] = jnp.zeros_like(out_ref)
    init = pltpu.make_async_copy(start_ref, S, loc_sem.at[3])
    init.start()
    trig_copy(0).start()
    cost_copy(0).start()
    init.wait()

    def layer_loop(step, carry):
        @pl.when(step < 6)
        def _():
            forward(step)

        @pl.when(step == 6)
        def _():
            turn(step)

        @pl.when(step > 6)
        def _():
            backward(step, 12 - step, False)
        mixer_body(step)
        return carry
    lax.fori_loop(0, 12, layer_loop, 0)
    backward(12, 0, True)


def trig_kernel(gam, c_ref, o_ref):
    form = pl.program_id(0)
    rows = c_ref.shape[2]
    for sub in range(3):
        g = gam[sub * 2 + form]

        def body(r, carry):
            sl = pl.ds(pl.multiple_of(r * 64, 64), 64)
            x = g * c_ref[0, 0, sl, :]
            q = jnp.round(x * 0.63661977236758134)
            y = x - q * 1.5703125
            y = y - q * 4.837512969970703125e-4
            y = y - q * 7.54978995489188216e-8
            z = y * y
            sn = ((z * -1.9515295891e-4 + 8.3321608736e-3) * z - 1.6666654611e-1) * z * y + y
            cs = ((z * 2.443315711809948e-5 - 1.388731625493765e-3) * z + 4.166664568298827e-2) * (z * z) - 0.5 * z + 1.0
            qi = q.astype(jnp.int32)
            odd = (qi & 1) != 0
            a = jnp.where(odd, cs, sn)
            b = jnp.where(odd, sn, cs)
            o_ref[0, sub, 1, 0, sl, :] = jnp.where((qi & 2) != 0, -a, a)
            o_ref[0, sub, 0, 0, sl, :] = jnp.where(((qi + 1) & 2) != 0, -b, b)
            return carry
        lax.fori_loop(0, rows // 64, body, 0)


def trig_tables(cost, gamma):
    rows = 1024
    blocks = 8192 // rows
    out = pl.pallas_call(
        trig_kernel, grid=(2, blocks),
        in_specs=[pl.BlockSpec(memory_space=pltpu.SMEM), pl.BlockSpec((1, 1, rows, 128), lambda f, b: (f, b, 0, 0))],
        out_specs=pl.BlockSpec((1, 3, 2, 1, rows, 128), lambda f, b: (f, 0, 0, b, 0, 0)),
        out_shape=jax.ShapeDtypeStruct((2, 3, 2, blocks, rows, 128), F32), name="trig",
    )(gamma, cost.reshape(2, blocks, rows, 128))
    return out.reshape((2, 3, 2) + STATE)


def solution(mesh):
    def device_fn(cost, gamma, beta):
        qx = lax.axis_index("qx")
        angle_set = qx // 2
        core = qx % 2
        full = lax.all_gather(cost, ("qy", "qx"), tiled=True).reshape(4, 2, 2, 2, 4, 128, 128)
        form0 = lax.dynamic_index_in_dim(full, core, 1, keepdims=False)
        form1 = jnp.swapaxes(lax.dynamic_index_in_dim(full, core, 2, keepdims=False), -1, -2)
        costs = jnp.stack([form0.reshape(STATE), form1.reshape(STATE)])
        gam = lax.dynamic_index_in_dim(gamma, angle_set, 0, keepdims=False)
        bet = lax.dynamic_index_in_dim(beta, angle_set, 0, keepdims=False)
        trig = trig_tables(costs, gam)
        c, s = jnp.cos(0.5 * bet), jnp.sin(0.5 * bet)
        cc = jnp.concatenate([c, c[::-1], jnp.ones(1, F32)])
        ss = jnp.concatenate([s, -s[::-1], jnp.zeros(1, F32)])
        angles = jnp.stack([cc, ss, jnp.roll(cc, 1), jnp.roll(ss, 1)])
        index = lax.broadcasted_iota(jnp.int32, (2 ** 20 // 128, 128), 0) * 128 + lax.broadcasted_iota(jnp.int32, (2 ** 20 // 128, 128), 1)
        ones = (lax.population_count(index) + core) & 3
        amp = F32(2.0 ** -10.5)
        start = jnp.stack([jnp.where(ones == 0, amp, jnp.where(ones == 2, -amp, 0.0)),
                           jnp.where(ones == 1, amp, jnp.where(ones == 3, -amp, 0.0))]).reshape((2,) + STATE)
        any_space = pl.BlockSpec(memory_space=pl.ANY)
        sums, _ = pl.pallas_call(
            main_kernel,
            out_shape=(jax.ShapeDtypeStruct((16, 8, 128), F32), jax.ShapeDtypeStruct((6, 2) + STATE, F32)),
            in_specs=[pl.BlockSpec(memory_space=pltpu.SMEM), any_space, any_space, any_space],
            out_specs=(pl.BlockSpec(memory_space=pltpu.VMEM), any_space),
            scratch_shapes=[
                pltpu.VMEM((2,) + STATE, F32), pltpu.VMEM((2, 2, 4, 2, 512, 128), F32), pltpu.VMEM((2,) + STATE, F32),
                pltpu.VMEM((2,) + STATE, F32), pltpu.VMEM(STATE, F32), pltpu.VMEM((2,) + STATE, F32),
                pltpu.SemaphoreType.DMA((PIECES,)), pltpu.SemaphoreType.DMA((2, PIECES)), pltpu.SemaphoreType.DMA((4,))],
            compiler_params=pltpu.CompilerParams(collective_id=0, has_side_effects=True, vmem_limit_bytes=60 * 2 ** 20),
            name="chain",
        )(angles, start, trig, costs)
        vec = jnp.sum(sums, axis=(1, 2))[:13]
        vec = vec * jnp.concatenate([jnp.ones(1, F32), jnp.full((6,), 2.0, F32), jnp.ones(6, F32)])
        mine = (jnp.arange(2) == angle_set).astype(F32)[:, None] * vec[None, :]
        totals = lax.psum(mine, ("qy", "qx"))
        return totals[:, 0], totals[:, 1:]

    spec = P("inst", None)
    return jax.shard_map(device_fn, mesh=mesh, in_specs=(P(("inst", "qy", "qx")), spec, spec), out_specs=(P("inst"), spec), check_vma=False)
```

time: 9000 us -> 405 us (0.04)
  other arithmetic: 3540 us -> 25.9 us
  waiting for transfers between devices: 3340 us -> 47.3 us
  local copies, waits for them, and re-layouts: 2030 us -> 15.1 us
  Pallas kernels: 0 us -> 272 us
    ppermute x36 -> x0, waiting for transfers between devices: 3340 us -> none  [the longest x18 2230 us: device_fn(): partner = lax.ppermute(jnp.stack(list(four_amps)), axis_name, pair_list)]
    slice x1081 -> x0, local copies, waits for them, and re-layouts: 1110 us -> none  [the longest x955 1020 us: flip_grid(): jnp.roll(amplitudes, shift, axis=axis_pos)]
    reduce_sum x122 -> x1, other arithmetic: 1080 us -> 1.04 us  [device_fn(): vec = jnp.sum(sums, axis=(1, 2))[:13]]
    add x133 -> x0, other arithmetic: 904 us -> none  [the longest x54 623 us: device_fn(): cos_b * psi_re + sin_b * flip_im]
    sub x111 -> x0, other arithmetic: 775 us -> none  [the longest x56 602 us: device_fn(): cos_b * psi_im - sin_b * flip_re]
    concatenate x214 -> x0, local copies, waits for them, and re-layouts: 757 us -> none  [the longest x139 471 us: flip_grid(): jnp.roll(amplitudes, shift, axis=axis_pos)]
    mul x34 -> x3, other arithmetic: 624 us -> 0.09 us  [the longest x1 0.07 us: device_fn(): mine = (jnp.arange(2) == angle_set).astype(F32)[:, None] * vec[None, :]]
    pallas_call x0 -> x2, Pallas kernels: none -> 272 us  [the longest x1 233 us: device_fn(): pl.pallas_call(main_kernel, out_shape=(jax.ShapeDtypeStruct((16, 8, 128),...]
  transfers between devices with their start and end apart: 36 -> 1, of which waited for: 36 -> 1; matrix products, arithmetic and copies ran while one was open for 0% -> 2% of each run, Pallas kernels for 0% -> 0%
where the time goes in v1:
time: 405 us
  Pallas kernels  272 us (67%)
  waiting for transfers between devices  47.3 us (12%)
  blocking collectives  30.4 us (8%)
  other arithmetic  25.9 us (6%)
  local copies, waits for them, and re-layouts  15.1 us (4%)
  between operations  14.1 us (3%)
    pallas_call x1, Pallas kernels, device_fn(): pl.pallas_call(main_kernel, out_shape=(jax.ShapeDtypeStruct((16, 8, 128),...  233 us
    all_gather x1, waiting for transfers between devices, device_fn(): lax.all_gather(cost, ('qy', 'qx'), tiled=True)  46.6 us
    pallas_call x1, Pallas kernels, trig_tables(): pl.pallas_call(trig_kernel, grid=(2, blocks), in_specs=[pl.BlockSpec(memo...  38.6 us
    psum x1, blocking collectives, device_fn(): totals = lax.psum(mine, ('qy', 'qx'))  30.4 us
    another operation x1, other arithmetic, device_fn(): jnp.stack([jnp.where(ones == 0, amp, jnp.where(ones == 2, -amp, 0.0)), jn...  11.1 us
  transfers between devices with their start and end apart: 1, of which 1 were waited for; matrix products, arithmetic and copies ran while one was open for 2% of the time, Pallas kernels for 0%

profile of v1, /device:TPU:0, one launch (start us, length us, event | category | flops | bytes accessed | tf_op | source)
XLA Modules:
  0.0 404.6 jit_solution(8548840498253592779)
XLA Ops:
  7.2 0.0 all-gather.2.cloned.1.call-start
  7.2 0.7 all-gather.2.cloned.1.call-update
  7.9 1.2 cosine_bitcast_fusion
  9.1 0.1 rev.6
  9.2 0.1 rev.7
  9.3 0.1 maximum_bitcast_fusion
  9.4 0.1 maximum_bitcast_fusion.1
  9.5 0.5 pad_maximum_fusion.3.ang
  10.1 4.3 %select_select_fusion.1 = (f32[1,4,2,2,512,128]{5,4,3,2,1,0:T(8,128)}, f32[1,4,2,2,512,128]{5,4,3,2,1,0:T(8,128)}) fusion(s32[]{:T(128)S(6)} %select_n.70, s32[4,2,2,512]{3,2,1,0:T(2,128)S(1)} %add_multiply_fusion), kind=kLoop, calls=%fused_computation.5 | loop fusion | flops 12582912 | bytes 8421380 | tf_op jit(solution)/shard_map/jit(_where)/select_n | solution.py:437
  14.3 46.6 %all-gather.2.cloned.1.call-done = f32[2097152]{0:T(1024)} async-done(((f32[262144]{0:T(1024)}), f32[2097152]{0:T(1024)}) %all-gather.2.cloned.1.call-update) | async-done | bytes 8388624 | tf_op jit(solution)/shard_map/all_gather | solution.py:423
  61.0 0.0 copy-start
  61.0 5.0 %constant_dynamic-slice_fusion = f32[4,1,2,2,4,128,128]{6,5,4,3,2,1,0:T(8,128)} fusion(f32[4,2,2,2,4,128,128]{6,5,4,3,2,1,0:T(8,128)} %bitcast.29, s32[]{:T(128)S(6)} %select_n.75), kind=kLoop, calls=%fused_computation.15 | loop fusion | bytes 8388612 | tf_op jit(solution)/shard_map/jit(dynamic_index_in_dim)/dynamic_slice | solution.py:424
  66.0 1.2 copy-done
  67.1 2.2 dynamic-slice_bitcast_fusion
  69.4 5.2 %copy.8 = f32[4,2,2,4,128,128]{5,4,3,2,1,0:T(8,128)} copy(f32[4,2,2,4,128,128]{4,5,3,2,1,0:T(8,128)} %dynamic-slice_bitcast_fusion) | data formatting | bytes 8388608 | tf_op jit(solution)/shard_map/transpose | solution.py:425
  74.6 7.5 %pad_maximum_fusion.1.c_ref = f32[2,8,1024,128]{3,2,1,0:T(8,128)} fusion(f32[1,8,1024,128]{3,2,1,0:T(8,128)} %bitcast.27, f32[1,8,1024,128]{3,2,1,0:T(8,128)} %bitcast.25), kind=kLoop, calls=%fused_computation.1 | loop fusion | flops 2097152 | bytes 16777216 | tf_op jit(solution)/shard_map/stack | solution.py:426
  82.1 38.6 %trig.1 = f32[2,3,2,8,1024,128]{5,4,3,2,1,0:T(8,128)} custom-call(f32[6]{0:T(128)} %get-tuple-element.12.gam, f32[2,8,1024,128]{3,2,1,0:T(8,128)} %pad_maximum_fusion.1.c_ref), custom_call_target="tpu_custom_call" | custom-call | tf_op jit(solution)/shard_map/trig/pallas_call | solution.py:409
  120.7 11.1 %pad_maximum_fusion = (f32[2,4,2,2,512,128]{5,4,3,2,1,0:T(8,128)}, f32[2,4,2,2,512,128]{5,4,3,2,1,0:T(8,128)}) fusion(f32[1,4,2,2,512,128]{5,4,3,2,1,0:T(8,128)} %get-tuple-element.5, f32[1,4,2,2,512,128]{5,4,3,2,1,0:T(8,128)} %get-tuple-element.4, f32[1,4,2,2,512,128]{5,4,3,2,1,0:T(8,128)} %bitcast.28, f32[1,4,2,2,512,128]{5,4,3,2,1,0:T(8,128)} %bitcast.26), kind=kLoop, calls=%fused_computation | loop fusion | flops 4194304 | bytes 33554432 | tf_op jit(solution)/shard_map/stack | solution.py:437
  131.8 0.0 copy-start.1
  131.8 233.1 %chain.1 = (f32[16,8,128]{2,1,0:T(8,128)}, f32[6,2,4,2,2,512,128]{6,5,4,3,2,1,0:T(8,128)}) custom-call(f32[4,13]{1,0:T(4,128)} %pad_maximum_fusion.3.ang, f32[2,4,2,2,512,128]{5,4,3,2,1,0:T(8,128)} %get-tuple-element.13.start_ref, f32[2,3,2,4,2,2,512,128]{7,6,5,4,3,2,1,0:T(8,128)} %bitcast.24, f32[2,4,2,2,512,128]{5,4,3,2,1,0:T(8,128)} %get-tuple-element.14.cost_ref), custom_call_target="tpu_custom_call" | custom-call | tf_op jit(solution)/shard_map/chain/pallas_call | solution.py:440
  365.0 1.0 reduce_sum.9
  366.0 0.0 copy-done.1
  366.0 0.1 broadcast_multiply_fusion
  366.1 30.4 %psum.7 = f32[2,13]{1,0:T(2,128)S(1)} all-reduce(f32[2,13]{1,0:T(2,128)S(1)} %broadcast_multiply_fusion), channel_id=1, replica_groups=mesh['inst'=1,'qy'=2,'qx'=4] {'qy','qx'}, use_global_device_ids=true, to_apply=%region_1.2 | all-reduce | flops 26 | bytes 208 | tf_op jit(solution)/shard_map/psum | solution.py:455
  396.5 0.6 slice_reduce_fusion
  397.1 0.6 slice.19
  (4 shorter events, 0.0 us)
Async XLA Ops:
  7.2 53.8 %all-gather.2.cloned.1.call-start = ((), (), s32[]{:S(2)}) async-start(), calls=%async_computation | async-start | bytes 9437184 | tf_op jit(solution)/shard_map/all_gather | solution.py:423
  61.0 6.2 %copy-start = (f32[2097152]{0:T(1024)S(1)}, f32[2097152]{0:T(1024)}, u32[]{:S(2)}) copy-start(f32[2097152]{0:T(1024)} %all-gather.2.cloned.1.call-done) | copy-start | bytes 25165828
  131.8 234.2 %copy-start.1 = (f32[13]{0:T(128)S(1)}, f32[13]{0:T(128)}, u32[]{:S(2)}) copy-start(f32[13]{0:T(128)} %constant.68.clone.1) | copy-start | bytes 160
Sparse Core Ops, SparseCore 0:
  9.8 51.1 all-gather.1

commit v2 on v1

--- a/solution.py
+++ b/solution.py
@@ -70,7 +70,7 @@
     return pl.ds(start, 8, stride=8)
 
 
-def main_kernel(ang, start_ref, trig_ref, cost_ref, out_ref, save_ref, S, R, TB, PB, CB, GB, send_sem, recv_sem, loc_sem):
+def main_kernel(ang, start_ref, trig_ref, cost_ref, out_ref, save_ref, S, R, TB, PB, CB, GB, acc_ref, all_ref, send_sem, recv_sem, loc_sem, fin_send, fin_recv):
     inst = lax.axis_index("inst")
     role = lax.axis_index("qy")
     qx = lax.axis_index("qx")
@@ -78,9 +78,15 @@
     partner = (inst, role, qx + 1 - 2 * core)
     other = 1 - core
 
+    me = role * 4 + qx
+
+    def peer(k):
+        return (inst, jnp.bitwise_xor(role, k // 4), jnp.bitwise_xor(qx, k % 4))
+
     barrier = pltpu.get_barrier_semaphore()
-    pl.semaphore_signal(barrier, inc=1, device_id=partner, device_id_type=MESH)
-    pl.semaphore_wait(barrier, 1)
+    for k in range(1, 8):
+        pl.semaphore_signal(barrier, inc=1, device_id=peer(k), device_id_type=MESH)
+    pl.semaphore_wait(barrier, 7)
 
     def piece(par, j):
         rows = pl.ds(pl.multiple_of(j * 64, 64), 64)
@@ -286,12 +292,12 @@
         @pl.when(role == 0)
         def _():
             acc_e, acc_b = sweep(step, second(False), (zero, zero), True)
-            out_ref[0] = acc_e
+            acc_ref[0] = acc_e
 
         @pl.when(role == 1)
         def _():
             acc_e, acc_b = sweep(step, second(True), (zero, zero), True)
-            out_ref[12] = acc_b
+            acc_ref[12] = acc_b
         load_copy(5).start()
         trig_copy(5).start()
         cost_copy(5).start()
@@ -337,22 +343,22 @@
         def _():
             generator(3)
             acc_g, acc_b = sweep(step, unit(True), (zero, zero), not last)
-            out_ref[7 + layer] = acc_b
+            acc_ref[7 + layer] = acc_b
 
         @pl.when(role == 1)
         def _():
             if not last:
                 generator(4)
             acc_g, acc_b = sweep(step, unit(False), (zero, zero), not last)
-            out_ref[1 + layer] = acc_g
+            acc_ref[1 + layer] = acc_g
             if not last:
-                out_ref[6 + layer] = acc_b
+                acc_ref[6 + layer] = acc_b
         if not last:
             load_copy(layer - 1).start()
             trig_copy(layer - 1).start()
             cost_copy(layer - 1).start()
 
-    out_ref[...] = jnp.zeros_like(out_ref)
+    acc_ref[...] = jnp.zeros_like(acc_ref)
     init = pltpu.make_async_copy(start_ref, S, loc_sem.at[3])
     init.start()
     trig_copy(0).start()
@@ -376,43 +382,146 @@
     lax.fori_loop(0, 12, layer_loop, 0)
     backward(12, 0, True)
 
-
-def trig_kernel(gam, c_ref, o_ref):
-    form = pl.program_id(0)
-    rows = c_ref.shape[2]
-    for sub in range(3):
-        g = gam[sub * 2 + form]
+    all_ref[me] = jnp.sum(acc_ref[...], axis=1)
+    copies = [pltpu.make_async_remote_copy(
+        src_ref=all_ref.at[me], dst_ref=all_ref.at[me], send_sem=fin_send.at[k], recv_sem=fin_recv.at[k],
+        device_id=peer(k), device_id_type=MESH) for k in range(1, 8)]
+    for cp in copies:
+        cp.start()
+    for cp in copies:
+        cp.wait()
+    for k in range(2):
+        total = (all_ref[2 * k] + all_ref[2 * k + 1]) + (all_ref[2 * k + 4] + all_ref[2 * k + 5])
+        out_ref[k] = jnp.broadcast_to(jnp.sum(total, axis=1, keepdims=True), (16, 128))
+
+
+def sincos(x):
+    q = jnp.round(x * 0.63661977236758134)
+    y = x - q * 1.5703125
+    y = y - q * 4.83826794896619e-4
+    z = y * y
+    sn = ((z * -1.9515295891e-4 + 8.3321608736e-3) * z - 1.6666654611e-1) * z * y + y
+    cs = ((z * 2.443315711809948e-5 - 1.388731625493765e-3) * z + 4.166664568298827e-2) * (z * z) - 0.5 * z + 1.0
+    qi = q.astype(jnp.int32)
+    odd = (qi & 1) != 0
+    a = jnp.where(odd, cs, sn)
+    b = jnp.where(odd, sn, cs)
+    return jnp.where(((qi + 1) & 2) != 0, -b, b), jnp.where((qi & 2) != 0, -a, a)
+
+
+def prep_kernel(gam, own_ref, cost_ref, trig_ref, F, E, G, T, own_sem, sx, sy, sf, se, rx, ry, rd, re_, out_sem, cost_sem):
+    inst = lax.axis_index("inst")
+    qy = lax.axis_index("qy")
+    qx = lax.axis_index("qx")
+    core = lax.rem(qx, 2)
+    xpos = lax.div(qx, 2)
+    me = qy * 2 + xpos
+    xnbr, ynbr, dnbr = qy * 2 + 1 - xpos, (1 - qy) * 2 + xpos, (1 - qy) * 2 + 1 - xpos
+    x_dev = (inst, qy, (1 - xpos) * 2 + core)
+    y_dev = (inst, 1 - qy, qx)
+    p_dev = (inst, qy, xpos * 2 + 1 - core)
+
+    own = pltpu.make_async_copy(own_ref, F.at[me], own_sem)
+    own.start()
+    barrier = pltpu.get_barrier_semaphore()
+    for dev in (x_dev, y_dev, p_dev):
+        pl.semaphore_signal(barrier, inc=1, device_id=dev, device_id_type=MESH)
+    pl.semaphore_wait(barrier, 3)
+    own.wait()
+
+    def push(blk, p, ssem, rsem, dev):
+        return pltpu.make_async_remote_copy(
+            src_ref=F.at[blk, p // 2, p % 2], dst_ref=F.at[blk, p // 2, p % 2],
+            send_sem=ssem.at[p], recv_sem=rsem.at[p], device_id=dev, device_id_type=MESH)
+
+    def give(blk, n0):
+        return pltpu.make_async_remote_copy(
+            src_ref=F.at[blk, 1 - core, n0], dst_ref=E.at[blk, n0],
+            send_sem=se.at[blk, n0], recv_sem=re_.at[blk, n0], device_id=p_dev, device_id_type=MESH)
+
+    def flush(form, slot, blk, u, n0):
+        return pltpu.make_async_copy(T.at[slot], trig_ref.at[form, :, :, blk, u, n0], out_sem.at[slot])
+
+    for p in range(4):
+        push(me, p, sx, rx, x_dev).start()
+        push(me, p, sy, ry, y_dev).start()
+
+    def tables(form, slot, src, blk, u, n0, busy):
+        if busy:
+            flush(form, slot, blk, u, n0).wait()
 
         def body(r, carry):
-            sl = pl.ds(pl.multiple_of(r * 64, 64), 64)
-            x = g * c_ref[0, 0, sl, :]
-            q = jnp.round(x * 0.63661977236758134)
-            y = x - q * 1.5703125
-            y = y - q * 4.837512969970703125e-4
-            y = y - q * 7.54978995489188216e-8
-            z = y * y
-            sn = ((z * -1.9515295891e-4 + 8.3321608736e-3) * z - 1.6666654611e-1) * z * y + y
-            cs = ((z * 2.443315711809948e-5 - 1.388731625493765e-3) * z + 4.166664568298827e-2) * (z * z) - 0.5 * z + 1.0
-            qi = q.astype(jnp.int32)
-            odd = (qi & 1) != 0
-            a = jnp.where(odd, cs, sn)
-            b = jnp.where(odd, sn, cs)
-            o_ref[0, sub, 1, 0, sl, :] = jnp.where((qi & 2) != 0, -a, a)
-            o_ref[0, sub, 0, 0, sl, :] = jnp.where(((qi + 1) & 2) != 0, -b, b)
-            return carry
-        lax.fori_loop(0, rows // 64, body, 0)
-
-
-def trig_tables(cost, gamma):
-    rows = 1024
-    blocks = 8192 // rows
-    out = pl.pallas_call(
-        trig_kernel, grid=(2, blocks),
-        in_specs=[pl.BlockSpec(memory_space=pltpu.SMEM), pl.BlockSpec((1, 1, rows, 128), lambda f, b: (f, b, 0, 0))],
-        out_specs=pl.BlockSpec((1, 3, 2, 1, rows, 128), lambda f, b: (f, 0, 0, b, 0, 0)),
-        out_shape=jax.ShapeDtypeStruct((2, 3, 2, blocks, rows, 128), F32), name="trig",
-    )(gamma, cost.reshape(2, blocks, rows, 128))
-    return out.reshape((2, 3, 2) + STATE)
+            rows = pl.ds(pl.multiple_of(r * 32, 32), 32)
+            c = src[rows, :]
+            for sub in range(3):
+                cs, sn = sincos(gam[sub * 2 + form] * c)
+                T[slot, sub, 0, rows, :] = cs
+                T[slot, sub, 1, rows, :] = sn
+            return carry
+        lax.fori_loop(0, 16, body, 0)
+        flush(form, slot, blk, u, n0).start()
+
+    def first_form(blk, p, slot, busy):
+        u, n0 = p // 2, p % 2
+
+        @pl.when(core != u)
+        def _():
+            give(blk, n0).start()
+        tables(0, slot, F.at[blk, u, n0], blk, u, n0, busy)
+
+    def second_form(blk):
+        def one(t, carry):
+            u, n0 = lax.div(t, 2), lax.rem(t, 2)
+
+            @pl.when(u != core)
+            def _():
+                give(blk, n0).wait()
+
+            def turn_over(q, cr):
+                rows = pl.ds(pl.multiple_of(q * 128, 128), 128)
+
+                @pl.when(u == core)
+                def _():
+                    G[blk, u, n0, rows, :] = jnp.transpose(F[blk, u, n0, rows, :])
+
+                @pl.when(u != core)
+                def _():
+                    G[blk, u, n0, rows, :] = jnp.transpose(E[blk, n0, rows, :])
+                return cr
+            lax.fori_loop(0, 4, turn_over, 0)
+            tables(1, lax.rem(t, 2), G.at[blk, u, n0], blk, u, n0, True)
+            return carry
+        lax.fori_loop(0, 4, one, 0)
+
+    for p in range(4):
+        first_form(me, p, p % 2, p >= 2)
+    second_form(me)
+    for p in range(4):
+        push(xnbr, p, sx, rx, x_dev).wait_recv()
+        if p < 2:
+            push(xnbr, p, sf, rd, y_dev).start()
+        first_form(xnbr, p, 0, True)
+        push(ynbr, p, sy, ry, y_dev).wait_recv()
+        if p >= 2:
+            push(ynbr, p, sf, rd, x_dev).start()
+        first_form(ynbr, p, 1, True)
+    second_form(xnbr)
+    second_form(ynbr)
+    for p in (0, 2, 1, 3):
+        push(dnbr, p, sf, rd, x_dev).wait_recv()
+        first_form(dnbr, p, p // 2, True)
+    second_form(dnbr)
+    outs = [pltpu.make_async_copy(src, cost_ref.at[f], cost_sem.at[f]) for f, src in ((0, F), (1, G))]
+    for cp in outs:
+        cp.start()
+    for p in range(4):
+        push(me, p, sx, rx, x_dev).wait_send()
+        push(me, p, sy, ry, y_dev).wait_send()
+        push(me, p, sf, rd, x_dev).wait_send()
+    for slot in range(2):
+        flush(0, slot, 0, 0, 0).wait()
+    for cp in outs:
+        cp.wait()
 
 
 def solution(mesh):
@@ -420,13 +529,21 @@
         qx = lax.axis_index("qx")
         angle_set = qx // 2
         core = qx % 2
-        full = lax.all_gather(cost, ("qy", "qx"), tiled=True).reshape(4, 2, 2, 2, 4, 128, 128)
-        form0 = lax.dynamic_index_in_dim(full, core, 1, keepdims=False)
-        form1 = jnp.swapaxes(lax.dynamic_index_in_dim(full, core, 2, keepdims=False), -1, -2)
-        costs = jnp.stack([form0.reshape(STATE), form1.reshape(STATE)])
         gam = lax.dynamic_index_in_dim(gamma, angle_set, 0, keepdims=False)
         bet = lax.dynamic_index_in_dim(beta, angle_set, 0, keepdims=False)
-        trig = trig_tables(costs, gam)
+        any_space = pl.BlockSpec(memory_space=pl.ANY)
+        smem = pl.BlockSpec(memory_space=pltpu.SMEM)
+        dma = pltpu.SemaphoreType.DMA
+        costs, trig = pl.pallas_call(
+            prep_kernel,
+            out_shape=(jax.ShapeDtypeStruct((2,) + STATE, F32), jax.ShapeDtypeStruct((2, 3, 2) + STATE, F32)),
+            in_specs=[smem, any_space], out_specs=(any_space, any_space),
+            scratch_shapes=[
+                pltpu.VMEM(STATE, F32), pltpu.VMEM((4, 2, 512, 128), F32), pltpu.VMEM(STATE, F32), pltpu.VMEM((2, 3, 2, 512, 128), F32),
+                dma, dma((4,)), dma((4,)), dma((4,)), dma((4, 2)), dma((4,)), dma((4,)), dma((4,)), dma((4, 2)), dma((2,)), dma((2,))],
+            compiler_params=pltpu.CompilerParams(collective_id=1, has_side_effects=True, vmem_limit_bytes=40 * 2 ** 20),
+            name="prep",
+        )(gam, cost.reshape(2, 2, 512, 128))
         c, s = jnp.cos(0.5 * bet), jnp.sin(0.5 * bet)
         cc = jnp.concatenate([c, c[::-1], jnp.ones(1, F32)])
         ss = jnp.concatenate([s, -s[::-1], jnp.zeros(1, F32)])
@@ -436,23 +553,20 @@
         amp = F32(2.0 ** -10.5)
         start = jnp.stack([jnp.where(ones == 0, amp, jnp.where(ones == 2, -amp, 0.0)),
                            jnp.where(ones == 1, amp, jnp.where(ones == 3, -amp, 0.0))]).reshape((2,) + STATE)
-        any_space = pl.BlockSpec(memory_space=pl.ANY)
         sums, _ = pl.pallas_call(
             main_kernel,
-            out_shape=(jax.ShapeDtypeStruct((16, 8, 128), F32), jax.ShapeDtypeStruct((6, 2) + STATE, F32)),
-            in_specs=[pl.BlockSpec(memory_space=pltpu.SMEM), any_space, any_space, any_space],
+            out_shape=(jax.ShapeDtypeStruct((2, 16, 128), F32), jax.ShapeDtypeStruct((6, 2) + STATE, F32)),
+            in_specs=[smem, any_space, any_space, any_space],
             out_specs=(pl.BlockSpec(memory_space=pltpu.VMEM), any_space),
             scratch_shapes=[
                 pltpu.VMEM((2,) + STATE, F32), pltpu.VMEM((2, 2, 4, 2, 512, 128), F32), pltpu.VMEM((2,) + STATE, F32),
                 pltpu.VMEM((2,) + STATE, F32), pltpu.VMEM(STATE, F32), pltpu.VMEM((2,) + STATE, F32),
-                pltpu.SemaphoreType.DMA((PIECES,)), pltpu.SemaphoreType.DMA((2, PIECES)), pltpu.SemaphoreType.DMA((4,))],
+                pltpu.VMEM((16, 8, 128), F32), pltpu.VMEM((8, 16, 128), F32),
+                dma((PIECES,)), dma((2, PIECES)), dma((4,)), dma((8,)), dma((8,))],
             compiler_params=pltpu.CompilerParams(collective_id=0, has_side_effects=True, vmem_limit_bytes=60 * 2 ** 20),
             name="chain",
         )(angles, start, trig, costs)
-        vec = jnp.sum(sums, axis=(1, 2))[:13]
-        vec = vec * jnp.concatenate([jnp.ones(1, F32), jnp.full((6,), 2.0, F32), jnp.ones(6, F32)])
-        mine = (jnp.arange(2) == angle_set).astype(F32)[:, None] * vec[None, :]
-        totals = lax.psum(mine, ("qy", "qx"))
+        totals = sums[:, :13, 0] * jnp.concatenate([jnp.ones(1, F32), jnp.full((6,), 2.0, F32), jnp.ones(6, F32)])
         return totals[:, 0], totals[:, 1:]
 
     spec = P("inst", None)

time: 405 us -> 315 us (0.78)
  waiting for transfers between devices: 47.3 us -> 0 us
  blocking collectives: 30.4 us -> 0 us
  Pallas kernels: 272 us -> 301 us
  other arithmetic: 25.9 us -> 7.28 us
  between operations: 14.1 us -> 0.7 us
  local copies, waits for them, and re-layouts: 15.1 us -> 5.45 us
    all_gather x1 -> x0, waiting for transfers between devices: 46.6 us -> none  [device_fn(): lax.all_gather(cost, ('qy', 'qx'), tiled=True)]
    psum x1 -> x0, blocking collectives: 30.4 us -> none  [device_fn(): totals = lax.psum(mine, ('qy', 'qx'))]
    pallas_call x2, Pallas kernels: 272 us -> 301 us  [the longest x1 246 us: device_fn(): pl.pallas_call(main_kernel, out_shape=(jax.ShapeDtypeStruct((2, 16, 128),...]
    another operation x1 -> x0, other arithmetic: 7.48 us -> none  [device_fn(): costs = jnp.stack([form0.reshape(STATE), form1.reshape(STATE)])]
    transpose x2 -> x0, local copies, waits for them, and re-layouts: 7.44 us -> none  [device_fn(): jnp.swapaxes(lax.dynamic_index_in_dim(full, core, 2, keepdims=False), -1,...]
    another operation x1, other arithmetic: 11.1 us -> 4.01 us  [device_fn(): jnp.stack([jnp.where(ones == 0, amp, jnp.where(ones == 2, -amp, 0.0)), jn...]
    dynamic_slice x1 -> x0, local copies, waits for them, and re-layouts: 4.97 us -> none  [device_fn(): form0 = lax.dynamic_index_in_dim(full, core, 1, keepdims=False)]
  transfers between devices with their start and end apart: 1 -> 0, of which waited for: 1 -> 0; matrix products, arithmetic and copies ran while one was open for 2% -> 0% of each run, Pallas kernels for 0% -> 0%
where the time goes in v2:
time: 315 us
  Pallas kernels  301 us (96%)
  other arithmetic  7.28 us (2%)
  local copies, waits for them, and re-layouts  5.45 us (2%)
    pallas_call x1, Pallas kernels, device_fn(): pl.pallas_call(main_kernel, out_shape=(jax.ShapeDtypeStruct((2, 16, 128),...  246 us
    pallas_call x1, Pallas kernels, device_fn(): pl.pallas_call(prep_kernel, out_shape=(jax.ShapeDtypeStruct((2,) + STATE,...  55.5 us

profile of v2, /device:TPU:0, one launch (start us, length us, event | category | flops | bytes accessed | tf_op | source)
XLA Modules:
  0.0 314.9 jit_solution(16958956877271283255)
XLA Ops:
  0.7 0.7 cosine_bitcast_fusion
  1.4 0.1 rev.6
  1.5 0.1 maximum_bitcast_fusion
  1.6 0.1 rev.7
  1.7 0.1 maximum_bitcast_fusion.1
  1.8 0.5 pad_maximum_fusion.1.ang
  2.3 1.8 select_select_fusion.1
  4.1 0.0 copy-start.1
  4.1 4.0 %pad_maximum_fusion.start_ref = f32[2,4,2,2,512,128]{5,4,3,2,1,0:T(8,128)} fusion(f32[1,4,2,2,512,128]{5,4,3,2,1,0:T(8,128)S(1)} %get-tuple-element.9, f32[1,4,2,2,512,128]{5,4,3,2,1,0:T(8,128)S(1)} %get-tuple-element.8), kind=kLoop, calls=%fused_computation | loop fusion | flops 2097152 | bytes 16777216 | tf_op jit(solution)/shard_map/stack | solution.py:554
  8.2 0.0 copy-done.1
  8.2 55.5 %prep.1 = (f32[2,4,2,2,512,128]{5,4,3,2,1,0:T(8,128)S(1)}, f32[2,3,2,4,2,2,512,128]{7,6,5,4,3,2,1,0:T(8,128)}) custom-call(f32[6]{0:T(128)S(1)} %get-tuple-element.16.gam, f32[2,2,512,128]{3,2,1,0:T(8,128)S(1)} %bitcast.15), custom_call_target="tpu_custom_call" | custom-call | tf_op jit(solution)/shard_map/prep/pallas_call | solution.py:537
  63.7 0.0 copy-start
  63.7 3.2 %copy-done = f32[2,4,2,2,512,128]{5,4,3,2,1,0:T(8,128)} copy-done((f32[2,4,2,2,512,128]{5,4,3,2,1,0:T(8,128)}, f32[2,4,2,2,512,128]{5,4,3,2,1,0:T(8,128)S(1)}, u32[]{:S(2)}) %copy-start) | copy-done | bytes 8388632
  66.8 0.0 copy-start.2
  66.8 246.0 %chain.1 = (f32[2,16,128]{2,1,0:T(8,128)}, f32[6,2,4,2,2,512,128]{6,5,4,3,2,1,0:T(8,128)}) custom-call(f32[4,13]{1,0:T(4,128)} %pad_maximum_fusion.1.ang, f32[2,4,2,2,512,128]{5,4,3,2,1,0:T(8,128)} %pad_maximum_fusion.start_ref, f32[2,3,2,4,2,2,512,128]{7,6,5,4,3,2,1,0:T(8,128)} %get-tuple-element.5.trig_ref, f32[2,4,2,2,512,128]{5,4,3,2,1,0:T(8,128)} %copy-done), custom_call_target="tpu_custom_call" | custom-call | tf_op jit(solution)/shard_map/chain/pallas_call | solution.py:556
  312.8 0.8 slice_reduce_fusion
  313.6 0.0 copy-done.2
  313.6 0.6 slice_reduce_fusion.1
  314.3 0.6 slice.19
  (3 shorter events, 0.0 us)
Async XLA Ops:
  4.1 4.0 %copy-start.1 = (f32[262144]{0:T(1024)S(1)}, f32[262144]{0:T(1024)}, u32[]{:S(2)}) copy-start(f32[262144]{0:T(1024)} %param.3) | copy-start | bytes 3145732
  63.7 3.2 %copy-start = (f32[2,4,2,2,512,128]{5,4,3,2,1,0:T(8,128)}, f32[2,4,2,2,512,128]{5,4,3,2,1,0:T(8,128)S(1)}, u32[]{:S(2)}) copy-start(f32[2,4,2,2,512,128]{5,4,3,2,1,0:T(8,128)S(1)} %get-tuple-element.6.cost_ref) | copy-start | bytes 25165828
  66.8 246.8 %copy-start.2 = (f32[13]{0:T(128)S(1)}, f32[13]{0:T(128)}, u32[]{:S(2)}) copy-start(f32[13]{0:T(128)} %constant.61.clone.1) | copy-start | bytes 160

commit v3 on v2

--- a/solution.py
+++ b/solution.py
@@ -8,7 +8,8 @@
 
 F32 = jnp.float32
 MESH = pl.DeviceIdType.MESH
-STATE = (4, 2, 2, 512, 128)
+AMPS = (16, 512, 128)
+PAIRS = (32, 512, 128)
 PIECES = 8
 
 
@@ -70,15 +71,19 @@
     return pl.ds(start, 8, stride=8)
 
 
-def main_kernel(ang, start_ref, trig_ref, cost_ref, out_ref, save_ref, S, R, TB, PB, CB, GB, acc_ref, all_ref, send_sem, recv_sem, loc_sem, fin_send, fin_recv):
+def spread(x):
+    return jnp.full((8, 128), x, F32)
+
+
+def main_kernel(beta_ref, trig_ref, cost_ref, out_ref, save_ref, B, TB, PB, CB, GB, ang, acc_ref, all_ref,
+                send_sem, recv_sem, loc_sem, fin_send, fin_recv):
     inst = lax.axis_index("inst")
     role = lax.axis_index("qy")
     qx = lax.axis_index("qx")
     core = lax.rem(qx, 2)
     partner = (inst, role, qx + 1 - 2 * core)
-    other = 1 - core
-
     me = role * 4 + qx
+    base = (2 + 16 * core, 18 - 16 * core)
 
     def peer(k):
         return (inst, jnp.bitwise_xor(role, k // 4), jnp.bitwise_xor(qx, k % 4))
@@ -91,7 +96,7 @@
     def piece(par, j):
         rows = pl.ds(pl.multiple_of(j * 64, 64), 64)
         return pltpu.make_async_remote_copy(
-            src_ref=S.at[:, :, other, :, rows, :], dst_ref=R.at[par, :, :, :, rows, :],
+            src_ref=B.at[pl.ds(18, 16), rows, :], dst_ref=B.at[pl.ds(36 + 16 * par, 16), rows, :],
             send_sem=send_sem.at[j], recv_sem=recv_sem.at[par, j], device_id=partner, device_id_type=MESH)
 
     def trig_copy(k):
@@ -106,12 +111,37 @@
     def load_copy(k):
         return pltpu.make_async_copy(save_ref.at[k], PB, loc_sem.at[3])
 
+    trig_copy(0).start()
+    cost_copy(0).start()
+
+    def state_at(i, ri):
+        return base[(i >> 1) & 1] + (ri * 8 + (i >> 2) * 2 + (i & 1))
+
+    def amp_at(i):
+        return ((i >> 1) & 1) * 8 + (i >> 2) * 2 + (i & 1)
+
+    def pair_at(i, ri):
+        return ((i >> 1) & 1) * 16 + ri * 8 + (i >> 2) * 2 + (i & 1)
+
+    def get_state(ri, row):
+        return [B[state_at(i, ri), pl.ds(row, 8), :] for i in range(16)]
+
+    def put_state(ri, row, v):
+        for i in range(16):
+            B[state_at(i, ri), pl.ds(row, 8), :] = v[i]
+
     def get16(ref, ri, row):
-        return [ref[ri, i >> 2, (i >> 1) & 1, i & 1, pl.ds(row, 8), :] for i in range(16)]
+        return [ref[pair_at(i, ri), pl.ds(row, 8), :] for i in range(16)]
 
     def put16(ref, ri, row, v):
         for i in range(16):
-            ref[ri, i >> 2, (i >> 1) & 1, i & 1, pl.ds(row, 8), :] = v[i]
+            ref[pair_at(i, ri), pl.ds(row, 8), :] = v[i]
+
+    def get_trig(which, i, row):
+        return TB[which, amp_at(i), pl.ds(row, 8), :]
+
+    def get_cost(i, row):
+        return CB[amp_at(i), pl.ds(row, 8), :]
 
     def post(v, c, s):
         return rot_pair(v, 2, 4, c, s)
@@ -119,56 +149,74 @@
     def pre(v, c, s):
         return rot_one(rot_pair(v, 2, 1, c, s), 8, c, s)
 
-    def block(src, src_idx, idx, c, s):
-        ri, nh, u, n0 = idx
-        for n4 in range(2):
-            for j in range(2):
-                pos = [(n4 * 2 + n3) * 128 + j * 64 + k for n3 in range(2) for k in range(8)]
-                v = rot16([src[src_idx + (strided(p), slice(None))] for p in pos], c, s)
-                for p, x in zip(pos, v):
-                    S[ri, nh, u, n0, strided(p), :] = x
-        for q in range(4):
-            v = rot16([S[ri, nh, u, n0, pl.ds(q * 128 + 8 * k, 8), :] for k in range(16)], c, s)
-            t = jnp.transpose(jnp.concatenate(v, axis=0))
-            v = rot16([t[8 * k:8 * k + 8, :] for k in range(16)], c, s)
-            for k in range(16):
-                S[ri, nh, u, n0, pl.ds(q * 128 + 8 * k, 8), :] = v[k]
-        for n3 in range(2):
-            for j in range(2):
-                pos = [(n4 * 2 + n3) * 128 + j * 64 + k for n4 in range(2) for k in range(8)]
-                v = rot16([S[ri, nh, u, n0, strided(p), :] for p in pos], c, s)
-                for p, x in zip(pos, v):
-                    S[ri, nh, u, n0, strided(p), :] = x
-
-    def half(u, par, from_r, c, s):
-        def body(b, carry):
-            nh = lax.div(b, 2)
-            n0 = lax.rem(b, 2)
-            ri = lax.rem(lax.div(b, 2), 2)
-            nh = lax.div(b, 4)
-            if from_r:
-                block(R, (par, ri, nh, n0), (ri, nh, u, n0), c, s)
-            else:
-                block(S, (ri, nh, u, n0), (ri, nh, u, n0), c, s)
-            return carry
-        lax.fori_loop(0, 16, body, 0)
-
-    def mixer_body(step):
+    angle_set = lax.div(qx, 2)
+    for k in range(6):
+        cs, sn = sincos(spread(beta_ref[angle_set, k] * 0.5))
+        ang[0, k], ang[1, k] = cs, sn
+        ang[0, 11 - k], ang[1, 11 - k] = cs, -sn
+    ang[0, 12], ang[1, 12] = spread(1.0), spread(0.0)
+
+    low = lax.population_count(
+        lax.broadcasted_iota(jnp.int32, (8, 128), 0) * 128 + lax.broadcasted_iota(jnp.int32, (8, 128), 1))
+
+    def fill(b, carry):
+        u, nh, n0 = lax.div(b, 8), lax.rem(lax.div(b, 2), 4), lax.rem(b, 2)
+        ones = (low + (core + u + lax.div(nh, 2) + lax.rem(nh, 2) + n0)) & 3
+        amp = F32(2.0 ** -10.5)
+        re = jnp.where(ones == 0, amp, jnp.where(ones == 2, -amp, 0.0))
+        im = jnp.where(ones == 1, amp, jnp.where(ones == 3, -amp, 0.0))
+        turns = [(re, im), (-im, re), (-re, -im), (im, -re)]
+        slot = 2 + lax.rem(core + u, 2) * 16 + nh * 2 + n0
+        for t in range(64):
+            x, y = turns[bin(t).count("1") % 4]
+            B[slot, 8 * t:8 * t + 8, :] = x
+            B[slot + 8, 8 * t:8 * t + 8, :] = y
+        return carry
+    lax.fori_loop(0, 16, fill, 0)
+
+    def body_loop(step):
         c, s = ang[0, step], ang[1, step]
         par = lax.rem(step, 2)
-        half(core, par, False, c, s)
-
-        def wait(j, carry):
-            piece(par, j).wait()
+
+        def one(t, carry):
+            @pl.when(t == 16)
+            def _():
+                def wait(j, cr):
+                    piece(par, j).wait()
+                    return cr
+                lax.fori_loop(0, PIECES, wait, 0)
+            src = t + 2 + lax.rem(lax.div(t, 16), 2) * (18 + 16 * par)
+            first, second, third = t + 2, t + 1, t
+            for n4 in range(2):
+                for h in range(2):
+                    rows = [pl.ds((n4 * 2 + n3) * 128 + h * 64 + 8 * k, 8) for n3 in range(2) for k in range(8)]
+                    v = rot16([B[src, r, :] for r in rows], c, s)
+                    for r, x in zip(rows, v):
+                        B[first, r, :] = x
+            for q in range(4):
+                v = rot16([B[second, strided(q * 128 + h * 64 + k), :] for h in range(2) for k in range(8)], c, s)
+                t_ = jnp.transpose(jnp.concatenate(v, axis=0))
+                v = rot16([t_[8 * k:8 * k + 8, :] for k in range(16)], c, s)
+                for k in range(16):
+                    B[second, pl.ds(q * 128 + 8 * k, 8), :] = v[k]
+            for n3 in range(2):
+                for h in range(2):
+                    at = [((n4 * 2 + n3) * 128 + h * 64, k) for n4 in range(2) for k in range(8)]
+                    v = rot16([B[third, strided(r + k), :] for r, k in at], c, s)
+                    for (r, k), x in zip(at, v):
+                        B[third, pl.ds(r + 8 * k, 8), :] = x
             return carry
-        lax.fori_loop(0, PIECES, wait, 0)
-        half(other, par, True, c, s)
+        lax.fori_loop(0, 34, one, 0)
 
     def sweep(step, unit, init, send):
         par = lax.rem(step, 2)
 
         def body(j, carry):
-            carry = lax.fori_loop(0, 8, lambda t, cr: unit(pl.multiple_of(j * 64 + t * 8, 8), cr), carry)
+            def two(t, cr):
+                for k in range(2):
+                    cr = unit(pl.multiple_of(j * 64 + t * 16 + k * 8, 8), cr)
+                return cr
+            carry = lax.fori_loop(0, 4, two, carry)
             if send:
                 @pl.when(j > 0)
                 def _():
@@ -179,17 +227,14 @@
             piece(par, PIECES - 1).start()
         return carry
 
-    def get_trig(which, i, row):
-        return TB[which, i >> 2, (i >> 1) & 1, i & 1, pl.ds(row, 8), :]
-
-    def get_cost(i, row):
-        return CB[i >> 2, (i >> 1) & 1, i & 1, pl.ds(row, 8), :]
-
     zero = jnp.zeros((8, 128), F32)
+
+    def before(step):
+        return lax.rem(step + 12, 13)
 
     def forward(step):
         k = step
-        c0, s0 = ang[2, step], ang[3, step]
+        c0, s0 = ang[0, before(step)], ang[1, before(step)]
         c1, s1 = ang[0, step], ang[1, step]
         trig_copy(k).wait()
 
@@ -199,8 +244,8 @@
 
         def unit(keep_before):
             def f(row, carry):
-                re = post(get16(S, 0, row), c0, s0)
-                im = post(get16(S, 1, row), c0, s0)
+                re = post(get_state(0, row), c0, s0)
+                im = post(get_state(1, row), c0, s0)
                 if keep_before:
                     put16(PB, 0, row, re)
                     put16(PB, 1, row, im)
@@ -212,8 +257,8 @@
                 if not keep_before:
                     put16(PB, 0, row, nre)
                     put16(PB, 1, row, nim)
-                put16(S, 0, row, pre(nre, c1, s1))
-                put16(S, 1, row, pre(nim, c1, s1))
+                put_state(0, row, pre(nre, c1, s1))
+                put_state(1, row, pre(nim, c1, s1))
                 return carry
             return f
 
@@ -231,24 +276,24 @@
             trig_copy(k + 1).start()
 
     def generator(bit):
-        def row_of(b, held, j, k):
+        def row_of(b, held, h, k):
             n4, n3 = (held, b) if bit == 3 else (b, held)
-            return (n4 * 2 + n3) * 128 + j * 64 + k
-
-        def body(b, carry):
-            nh, u, n0 = lax.div(b, 4), lax.rem(lax.div(b, 2), 2), lax.rem(b, 2)
+            return (n4 * 2 + n3) * 128 + h * 64 + k
+
+        def body(t, carry):
             for ri in range(2):
+                b = t + 16 * ri
+                for q in range(4):
+                    g = gen16([PB[b, strided(q * 128 + h * 64 + k), :] for h in range(2) for k in range(8)])
+                    for k in range(16):
+                        GB[b, pl.ds(q * 128 + 8 * k, 8), :] = g[k]
                 for held in range(2):
-                    for j in range(2):
-                        pos = [row_of(b, held, j, k) for b in range(2) for k in range(8)]
-                        g = gen16([PB[ri, nh, u, n0, strided(p), :] for p in pos])
-                        for p, x in zip(pos, g):
-                            GB[ri, nh, u, n0, strided(p), :] = x
-                for q in range(4):
-                    g = gen16([PB[ri, nh, u, n0, pl.ds(q * 128 + 8 * k, 8), :] for k in range(16)])
-                    for k in range(16):
-                        rows = pl.ds(q * 128 + 8 * k, 8)
-                        GB[ri, nh, u, n0, rows, :] = GB[ri, nh, u, n0, rows, :] + g[k]
+                    for h in range(2):
+                        g = gen16([PB[b, pl.ds(row_of(e, held, h, 8 * k), 8), :] for e in range(2) for k in range(8)])
+                        g = [x + GB[b, strided(row_of(e, held, h, k)), :] for x, (e, k) in
+                             zip(g, [(e, k) for e in range(2) for k in range(8)])]
+                        for x, (e, k) in zip(g, [(e, k) for e in range(2) for k in range(8)]):
+                            GB[b, pl.ds(row_of(e, held, h, 8 * k), 8), :] = x
             return carry
         lax.fori_loop(0, 16, body, 0)
 
@@ -256,14 +301,14 @@
         return [g[i] + v[i ^ 2] if i & 2 else g[i] - v[i ^ 2] for i in range(16)]
 
     def turn(step):
-        c0, s0 = ang[2, step], ang[3, step]
+        c0, s0 = ang[0, step - 1], ang[1, step - 1]
         c1, s1 = ang[0, step], ang[1, step]
         save_copy(5).wait()
         cost_copy(0).wait()
 
         def first(row, carry):
             for ri in range(2):
-                put16(PB, ri, row, post(get16(S, ri, row), c0, s0))
+                put16(PB, ri, row, post(get_state(ri, row), c0, s0))
             return carry
         sweep(step, first, 0, False)
 
@@ -283,7 +328,7 @@
                         acc_b = acc_b + dot_lists(lam, add_u(get16(GB, ri, row), psi))
                     else:
                         e.append(dot_lists(lam, psi))
-                    put16(S, ri, row, pre(lam, c1, s1))
+                    put_state(ri, row, pre(lam, c1, s1))
                 if not with_beta:
                     acc_e = acc_e + (e[0] + e[1])
                 return acc_e, acc_b
@@ -303,7 +348,7 @@
         cost_copy(5).start()
 
     def backward(step, layer, last):
-        c0, s0 = ang[2, step], ang[3, step]
+        c0, s0 = ang[0, step - 1], ang[1, step - 1]
         c1, s1 = (None, None) if last else (ang[0, step], ang[1, step])
         trig_copy(layer).wait()
         cost_copy(layer).wait()
@@ -312,8 +357,8 @@
         def unit(is_role0):
             def f(row, carry):
                 acc_g, acc_b = carry
-                lre = post(get16(S, 0, row), c0, s0)
-                lim = post(get16(S, 1, row), c0, s0)
+                lre = post(get_state(0, row), c0, s0)
+                lim = post(get_state(1, row), c0, s0)
                 if is_role0:
                     for ri, lam in ((0, lre), (1, lim)):
                         psi = get16(PB, ri, row)
@@ -334,8 +379,8 @@
                             acc_b = acc_b + dot_lists(nre, add_u(get16(GB, 0, row), pre_))
                             acc_b = acc_b + dot_lists(nim, add_u(get16(GB, 1, row), pim))
                     if not last:
-                        put16(S, 0, row, pre(nre, c1, s1))
-                        put16(S, 1, row, pre(nim, c1, s1))
+                        put_state(0, row, pre(nre, c1, s1))
+                        put_state(1, row, pre(nim, c1, s1))
                 return acc_g, acc_b
             return f
 
@@ -359,11 +404,6 @@
             cost_copy(layer - 1).start()
 
     acc_ref[...] = jnp.zeros_like(acc_ref)
-    init = pltpu.make_async_copy(start_ref, S, loc_sem.at[3])
-    init.start()
-    trig_copy(0).start()
-    cost_copy(0).start()
-    init.wait()
 
     def layer_loop(step, carry):
         @pl.when(step < 6)
@@ -377,7 +417,7 @@
         @pl.when(step > 6)
         def _():
             backward(step, 12 - step, False)
-        mixer_body(step)
+        body_loop(step)
         return carry
     lax.fori_loop(0, 12, layer_loop, 0)
     backward(12, 0, True)
@@ -440,7 +480,11 @@
             send_sem=se.at[blk, n0], recv_sem=re_.at[blk, n0], device_id=p_dev, device_id_type=MESH)
 
     def flush(form, slot, blk, u, n0):
-        return pltpu.make_async_copy(T.at[slot], trig_ref.at[form, :, :, blk, u, n0], out_sem.at[slot])
+        return pltpu.make_async_copy(T.at[slot], trig_ref.at[form, :, :, u * 8 + blk * 2 + n0], out_sem.at[slot])
+
+    def keep(form, blk, u, n0):
+        at = u * 8 + blk * 2 + n0
+        return pltpu.make_async_copy((F, G)[form].at[blk, u, n0], cost_ref.at[form, at], cost_sem.at[form, at])
 
     for p in range(4):
         push(me, p, sx, rx, x_dev).start()
@@ -454,12 +498,13 @@
             rows = pl.ds(pl.multiple_of(r * 32, 32), 32)
             c = src[rows, :]
             for sub in range(3):
-                cs, sn = sincos(gam[sub * 2 + form] * c)
+                cs, sn = sincos(gam[xpos, sub * 2 + form] * c)
                 T[slot, sub, 0, rows, :] = cs
                 T[slot, sub, 1, rows, :] = sn
             return carry
         lax.fori_loop(0, 16, body, 0)
         flush(form, slot, blk, u, n0).start()
+        keep(form, blk, u, n0).start()
 
     def first_form(blk, p, slot, busy):
         u, n0 = p // 2, p % 2
@@ -477,18 +522,21 @@
             def _():
                 give(blk, n0).wait()
 
-            def turn_over(q, cr):
-                rows = pl.ds(pl.multiple_of(q * 128, 128), 128)
-
-                @pl.when(u == core)
-                def _():
-                    G[blk, u, n0, rows, :] = jnp.transpose(F[blk, u, n0, rows, :])
-
-                @pl.when(u != core)
-                def _():
-                    G[blk, u, n0, rows, :] = jnp.transpose(E[blk, n0, rows, :])
-                return cr
-            lax.fori_loop(0, 4, turn_over, 0)
+            def turn_over(src):
+                for q in range(4):
+                    x = jnp.concatenate([src[strided(q * 128 + h * 64 + k), :] for h in range(2) for k in range(8)], axis=0)
+                    x = jnp.transpose(x)
+                    for h in range(2):
+                        for k in range(8):
+                            G[blk, u, n0, strided(q * 128 + h * 64 + k), :] = x[h * 64 + k * 8:h * 64 + k * 8 + 8, :]
+
+            @pl.when(u == core)
+            def _():
+                turn_over(F.at[blk, core, n0])
+
+            @pl.when(u != core)
+            def _():
+                turn_over(E.at[blk, n0])
             tables(1, lax.rem(t, 2), G.at[blk, u, n0], blk, u, n0, True)
             return carry
         lax.fori_loop(0, 4, one, 0)
@@ -511,61 +559,48 @@
         push(dnbr, p, sf, rd, x_dev).wait_recv()
         first_form(dnbr, p, p // 2, True)
     second_form(dnbr)
-    outs = [pltpu.make_async_copy(src, cost_ref.at[f], cost_sem.at[f]) for f, src in ((0, F), (1, G))]
-    for cp in outs:
-        cp.start()
     for p in range(4):
         push(me, p, sx, rx, x_dev).wait_send()
         push(me, p, sy, ry, y_dev).wait_send()
         push(me, p, sf, rd, x_dev).wait_send()
     for slot in range(2):
         flush(0, slot, 0, 0, 0).wait()
-    for cp in outs:
-        cp.wait()
+
+    def kept(t, carry):
+        for form in range(2):
+            keep(form, lax.div(t, 4), lax.div(lax.rem(t, 4), 2), lax.rem(t, 2)).wait()
+        return carry
+    lax.fori_loop(0, 16, kept, 0)
 
 
 def solution(mesh):
     def device_fn(cost, gamma, beta):
-        qx = lax.axis_index("qx")
-        angle_set = qx // 2
-        core = qx % 2
-        gam = lax.dynamic_index_in_dim(gamma, angle_set, 0, keepdims=False)
-        bet = lax.dynamic_index_in_dim(beta, angle_set, 0, keepdims=False)
         any_space = pl.BlockSpec(memory_space=pl.ANY)
         smem = pl.BlockSpec(memory_space=pltpu.SMEM)
         dma = pltpu.SemaphoreType.DMA
+        vmem = pltpu.VMEM
         costs, trig = pl.pallas_call(
             prep_kernel,
-            out_shape=(jax.ShapeDtypeStruct((2,) + STATE, F32), jax.ShapeDtypeStruct((2, 3, 2) + STATE, F32)),
+            out_shape=(jax.ShapeDtypeStruct((2,) + AMPS, F32), jax.ShapeDtypeStruct((2, 3, 2) + AMPS, F32)),
             in_specs=[smem, any_space], out_specs=(any_space, any_space),
             scratch_shapes=[
-                pltpu.VMEM(STATE, F32), pltpu.VMEM((4, 2, 512, 128), F32), pltpu.VMEM(STATE, F32), pltpu.VMEM((2, 3, 2, 512, 128), F32),
-                dma, dma((4,)), dma((4,)), dma((4,)), dma((4, 2)), dma((4,)), dma((4,)), dma((4,)), dma((4, 2)), dma((2,)), dma((2,))],
+                vmem((4, 2, 2, 512, 128), F32), vmem((4, 2, 512, 128), F32), vmem((4, 2, 2, 512, 128), F32), vmem((2, 3, 2, 512, 128), F32),
+                dma, dma((4,)), dma((4,)), dma((4,)), dma((4, 2)), dma((4,)), dma((4,)), dma((4,)), dma((4, 2)), dma((2,)), dma((2, 16))],
             compiler_params=pltpu.CompilerParams(collective_id=1, has_side_effects=True, vmem_limit_bytes=40 * 2 ** 20),
             name="prep",
-        )(gam, cost.reshape(2, 2, 512, 128))
-        c, s = jnp.cos(0.5 * bet), jnp.sin(0.5 * bet)
-        cc = jnp.concatenate([c, c[::-1], jnp.ones(1, F32)])
-        ss = jnp.concatenate([s, -s[::-1], jnp.zeros(1, F32)])
-        angles = jnp.stack([cc, ss, jnp.roll(cc, 1), jnp.roll(ss, 1)])
-        index = lax.broadcasted_iota(jnp.int32, (2 ** 20 // 128, 128), 0) * 128 + lax.broadcasted_iota(jnp.int32, (2 ** 20 // 128, 128), 1)
-        ones = (lax.population_count(index) + core) & 3
-        amp = F32(2.0 ** -10.5)
-        start = jnp.stack([jnp.where(ones == 0, amp, jnp.where(ones == 2, -amp, 0.0)),
-                           jnp.where(ones == 1, amp, jnp.where(ones == 3, -amp, 0.0))]).reshape((2,) + STATE)
+        )(gamma, cost.reshape(2, 2, 512, 128))
         sums, _ = pl.pallas_call(
             main_kernel,
-            out_shape=(jax.ShapeDtypeStruct((2, 16, 128), F32), jax.ShapeDtypeStruct((6, 2) + STATE, F32)),
-            in_specs=[smem, any_space, any_space, any_space],
+            out_shape=(jax.ShapeDtypeStruct((2, 16, 128), F32), jax.ShapeDtypeStruct((6,) + PAIRS, F32)),
+            in_specs=[smem, any_space, any_space],
             out_specs=(pl.BlockSpec(memory_space=pltpu.VMEM), any_space),
             scratch_shapes=[
-                pltpu.VMEM((2,) + STATE, F32), pltpu.VMEM((2, 2, 4, 2, 512, 128), F32), pltpu.VMEM((2,) + STATE, F32),
-                pltpu.VMEM((2,) + STATE, F32), pltpu.VMEM(STATE, F32), pltpu.VMEM((2,) + STATE, F32),
-                pltpu.VMEM((16, 8, 128), F32), pltpu.VMEM((8, 16, 128), F32),
+                vmem((68, 512, 128), F32), vmem((2,) + AMPS, F32), vmem(PAIRS, F32), vmem(AMPS, F32), vmem(PAIRS, F32),
+                vmem((2, 13, 8, 128), F32), vmem((16, 8, 128), F32), vmem((8, 16, 128), F32),
                 dma((PIECES,)), dma((2, PIECES)), dma((4,)), dma((8,)), dma((8,))],
             compiler_params=pltpu.CompilerParams(collective_id=0, has_side_effects=True, vmem_limit_bytes=60 * 2 ** 20),
             name="chain",
-        )(angles, start, trig, costs)
+        )(beta, trig, costs)
         totals = sums[:, :13, 0] * jnp.concatenate([jnp.ones(1, F32), jnp.full((6,), 2.0, F32), jnp.ones(6, F32)])
         return totals[:, 0], totals[:, 1:]
 

time: 315 us -> 278 us (0.88)
  Pallas kernels: 301 us -> 270 us
  other arithmetic: 7.28 us -> 0.01 us
    pallas_call x1, Pallas kernels: 246 us -> 216 us  [device_fn(): pl.pallas_call(main_kernel, out_shape=(jax.ShapeDtypeStruct((2, 16, 128),...]
    another operation x4 -> x0, other arithmetic: 4.71 us -> none  [the longest x1 4.01 us: device_fn(): jnp.stack([jnp.where(ones == 0, amp, jnp.where(ones == 2, -amp, 0.0)), jn...]
where the time goes in v3:
time: 278 us
  Pallas kernels  270 us (97%)
  local copies, waits for them, and re-layouts  7.28 us (3%)
    pallas_call x1, Pallas kernels, device_fn(): pl.pallas_call(main_kernel, out_shape=(jax.ShapeDtypeStruct((2, 16, 128),...  216 us
    pallas_call x1, Pallas kernels, device_fn(): pl.pallas_call(prep_kernel, out_shape=(jax.ShapeDtypeStruct((2,) + AMPS,...  53.6 us

profile of v3, /device:TPU:0, one launch (start us, length us, event | category | flops | bytes accessed | tf_op | source)
XLA Modules:
  0.0 277.6 jit_solution(1920196555694161479)
XLA Ops:
  0.6 0.0 copy-start.3
  0.6 0.0 copy-start.1
  0.7 1.2 copy-done.1
  1.9 0.0 copy-start.2
  1.9 0.7 copy-done.2
  2.6 53.6 %prep.1 = (f32[2,16,512,128]{3,2,1,0:T(8,128)S(1)}, f32[2,3,2,16,512,128]{5,4,3,2,1,0:T(8,128)}) custom-call(f32[2,6]{1,0:T(2,128)S(1)} %copy-done.2, f32[2,2,512,128]{3,2,1,0:T(8,128)S(1)} %bitcast.1), custom_call_target="tpu_custom_call" | custom-call | tf_op jit(solution)/shard_map/prep/pallas_call | solution.py:582
  56.2 0.0 copy-start
  56.2 3.3 %copy-done = f32[2,16,512,128]{3,2,1,0:T(8,128)} copy-done((f32[2,16,512,128]{3,2,1,0:T(8,128)}, f32[2,16,512,128]{3,2,1,0:T(8,128)S(1)}, u32[]{:S(2)}) %copy-start) | copy-done | bytes 8388632
  59.5 216.0 %chain.1 = (f32[2,16,128]{2,1,0:T(8,128)}, f32[6,32,512,128]{3,2,1,0:T(8,128)}) custom-call(f32[2,6]{1,0:T(2,128)} %beta_ref.1, f32[2,3,2,16,512,128]{5,4,3,2,1,0:T(8,128)} %get-tuple-element.5.trig_ref, f32[2,16,512,128]{3,2,1,0:T(8,128)} %copy-done), custom_call_target="tpu_custom_call" | custom-call | tf_op jit(solution)/shard_map/chain/pallas_call | solution.py:592
  275.5 0.8 slice_reduce_fusion
  276.3 0.0 copy-done.3
  276.3 0.6 slice_reduce_fusion.1
  276.9 0.6 slice.11
  (1 shorter events, 0.0 us)
Async XLA Ops:
  0.6 275.7 %copy-start.3 = (f32[13]{0:T(128)S(1)}, f32[13]{0:T(128)}, u32[]{:S(2)}) copy-start(f32[13]{0:T(128)} %constant.2.clone.1) | copy-start | bytes 160
  0.6 1.2 copy-start.1
  1.9 0.7 copy-start.2
  56.2 3.3 %copy-start = (f32[2,16,512,128]{3,2,1,0:T(8,128)}, f32[2,16,512,128]{3,2,1,0:T(8,128)S(1)}, u32[]{:S(2)}) copy-start(f32[2,16,512,128]{3,2,1,0:T(8,128)S(1)} %get-tuple-element.6.cost_ref) | copy-start | bytes 25165828

commit v4 on v0

v4 whole, which is shorter than its diff:
```python
import jax
import jax.numpy as jnp
from jax import lax
from jax.experimental import pallas as pl
from jax.experimental.pallas import tpu as pltpu
from jax.sharding import PartitionSpec as P

F32 = jnp.float32
MESH = pl.DeviceIdType.MESH
TILE, GROUP, LANES, ROWS = 8, 64, 128, 512
HALF = 16
AMPS = (HALF, ROWS, LANES)
PAIRS = (2 * HALF, ROWS, LANES)
BITS = range(2)
EIGHT = range(TILE)
REGS = range(HALF)
N0, U, N1, N2 = 1, 2, 4, 8
LAYERS = 6


def pair4(a00, a01, a10, a11, turn):
    tan, cos2, cossin = turn
    w = (a11 - a00) + tan * (a01 + a10)
    cw = cos2 * w
    sw = cossin * w
    return a11 - cw, a01 - sw, a10 - sw, a00 + cw


def rot16(load, store, turn):
    v = []
    for g in range(N1):
        v += pair4(*[load(N1 * g + k) for k in range(N1)], turn)
    for k in range(N1):
        at = [N1 * g + k for g in range(N1)]
        for i, x in zip(at, pair4(*[v[i] for i in at], turn)):
            store(i, x)


def gen_sums(load):
    four = range(N1)
    last = N1 - 1
    v, lo = [], []
    for h in four:
        v += [load(N1 * h + k) for k in four]
        lo.append((v[N1 * h + 1] + v[N1 * h + U], v[N1 * h] - v[N1 * h + last]))
    hi = [(v[N1 + k] + v[N2 + k], v[k] - v[N1 * last + k]) for k in four]

    def value(i):
        h, k = i // N1, i % N1
        x, y = lo[h][k in (1, U)], hi[k][h in (1, U)]
        if k == 0:
            return -(x + y) if h == 0 else y - x
        return x - y if h == 0 else x + y
    return value


def tree_sum(terms):
    terms = list(terms)
    while len(terms) > 1:
        rest = terms[len(terms) // 2 * 2:]
        terms = [x + y for x, y in zip(terms[::2], terms[1::2])] + rest
    return terms[0]


def tile(start):
    return pl.ds(start, TILE)


def strided(start):
    return pl.ds(start, TILE, stride=TILE)


def spread(x):
    return jnp.full((TILE, LANES), x, F32)


def sincos(x):
    q = jnp.round(x * 0.63661977236758134)
    y = x - q * 1.5703125
    y = y - q * 4.83826794896619e-4
    z = y * y
    sn = ((z * -1.9515295891e-4 + 8.3321608736e-3) * z - 1.6666654611e-1) * z * y + y
    cs = ((z * 2.443315711809948e-5 - 1.388731625493765e-3) * z + 4.166664568298827e-2) * (z * z) - 0.5 * z + 1.0
    qi = q.astype(jnp.int32)
    odd = (qi & 1) != 0
    a = jnp.where(odd, cs, sn)
    b = jnp.where(odd, sn, cs)
    return jnp.where(((qi + 1) & 2) != 0, -b, b), jnp.where((qi & 2) != 0, -a, a)


PIECES = 8
UNROLL = 2
BATCH = 2
TAN, COS2, COSSIN, COS, SIN = range(5)


def main_kernel(beta_ref, trig_ref, cost_ref, energy_ref, grad_ref, save_ref, B, R, TB, PB, CB, GA, GB, ang, acc_ref,
                all_ref, send_sem, recv_sem, loc_sem, fin_send, fin_recv):
    inst = lax.axis_index("inst")
    role = lax.axis_index("qy")
    qx = lax.axis_index("qx")
    core = lax.rem(qx, 2)
    partner = (inst, role, qx + 1 - 2 * core)
    me = role * 4 + qx

    def half_at(u):
        return HALF * u
    devices = range(1, 8)

    def peer(k):
        return (inst, jnp.bitwise_xor(role, k // 4), jnp.bitwise_xor(qx, k % 4))

    barrier = pltpu.get_barrier_semaphore()
    for k in devices:
        pl.semaphore_signal(barrier, inc=1, device_id=peer(k), device_id_type=MESH)
    pl.semaphore_wait(barrier, len(devices))

    def piece(par, j):
        rows = pl.ds(pl.multiple_of(j * GROUP, GROUP), GROUP)
        return pltpu.make_async_remote_copy(
            src_ref=B.at[pl.ds(half_at(1 - core), HALF), rows, :], dst_ref=R.at[par, pl.ds(0, HALF), rows, :],
            send_sem=send_sem.at[j], recv_sem=recv_sem.at[par, j], device_id=partner, device_id_type=MESH)

    def full(ref):
        return ref.at[(slice(None),) * (len(ref.shape) - 2) + (pl.ds(0, ROWS),)]

    def trig_copy(k):
        return pltpu.make_async_copy(trig_ref.at[lax.rem(k, 2), lax.div(k, 2)], full(TB), loc_sem.at[0])

    def cost_copy(k):
        return pltpu.make_async_copy(cost_ref.at[lax.rem(k, 2)], full(CB), loc_sem.at[1])

    def save_copy(k):
        return pltpu.make_async_copy(full(PB), save_ref.at[k], loc_sem.at[2])

    def load_copy(k):
        return pltpu.make_async_copy(save_ref.at[k], full(PB), loc_sem.at[3])

    trig_copy(0).start()
    cost_copy(0).start()

    def low(i):
        return (i >> 2) * 2 + (i & 1)

    def up(i):
        return (i >> 1) & 1

    def state_at(i, ri):
        return half_at(up(i)) + ri * TILE + low(i)

    def pair_at(i, ri):
        return up(i) * HALF + ri * TILE + low(i)

    def amp_at(i):
        return up(i) * TILE + low(i)

    def turn_of(step):
        return tuple(ang[k, step] for k in (TAN, COS2, COSSIN))

    post_groups = [[n0 + n2 + b for b in (0, U, N1, U + N1)] for n2 in (0, N2) for n0 in (0, N0)]
    pre_groups = [[n1 + n2 + b for b in (0, U, N0, U + N0)] for n1 in (0, N1) for n2 in (0, N2)]

    def finish(ri, row, v, group, one):
        c, s = one
        for i in group:
            a0, a1 = v[i - N2], v[i]
            B[state_at(i - N2, ri), tile(row), :] = c * a0 - s * a1
            B[state_at(i, ri), tile(row), :] = s * a0 + c * a1

    angle_set = lax.div(qx, 2)
    for k in range(LAYERS):
        cs, sn = sincos(spread(beta_ref[angle_set, k] * 0.5))
        for at, sine in ((k, sn), (2 * LAYERS - 1 - k, -sn)):
            for where, value in ((TAN, sine / cs), (COS2, cs * cs), (COSSIN, cs * sine), (COS, cs), (SIN, sine)):
                ang[where, at] = value
    for where in (TAN, COS2, COSSIN, COS, SIN):
        ang[where, 2 * LAYERS] = spread(1.0 if where in (COS2, COS) else 0.0)

    inside = lax.population_count(
        lax.broadcasted_iota(jnp.int32, (TILE, LANES), 0) * LANES + lax.broadcasted_iota(jnp.int32, (TILE, LANES), 1))

    def fill(b, carry):
        u, nh, n0 = lax.div(b, 8), lax.rem(lax.div(b, 2), 4), lax.rem(b, 2)
        ones = (inside + (core + u + lax.div(nh, 2) + lax.rem(nh, 2) + n0)) & 3
        amp = F32(2.0 ** -10.5)
        re = jnp.where(ones == 0, amp, jnp.where(ones == 2, -amp, 0.0))
        im = jnp.where(ones == 1, amp, jnp.where(ones == 3, -amp, 0.0))
        turns = [(re, im), (-im, re), (-re, -im), (im, -re)]
        slot = half_at(u) + nh * 2 + n0
        for t in range(GROUP):
            x, y = turns[bin(t).count("1") % len(turns)]
            B[slot, tile(TILE * t), :] = x
            B[slot + TILE, tile(TILE * t), :] = y
        return carry
    lax.fori_loop(0, HALF, fill, 0)

    def at_row(n4, n3, h):
        return (n4 * 2 + n3) * LANES + h * GROUP

    def half_loop(turn, u, got):
        def put(blk, rows):
            def store(i, x):
                B[blk, rows[i], :] = x
            return store

        def stage1(blk, src, n4, h):
            rows = [tile(at_row(n4, n3, h) + TILE * k) for n3 in BITS for k in EIGHT]
            rot16(lambda i: B[blk, rows[i], :] if got is None else R[got, src, rows[i], :], put(blk, rows), turn)

        def stage2(blk, n4, n3):
            rows = [tile(at_row(n4, n3, 0) + TILE * k) for k in REGS]
            spots = [strided(at_row(n4, n3, h) + k) for h in BITS for k in EIGHT]
            v = {}
            rot16(lambda i: B[blk, spots[i], :], v.__setitem__, turn)
            flip = jnp.transpose(jnp.concatenate([v[i] for i in REGS], axis=0))
            rot16(lambda i: flip[TILE * i:TILE * i + TILE, :], put(blk, rows), turn)

        def stage3(blk, n3, h):
            rows = [tile(at_row(n4, n3, h) + TILE * k) for n4 in BITS for k in EIGHT]
            spots = [strided(at_row(n4, n3, h) + k) for n4 in BITS for k in EIGHT]
            rot16(lambda i: B[blk, spots[i], :], put(blk, rows), turn)

        def some(t, carry):
            first = half_at(u) + t * BATCH
            parts = [(x, y) for x in BITS for y in BITS]
            for k in range(BATCH):
                for part in parts:
                    stage1(first + k, t * BATCH + k, *part)
            for k in range(BATCH):
                for part in parts:
                    stage2(first + k, *part)
            for k in range(BATCH):
                for part in parts:
                    stage3(first + k, *part)
            return carry
        lax.fori_loop(0, HALF // BATCH, some, 0)

    def body_loop(step):
        turn = turn_of(step)
        par = lax.rem(step, 2)
        half_loop(turn, core, None)

        def wait(j, carry):
            piece(par, j).wait()
            return carry
        lax.fori_loop(0, PIECES, wait, 0)
        half_loop(turn, 1 - core, par)

    def sweep(step, unit, init, send):
        par = lax.rem(step, 2)

        def body(j, carry):
            def two(t, cr):
                spot = j * GROUP + t * UNROLL
                row = pl.multiple_of(j * GROUP + t * (UNROLL * TILE), TILE)
                for k in range(UNROLL):
                    cr = unit(spot + k, row + k * TILE, cr)
                return cr
            carry = lax.fori_loop(0, TILE // UNROLL, two, carry)
            if send:
                @pl.when(j > 0)
                def _():
                    piece(par, j - 1).start()
            return carry
        carry = lax.fori_loop(0, PIECES, body, init)
        if send:
            piece(par, PIECES - 1).start()
        return carry

    zero = spread(0.0)

    def forward(step):
        k = step
        c0 = turn_of(lax.rem(step + 2 * LAYERS, 2 * LAYERS + 1))
        c1, one1 = turn_of(step), (ang[COS, step], ang[SIN, step])
        trig_copy(k).wait()

        @pl.when(k > 0)
        def _():
            save_copy(k - 1).wait()

        def unit(keep_before):
            def f(spot, row, carry):
                re, im = {}, {}
                for half in BITS:
                    for group in post_groups[half * 2:half * 2 + 2]:
                        a = pair4(*[B[state_at(i, 0), tile(row), :] for i in group], c0)
                        b = pair4(*[B[state_at(i, 1), tile(row), :] for i in group], c0)
                        for i, x, y in zip(group, a, b):
                            cs, sn = TB[0, amp_at(i), tile(row), :], TB[1, amp_at(i), tile(row), :]
                            re[i], im[i] = x * cs + y * sn, y * cs - x * sn
                            PB[pair_at(i, 0), tile(row), :] = x if keep_before else re[i]
                            PB[pair_at(i, 1), tile(row), :] = y if keep_before else im[i]
                    for group in pre_groups[half::2]:
                        for ri, v in ((0, re), (1, im)):
                            v.update(zip(group, pair4(*[v[i] for i in group], c1)))
                            if half:
                                finish(ri, row, v, group, one1)
                return carry
            return f

        for r in BITS:
            @pl.when(role == r)
            def _():
                sweep(step, unit(r == 1), 0, True)
        save_copy(k).start()

        @pl.when(k < LAYERS - 1)
        def _():
            trig_copy(k + 1).start()

    def generator(swap):
        def body(t, carry):
            for ri in BITS:
                b = t + HALF * ri
                for q in BITS:
                    for p in BITS:
                        spots = [strided(at_row(q, p, h) + k) for h in BITS for k in EIGHT]
                        g = gen_sums(lambda i: PB[b, spots[i], :])
                        for k in REGS:
                            GA[b, tile(at_row(q, p, 0) + TILE * k), :] = g(k)
                for held in BITS:
                    for h in BITS:
                        rows = [tile((at_row(e, held, h) if swap else at_row(held, e, h)) + TILE * k) for e in BITS for k in EIGHT]
                        g = gen_sums(lambda i: PB[b, rows[i], :])
                        for k in REGS:
                            GB[b, rows[k], :] = g(k)
            return carry
        lax.fori_loop(0, HALF, body, 0)

    def generated(i, ri, spot, row):
        return GA[pair_at(i, ri), strided(spot), :] + GB[pair_at(i, ri), tile(row), :]

    def beta_u(lam, psi, group, ri, spot, row):
        terms = []
        for k, i in enumerate(group):
            g = generated(i, ri, spot, row)
            terms.append(lam[k] * (g + psi[k - 1] if i & U else g - psi[k + 1]))
        return tree_sum(terms)

    def turn(step):
        c0 = turn_of(step - 1)
        c1, one1 = turn_of(step), (ang[COS, step], ang[SIN, step])
        save_copy(LAYERS - 1).wait()
        cost_copy(0).wait()

        def only_energy(spot, row, acc):
            for ri in BITS:
                v = {}
                for half in BITS:
                    for group in post_groups[half * 2:half * 2 + 2]:
                        psi = pair4(*[B[state_at(i, ri), tile(row), :] for i in group], c0)
                        for i, x in zip(group, psi):
                            v[i] = CB[amp_at(i), tile(row), :] * x
                        acc = acc + tree_sum([v[i] * x for i, x in zip(group, psi)])
                    for group in pre_groups[half::2]:
                        v.update(zip(group, pair4(*[v[i] for i in group], c1)))
                        if half:
                            finish(ri, row, v, group, one1)
            return acc

        def keep(spot, row, acc):
            for ri in BITS:
                for group in post_groups:
                    for i, x in zip(group, pair4(*[B[state_at(i, ri), tile(row), :] for i in group], c0)):
                        PB[pair_at(i, ri), tile(row), :] = x
            return acc

        def with_beta(spot, row, acc):
            for ri in BITS:
                v = {}
                for n, group in enumerate(pre_groups):
                    psi = [PB[pair_at(i, ri), tile(row), :] for i in group]
                    lam = [CB[amp_at(i), tile(row), :] * x for i, x in zip(group, psi)]
                    acc = acc + beta_u(lam, psi, group, ri, spot, row)
                    v.update(zip(group, pair4(*lam, c1)))
                    if n % 2:
                        finish(ri, row, v, group, one1)
            return acc

        @pl.when(role == 0)
        def _():
            acc_ref[0] = sweep(step, only_energy, zero, True)

        @pl.when(role == 1)
        def _():
            sweep(step, keep, 0, False)
            generator(True)
            acc_ref[2 * LAYERS] = sweep(step, with_beta, zero, True)
        load_copy(LAYERS - 1).start()
        trig_copy(LAYERS - 1).start()
        cost_copy(LAYERS - 1).start()

    def backward(step, layer, last):
        c0 = turn_of(step - 1)
        c1, one1 = (None, None) if last else (turn_of(step), (ang[COS, step], ang[SIN, step]))
        trig_copy(layer).wait()
        cost_copy(layer).wait()
        load_copy(layer).wait()

        def un_phase(i, x, y, row):
            cs, sn = TB[0, amp_at(i), tile(row), :], TB[1, amp_at(i), tile(row), :]
            return x * cs - y * sn, y * cs + x * sn

        def beta_after(spot, row, acc):
            for ri in BITS:
                g = gen_sums(lambda i: PB[pair_at(i, ri), tile(row), :])
                for group in post_groups:
                    lam = pair4(*[B[state_at(i, ri), tile(row), :] for i in group], c0)
                    acc = acc + tree_sum([x * (generated(i, ri, spot, row) + g(i)) for i, x in zip(group, lam)])
                    if not last:
                        for i, x in zip(group, lam):
                            B[state_at(i, ri), tile(row), :] = x
            return acc

        def to_before(spot, row, acc):
            re, im = {}, {}
            for n, group in enumerate(pre_groups):
                for i in group:
                    re[i], im[i] = un_phase(i, B[state_at(i, 0), tile(row), :], B[state_at(i, 1), tile(row), :], row)
                for ri, v in ((0, re), (1, im)):
                    v.update(zip(group, pair4(*[v[i] for i in group], c1)))
                    if n % 2:
                        finish(ri, row, v, group, one1)
            return acc

        def to_phase(spot, row, acc):
            for group in post_groups:
                lam = [pair4(*[B[state_at(i, ri), tile(row), :] for i in group], c0) for ri in BITS]
                for i, x, y in zip(group, *lam):
                    for ri, z in enumerate(un_phase(i, x, y, row)):
                        B[state_at(i, ri), tile(row), :] = z
            return acc

        def sums_before(spot, row, acc):
            acc_g, acc_b = acc
            out = ({}, {})
            for n, group in enumerate(pre_groups):
                psi = [[PB[pair_at(i, ri), tile(row), :] for i in group] for ri in BITS]
                lam = [[B[state_at(i, ri), tile(row), :] for i in group] for ri in BITS]
                acc_g = acc_g + tree_sum([
                    CB[amp_at(i), tile(row), :] * (lam[0][k] * psi[1][k] - lam[1][k] * psi[0][k]) for k, i in enumerate(group)])
                if not last:
                    for ri in BITS:
                        acc_b = acc_b + beta_u(lam[ri], psi[ri], group, ri, spot, row)
                        out[ri].update(zip(group, pair4(*lam[ri], c1)))
                        if n % 2:
                            finish(ri, row, out[ri], group, one1)
            return acc_g, acc_b

        @pl.when(role == 0)
        def _():
            generator(False)
            acc_ref[1 + LAYERS + layer] = sweep(step, beta_after, zero, False)
            if not last:
                sweep(step, to_before, 0, True)

        @pl.when(role == 1)
        def _():
            if not last:
                generator(True)
            sweep(step, to_phase, 0, False)
            acc_g, acc_b = sweep(step, sums_before, (zero, zero), not last)
            acc_ref[1 + layer] = acc_g + acc_g
            if not last:
                acc_ref[LAYERS + layer] = acc_b
        if not last:
            load_copy(layer - 1).start()
            trig_copy(layer - 1).start()
            cost_copy(layer - 1).start()

    acc_ref[...] = jnp.zeros_like(acc_ref)

    def layer_loop(step, carry):
        @pl.when(step < LAYERS)
        def _():
            forward(step)

        @pl.when(step == LAYERS)
        def _():
            turn(step)

        @pl.when(step > LAYERS)
        def _():
            backward(step, 2 * LAYERS - step, False)
        body_loop(step)
        return carry
    lax.fori_loop(0, 2 * LAYERS, layer_loop, 0)
    backward(2 * LAYERS, 0, True)

    all_ref[me] = jnp.sum(acc_ref[...], axis=1)
    copies = [pltpu.make_async_remote_copy(
        src_ref=all_ref.at[me], dst_ref=all_ref.at[me], send_sem=fin_send.at[k], recv_sem=fin_recv.at[k],
        device_id=peer(k), device_id_type=MESH) for k in devices]
    for cp in copies:
        cp.start()
    for cp in copies:
        cp.wait()
    row = lax.broadcasted_iota(jnp.int32, (HALF, LANES), 0)
    lane = lax.broadcasted_iota(jnp.int32, (HALF, LANES), 1)
    lines = []
    for k in BITS:
        total = (all_ref[2 * k] + all_ref[2 * k + 1]) + (all_ref[2 * k + 4] + all_ref[2 * k + 5])
        total = jnp.broadcast_to(jnp.sum(total, axis=1, keepdims=True), (HALF, LANES))
        lines.append(jnp.sum(jnp.where(row == lane + 1, total, 0.0), axis=0, keepdims=True))
        energy_ref[k, :] = total[0, :]
    grad_ref[...] = jnp.concatenate(lines, axis=0)[:, :2 * LAYERS]


def prep_kernel(gam, own_ref, cost_ref, trig_ref, F, E, G, T, own_sem, sx, sy, sf, se, rx, ry, rd, re_, out_sem, cost_sem):
    inst = lax.axis_index("inst")
    qy = lax.axis_index("qy")
    qx = lax.axis_index("qx")
    core = lax.rem(qx, 2)
    xpos = lax.div(qx, 2)
    me = qy * 2 + xpos
    xnbr, ynbr, dnbr = qy * 2 + 1 - xpos, (1 - qy) * 2 + xpos, (1 - qy) * 2 + 1 - xpos
    x_dev = (inst, qy, (1 - xpos) * 2 + core)
    y_dev = (inst, 1 - qy, qx)
    p_dev = (inst, qy, xpos * 2 + 1 - core)
    near = (x_dev, y_dev, p_dev)
    four = range(4)

    own = pltpu.make_async_copy(own_ref, F.at[me], own_sem)
    own.start()
    barrier = pltpu.get_barrier_semaphore()
    for dev in near:
        pl.semaphore_signal(barrier, inc=1, device_id=dev, device_id_type=MESH)
    pl.semaphore_wait(barrier, len(near))
    own.wait()

    def half_of(p):
        return core if p < 2 else 1 - core

    def push(blk, p, ssem, rsem, dev):
        return pltpu.make_async_remote_copy(
            src_ref=F.at[blk, half_of(p), p % 2], dst_ref=F.at[blk, half_of(p), p % 2],
            send_sem=ssem.at[p], recv_sem=rsem.at[p], device_id=dev, device_id_type=MESH)

    def give(blk, n0):
        return pltpu.make_async_remote_copy(
            src_ref=F.at[blk, 1 - core, n0], dst_ref=E.at[blk, n0],
            send_sem=se.at[blk, n0], recv_sem=re_.at[blk, n0], device_id=p_dev, device_id_type=MESH)

    def index(blk, u, n0):
        return u * TILE + blk * 2 + n0

    def flush(form, slot, blk, u, n0):
        return pltpu.make_async_copy(T.at[slot], trig_ref.at[form, :, :, index(blk, u, n0)], out_sem.at[slot])

    def keep(form, blk, u, n0):
        at = index(blk, u, n0)
        return pltpu.make_async_copy((F, G)[form].at[blk, u, n0], cost_ref.at[form, at], cost_sem.at[form, at])

    for p in four:
        push(me, p, sx, rx, x_dev).start()
        push(me, p, sy, ry, y_dev).start()
    done = []

    def tables(form, src, blk, u, n0):
        slot = len(done) % 2
        if len(done) > 1:
            flush(form, slot, blk, u, n0).wait()
        done.append(form)
        chunk = 32

        def body(r, carry):
            rows = pl.ds(pl.multiple_of(r * chunk, chunk), chunk)
            c = src[rows, :]
            for sub in range(3):
                cs, sn = sincos(gam[xpos, sub * 2 + form] * c)
                T[slot, sub, 0, rows, :] = cs
                T[slot, sub, 1, rows, :] = sn
            return carry
        lax.fori_loop(0, ROWS // chunk, body, 0)
        flush(form, slot, blk, u, n0).start()
        keep(form, blk, u, n0).start()

    def first_form(blk, p):
        if p >= 2:
            give(blk, p % 2).start()
        tables(0, F.at[blk, half_of(p), p % 2], blk, half_of(p), p % 2)

    def second_form(blk, p):
        n0, u = p % 2, half_of(p)
        if p >= 2:
            give(blk, n0).wait()
        src = F.at[blk, core, n0] if p < 2 else E.at[blk, n0]
        dst = G.at[blk, u, n0]

        def turn_over(q, carry):
            spots = [q * LANES + h * GROUP + k for h in BITS for k in EIGHT]
            x = jnp.transpose(jnp.concatenate([src[strided(r), :] for r in spots], axis=0))
            for i, r in enumerate(spots):
                dst[strided(r), :] = x[TILE * i:TILE * i + TILE, :]
            return carry
        lax.fori_loop(0, 4, turn_over, 0)
        tables(1, dst, blk, u, n0)

    def from_x(p):
        push(xnbr, p, sx, rx, x_dev).wait_recv()
        if p < 2:
            push(xnbr, p, sf, rd, y_dev).start()
        first_form(xnbr, p)

    def from_y(p):
        push(ynbr, p, sy, ry, y_dev).wait_recv()
        if p >= 2:
            push(ynbr, p, sf, rd, x_dev).start()
        first_form(ynbr, p)

    def from_d(p):
        push(dnbr, p, sf, rd, x_dev).wait_recv()
        first_form(dnbr, p)

    def both(p):
        from_x(p)
        from_y(p)

    def both_second(p):
        second_form(xnbr, p)
        second_form(ynbr, p)

    for p in four:
        first_form(me, p)
    for p in four:
        second_form(me, p)
    early, late = four[:2], four[2:]
    for p in early:
        both(p)
    for p in early:
        both_second(p)
    for p in late:
        both(p)
        both_second(p)
    for p in early:
        for k in (p, p + 2):
            from_d(k)
        for k in (p, p + 2):
            second_form(dnbr, k)

    for p in four:
        push(me, p, sx, rx, x_dev).wait_send()
        push(me, p, sy, ry, y_dev).wait_send()
        push(me, p, sf, rd, x_dev).wait_send()
    for slot in BITS:
        flush(0, slot, 0, 0, 0).wait()

    def kept(t, carry):
        for form in BITS:
            keep(form, lax.div(t, 4), lax.div(lax.rem(t, 4), 2), lax.rem(t, 2)).wait()
        return carry
    lax.fori_loop(0, HALF, kept, 0)


def solution(mesh):
    def device_fn(cost, gamma, beta):
        any_space = pl.BlockSpec(memory_space=pl.ANY)
        smem = pl.BlockSpec(memory_space=pltpu.SMEM)
        in_vmem = pl.BlockSpec(memory_space=pltpu.VMEM)
        dma = pltpu.SemaphoreType.DMA
        vmem = pltpu.VMEM
        mib = 2 ** 20
        quarter = (4, 2, 2, ROWS, LANES)

        def params(number):
            return pltpu.CompilerParams(collective_id=number, has_side_effects=True, vmem_limit_bytes=63 * mib)

        def padded(*shape):
            return (*shape, ROWS + TILE, LANES)

        def out(*shape):
            return jax.ShapeDtypeStruct(shape, F32)

        costs, trig = pl.pallas_call(
            prep_kernel, out_shape=(out(2, *AMPS), out(2, 3, 2, *AMPS)),
            in_specs=[smem, any_space], out_specs=(any_space, any_space),
            scratch_shapes=[
                vmem(quarter, F32), vmem((4, 2, ROWS, LANES), F32), vmem(quarter, F32), vmem((2, 3, 2, ROWS, LANES), F32),
                dma] + [dma((4,))] * 3 + [dma((4, 2))] + [dma((4,))] * 3 + [dma((4, 2)), dma((2,)), dma((2, HALF))],
            compiler_params=params(1), name="prep",
        )(gamma, cost.reshape(quarter[1:]))
        energy, grad, _ = pl.pallas_call(
            main_kernel, out_shape=(out(2, LANES), out(2, 2 * LAYERS), out(LAYERS, *PAIRS)),
            in_specs=[smem, any_space, any_space], out_specs=(in_vmem, in_vmem, any_space),
            scratch_shapes=[
                vmem(padded(2 * HALF), F32), vmem(padded(2, HALF), F32), vmem(padded(2, HALF), F32), vmem(padded(2 * HALF), F32),
                vmem(padded(HALF), F32), vmem(padded(2 * HALF), F32), vmem(padded(2 * HALF), F32),
                vmem((5, 2 * LAYERS + 1, TILE, LANES), F32), vmem((HALF, TILE, LANES), F32), vmem((TILE, HALF, LANES), F32),
                dma((PIECES,)), dma((2, PIECES)), dma((4,)), dma((8,)), dma((8,))],
            compiler_params=params(0), name="chain",
        )(beta, trig, costs)
        return energy[:, 0], grad

    spec = P("inst", None)
    return jax.shard_map(device_fn, mesh=mesh, in_specs=(P(("inst", "qy", "qx")), spec, spec), out_specs=(P("inst"), spec), check_vma=False)
```

time: 9000 us -> 234 us (0.03)
  other arithmetic: 3540 us -> 0 us
  waiting for transfers between devices: 3340 us -> 0 us
  local copies, waits for them, and re-layouts: 2030 us -> 2.43 us
  Pallas kernels: 0 us -> 230 us
    ppermute x36 -> x0, waiting for transfers between devices: 3340 us -> none  [the longest x18 2230 us: device_fn(): partner = lax.ppermute(jnp.stack(list(four_amps)), axis_name, pair_list)]
    slice x1083 -> x1, local copies, waits for them, and re-layouts: 1110 us -> 1.24 us  [device_fn(): return (energy[:, 0], grad)]
    reduce_sum x122 -> x0, other arithmetic: 1080 us -> none  [the longest x121 1070 us: inverse_step(): term = jnp.sum(lam_re * partner[1] - lam_im * partner[0], axis=(1, 2))]
    add x133 -> x0, other arithmetic: 904 us -> none  [the longest x54 623 us: device_fn(): cos_b * psi_re + sin_b * flip_im]
    sub x111 -> x0, other arithmetic: 775 us -> none  [the longest x56 602 us: device_fn(): cos_b * psi_im - sin_b * flip_re]
    concatenate x214 -> x0, local copies, waits for them, and re-layouts: 757 us -> none  [the longest x139 471 us: flip_grid(): jnp.roll(amplitudes, shift, axis=axis_pos)]
    mul x34 -> x0, other arithmetic: 624 us -> none  [the longest x8 200 us: device_fn(): sin_b * flip_im]
    pallas_call x0 -> x2, Pallas kernels: none -> 230 us  [the longest x1 181 us: device_fn(): pl.pallas_call(main_kernel, out_shape=(out(2, LANES), out(2, 2 * LAYERS),...]
  transfers between devices with their start and end apart: 36 -> 0, of which waited for: 36 -> 0; matrix products, arithmetic and copies ran while one was open for 0% -> 0% of each run, Pallas kernels for 0% -> 0%
where the time goes in v4:
time: 234 us
  Pallas kernels  230 us (98%)
  local copies, waits for them, and re-layouts  2.43 us (1%)
    pallas_call x1, Pallas kernels, device_fn(): pl.pallas_call(main_kernel, out_shape=(out(2, LANES), out(2, 2 * LAYERS),...  181 us
    pallas_call x1, Pallas kernels, device_fn(): pl.pallas_call(prep_kernel, out_shape=(out(2, *AMPS), out(2, 3, 2, *AMPS)...  49.3 us

profile of v4, /device:TPU:0, one launch (start us, length us, event | category | flops | bytes accessed | tf_op | source)
XLA Modules:
  0.0 233.5 jit_solution(2846846035638846083)
XLA Ops:
  0.6 49.3 %prep.1 = (f32[2,16,512,128]{3,2,1,0:T(8,128)}, f32[2,3,2,16,512,128]{5,4,3,2,1,0:T(8,128)}) custom-call(f32[2,6]{1,0:T(2,128)} %gam.1, f32[2,2,512,128]{3,2,1,0:T(8,128)} %bitcast.1), custom_call_target="tpu_custom_call" | custom-call | tf_op jit(solution)/shard_map/prep/pallas_call | solution.py:675
  49.9 181.2 %chain.1 = (f32[2,128]{1,0:T(2,128)}, f32[2,12]{1,0:T(2,128)}, f32[6,32,512,128]{3,2,1,0:T(8,128)}) custom-call(f32[2,6]{1,0:T(2,128)} %beta_ref.1, f32[2,3,2,16,512,128]{5,4,3,2,1,0:T(8,128)} %get-tuple-element.6.trig_ref, f32[2,16,512,128]{3,2,1,0:T(8,128)} %get-tuple-element.7.cost_ref), custom_call_target="tpu_custom_call" | custom-call | tf_op jit(solution)/shard_map/chain/pallas_call | solution.py:683
  231.1 1.2 slice_reduce_fusion
  232.3 1.2 copy.6

commit v5 on v4

v5 whole, which is shorter than its diff:
```python
import jax
import jax.numpy as jnp
from jax import lax
from jax.experimental import pallas as pl
from jax.experimental.pallas import tpu as pltpu
from jax.sharding import PartitionSpec as P

F32 = jnp.float32
MESH = pl.DeviceIdType.MESH
TILE, GROUP, LANES, ROWS = 8, 64, 128, 512
HALF = 16
AMPS = (HALF, ROWS, LANES)
PAIRS = (2 * HALF, ROWS, LANES)
BITS = range(2)
EIGHT = range(TILE)
REGS = range(HALF)
N0, U, N1, N2 = 1, 2, 4, 8
LAYERS = 6


def pair4(a00, a01, a10, a11, turn):
    tan, cos2, cossin = turn
    w = (a11 - a00) + tan * (a01 + a10)
    cw = cos2 * w
    sw = cossin * w
    return a11 - cw, a01 - sw, a10 - sw, a00 + cw


def rot16(load, store, turn):
    v = []
    for g in range(N1):
        v += pair4(*[load(N1 * g + k) for k in range(N1)], turn)
    for k in range(N1):
        at = [N1 * g + k for g in range(N1)]
        for i, x in zip(at, pair4(*[v[i] for i in at], turn)):
            store(i, x)


def gen_sums(load):
    four = range(N1)
    last = N1 - 1
    v, lo = [], []
    for h in four:
        v += [load(N1 * h + k) for k in four]
        lo.append((v[N1 * h + 1] + v[N1 * h + U], v[N1 * h] - v[N1 * h + last]))
    hi = [(v[N1 + k] + v[N2 + k], v[k] - v[N1 * last + k]) for k in four]

    def value(i):
        h, k = i // N1, i % N1
        x, y = lo[h][k in (1, U)], hi[k][h in (1, U)]
        if k == 0:
            return -(x + y) if h == 0 else y - x
        return x - y if h == 0 else x + y
    return value


def tree_sum(terms):
    terms = list(terms)
    while len(terms) > 1:
        rest = terms[len(terms) // 2 * 2:]
        terms = [x + y for x, y in zip(terms[::2], terms[1::2])] + rest
    return terms[0]


def tile(start):
    return pl.ds(start, TILE)


def strided(start):
    return pl.ds(start, TILE, stride=TILE)


def spread(x):
    return jnp.full((TILE, LANES), x, F32)


def poly(coefs, z):
    acc = coefs[-1]
    for c in coefs[-2::-1]:
        acc = acc * z + c
    return acc


SIN_HALF = (4.442882834149774, -7.308241154537804, 3.6062889581019757, -0.8457635954863518, 0.10920575246185597)
COS_HALF = (1.41421356206289, -6.978864110095999, 5.73988154593808, -1.8882749991429137, 0.33225188199103406, -0.03450216718833275)
PER_TURN = 0.15915494309189535


def sincos(turns):
    f = turns - jnp.round(turns)
    z = f * f
    sn = poly(SIN_HALF, z) * f
    return 1.0 - sn * sn, sn * poly(COS_HALF, z)


PIECES = 8
SPAN = ROWS // PIECES
UNROLL = 2
BATCH = 2
TAN, COS2, COSSIN, COS, SIN = range(5)


def main_kernel(gamma_ref, beta_ref, own_ref, energy_ref, grad_ref, save_ref, cost_ref, trig_ref,
                B, R, TB, PB, CB, GA, GB, ang, acc_ref, all_ref, send_sem, recv_sem, loc_sem, fin_send, fin_recv,
                near_send, pass_send, near_recv, far_recv, give_send, give_recv, first_send, first_recv, out_sem, cost_sem):
    inst = lax.axis_index("inst")
    role = lax.axis_index("qy")
    qx = lax.axis_index("qx")
    core = lax.rem(qx, 2)
    angle_set = lax.div(qx, 2)
    chip = role * 2 + angle_set
    partner = (inst, role, qx + 1 - 2 * core)

    def neighbour(d):
        return (inst, jnp.bitwise_xor(role, d), jnp.bitwise_xor(qx, 2 - 2 * d))

    me = role * 4 + qx
    rows_all = pl.ds(0, ROWS)
    four = range(4)

    def cost_at(form, blk, u, n0):
        return form * HALF + (blk * 2 + u) * 2 + n0

    own = pltpu.make_async_copy(own_ref, GA.at[pl.ds(cost_at(0, chip, 0, 0), 4), rows_all, :], loc_sem.at[0])
    own.start()

    def half_at(u):
        return HALF * u

    devices = range(1, 8)

    def peer(k):
        return (inst, jnp.bitwise_xor(role, k // 4), jnp.bitwise_xor(qx, k % 4))

    barrier = pltpu.get_barrier_semaphore()
    for k in devices:
        pl.semaphore_signal(barrier, inc=1, device_id=peer(k), device_id_type=MESH)
    pl.semaphore_wait(barrier, len(devices))
    own.wait()

    def half_of(p):
        return jnp.bitwise_xor(core, lax.div(p, 2))

    def push(blk, p, ssem, rsem, d):
        at = cost_at(0, blk, half_of(p), lax.rem(p, 2))
        return pltpu.make_async_remote_copy(
            src_ref=GA.at[at, rows_all, :], dst_ref=GA.at[at, rows_all, :], send_sem=ssem, recv_sem=rsem,
            device_id=neighbour(d), device_id_type=MESH)

    def push_own(d, p):
        return push(chip, p, near_send.at[d, p], near_recv.at[d, p], d)

    def from_near(d, p):
        return push(jnp.bitwise_xor(chip, 1 + d), p, near_send.at[d, p], near_recv.at[d, p], d)

    def pass_on(d, p):
        return push(jnp.bitwise_xor(chip, 1 + d), p, pass_send.at[p], far_recv.at[p], 1 - d)

    def from_far(p):
        return push(jnp.bitwise_xor(chip, 3), p, pass_send.at[p], far_recv.at[p], 0)

    def send_own(i, carry):
        push_own(lax.rem(i, 2), lax.div(i, 2)).start()
        return carry
    lax.fori_loop(0, 8, send_own, 0)

    def piece(par, j):
        rows = pl.ds(pl.multiple_of(j * SPAN, SPAN), SPAN)
        return pltpu.make_async_remote_copy(
            src_ref=B.at[pl.ds(half_at(1 - core), HALF), rows, :], dst_ref=R.at[par, pl.ds(0, HALF), rows, :],
            send_sem=send_sem.at[j], recv_sem=recv_sem.at[par, j], device_id=partner, device_id_type=MESH)

    def full(ref):
        return ref.at[(slice(None),) * (len(ref.shape) - 2) + (rows_all,)]

    def trig_copy(k):
        return pltpu.make_async_copy(trig_ref.at[lax.rem(k, 2), pl.ds(lax.div(k, 2) * 2, 2)], full(TB), loc_sem.at[0])

    def cost_copy(k):
        return pltpu.make_async_copy(cost_ref.at[lax.rem(k, 2)], full(CB), loc_sem.at[1])

    def save_copy(k, src=PB):
        return pltpu.make_async_copy(full(src), save_ref.at[k], loc_sem.at[2])

    def load_copy(k):
        return pltpu.make_async_copy(save_ref.at[k], full(PB), loc_sem.at[3])

    def low(i):
        return (i >> 2) * 2 + (i & 1)

    def up(i):
        return (i >> 1) & 1

    def pair_at(i, ri):
        return up(i) * HALF + ri * TILE + low(i)

    def amp_at(i):
        return up(i) * TILE + low(i)

    def turn_of(step):
        return tuple(ang[k, step] for k in (TAN, COS2, COSSIN))

    post_pairs = [tuple([n0 + n2 + b for b in (0, U, N1, U + N1)] for n2 in (0, N2)) for n0 in (0, N0)]
    pre_groups = [[n1 + n2 + b for b in (0, U, N0, U + N0)] for n1 in (0, N1) for n2 in (0, N2)]

    def post_of(step):
        return turn_of(step), ang[COS, step], ang[SIN, step]

    def posted(load, groups, angles):
        turn, c, s = angles
        parts = [pair4(*[load(i) for i in group], turn) for group in groups]
        out = []
        for i, k, x, y in zip(*groups, *parts):
            out += [(i, c * x - s * y), (k, s * x + c * y)]
        return out

    def get(ri, row):
        return lambda i: B[pair_at(i, ri), tile(row), :]

    for k in range(LAYERS):
        cs, sn = sincos(spread(beta_ref[angle_set, k] * (0.5 * PER_TURN)))
        for at, sine in ((k, sn), (2 * LAYERS - 1 - k, -sn)):
            for where, value in ((TAN, sine / cs), (COS2, cs * cs), (COSSIN, cs * sine), (COS, cs), (SIN, sine)):
                ang[where, at] = value
    for where in (TAN, COS2, COSSIN, COS, SIN):
        ang[where, 2 * LAYERS] = spread(1.0 if where in (COS2, COS) else 0.0)

    inside = lax.population_count(
        lax.broadcasted_iota(jnp.int32, (TILE, LANES), 0) * LANES + lax.broadcasted_iota(jnp.int32, (TILE, LANES), 1))

    def fill(b, carry):
        u, nh, n0 = lax.div(b, 8), lax.rem(lax.div(b, 2), 4), lax.rem(b, 2)
        ones = (inside + (core + u + lax.div(nh, 2) + lax.rem(nh, 2) + n0)) & 3
        amp = F32(2.0 ** -10.5)
        re = jnp.where(ones == 0, amp, jnp.where(ones == 2, -amp, 0.0))
        im = jnp.where(ones == 1, amp, jnp.where(ones == 3, -amp, 0.0))
        turns = [(re, im), (-im, re), (-re, -im), (im, -re)]
        slot = half_at(u) + nh * 2 + n0
        for t in range(GROUP):
            x, y = turns[bin(t).count("1") % len(turns)]
            B[slot, tile(TILE * t), :] = x
            B[slot + TILE, tile(TILE * t), :] = y
        return carry
    lax.fori_loop(0, HALF, fill, 0)

    @pl.when(role == 1)
    def _():
        save_copy(0, B).start()
        save_copy(0, B).wait()

    def at_row(n4, n3, h):
        return (n4 * 2 + n3) * LANES + h * GROUP

    def half_loop(turn, u, got):
        def put(blk, rows):
            def store(i, x):
                B[blk, rows[i], :] = x
            return store

        def stage1(blk, src, n4, h):
            rows = [tile(at_row(n4, n3, h) + TILE * k) for n3 in BITS for k in EIGHT]
            rot16(lambda i: B[blk, rows[i], :] if got is None else R[got, src, rows[i], :], put(blk, rows), turn)

        def stage2(blk, n4, n3):
            rows = [tile(at_row(n4, n3, 0) + TILE * k) for k in REGS]
            spots = [strided(at_row(n4, n3, h) + k) for h in BITS for k in EIGHT]
            v = {}
            rot16(lambda i: B[blk, spots[i], :], v.__setitem__, turn)
            flip = jnp.transpose(jnp.concatenate([v[i] for i in REGS], axis=0))
            rot16(lambda i: flip[TILE * i:TILE * i + TILE, :], put(blk, rows), turn)

        def stage3(blk, n3, h):
            rows = [tile(at_row(n4, n3, h) + TILE * k) for n4 in BITS for k in EIGHT]
            spots = [strided(at_row(n4, n3, h) + k) for n4 in BITS for k in EIGHT]
            rot16(lambda i: B[blk, spots[i], :], put(blk, rows), turn)

        def some(t, carry):
            first = half_at(u) + t * BATCH
            parts = [(x, y) for x in BITS for y in BITS]
            for k in range(BATCH):
                for part in parts:
                    stage1(first + k, t * BATCH + k, *part)
            for k in range(BATCH):
                for part in parts:
                    stage2(first + k, *part)
            for k in range(BATCH):
                for part in parts:
                    stage3(first + k, *part)
            return carry
        return some

    def give(blk, n0):
        return pltpu.make_async_remote_copy(
            src_ref=GA.at[cost_at(0, blk, 1 - core, n0), rows_all, :], dst_ref=GB.at[blk * 2 + n0, rows_all, :],
            send_sem=give_send.at[blk, n0], recv_sem=give_recv.at[blk, n0], device_id=partner, device_id_type=MESH)

    def table_at(slot):
        return TILE + slot * LAYERS

    def flush(form, slot, blk, u, n0):
        return pltpu.make_async_copy(
            GB.at[pl.ds(table_at(slot), LAYERS), rows_all, :], trig_ref.at[form, :, u * TILE + blk * 2 + n0], out_sem.at[slot])

    def keep_cost(form, blk, u, n0):
        at = u * TILE + blk * 2 + n0
        return pltpu.make_async_copy(GA.at[cost_at(form, blk, u, n0), rows_all, :], cost_ref.at[form, at], cost_sem.at[form, at])

    def tables(form, slot, blk, u, n0):
        state = u * HALF + blk * 2 + n0
        chunk = 32

        def body(r, carry):
            rows = pl.ds(pl.multiple_of(r * chunk, chunk), chunk)
            c = GA[cost_at(form, blk, u, n0), rows, :]
            for sub in range(LAYERS // 2):
                cs, sn = sincos((gamma_ref[angle_set, sub * 2 + form] * PER_TURN) * c)
                GB[table_at(slot) + sub * 2, rows, :] = cs
                GB[table_at(slot) + sub * 2 + 1, rows, :] = sn
                if form == 0 and sub == 0:
                    re, im = B[state, rows, :], B[state + TILE, rows, :]
                    re, im = re * cs + im * sn, im * cs - re * sn
                    for ref in (B, PB):
                        ref[state, rows, :] = re
                        ref[state + TILE, rows, :] = im
            return carry
        lax.fori_loop(0, ROWS // chunk, body, 0)
        flush(form, slot, blk, u, n0).start()
        keep_cost(form, blk, u, n0).start()

    def first_form(blk, p, slot, fresh):
        u, n0 = half_of(p), lax.rem(p, 2)

        @pl.when(p > 1)
        def _():
            give(blk, n0).start()
        if fresh:
            @pl.when(p > 1)
            def _():
                flush(0, slot, blk, u, n0).wait()
        else:
            flush(0, slot, blk, u, n0).wait()
        tables(0, slot, blk, u, n0)

    def second_form(blk, p, slot):
        u, n0 = half_of(p), lax.rem(p, 2)
        dst = cost_at(1, blk, u, n0)

        def turn_over(ref, at):
            def body(q, carry):
                spots = [q * LANES + h * GROUP + k for h in BITS for k in EIGHT]
                x = jnp.transpose(jnp.concatenate([ref[at, strided(r), :] for r in spots], axis=0))
                for i, r in enumerate(spots):
                    GA[dst, strided(r), :] = x[TILE * i:TILE * i + TILE, :]
                return carry
            lax.fori_loop(0, 4, body, 0)

        @pl.when(p < 2)
        def _():
            turn_over(GA, cost_at(0, blk, core, n0))

        @pl.when(p > 1)
        def _():
            give(blk, n0).wait()
            turn_over(GB, blk * 2 + n0)
        flush(1, slot, blk, u, n0).wait()
        tables(1, slot, blk, u, n0)

    def first_piece(k, ri):
        at = ri * TILE + jnp.bitwise_xor(chip, k) * 2
        return pltpu.make_async_remote_copy(
            src_ref=B.at[pl.ds(half_at(1 - core) + at, 2), rows_all, :], dst_ref=R.at[0, pl.ds(at, 2), rows_all, :],
            send_sem=first_send.at[k, ri], recv_sem=first_recv.at[k, ri], device_id=partner, device_id_type=MESH)

    def own_second(blk):
        def step(p, carry):
            second_form(blk, p, lax.rem(p, 2))
            return carry
        lax.fori_loop(0, 4, step, 0)

    def gather(k):
        @pl.when(k == 0)
        def _():
            def step(p, carry):
                first_form(chip, p, lax.rem(p, 2), True)
                return carry
            lax.fori_loop(0, 4, step, 0)

        @pl.when(k == 1)
        def _():
            own_second(chip)

            def step(p, carry):
                def near(d, cr):
                    from_near(d, p).wait_recv()

                    @pl.when(lax.div(p, 2) == d)
                    def _():
                        pass_on(d, p).start()
                    first_form(jnp.bitwise_xor(chip, 1 + d), p, d, False)
                    return cr
                lax.fori_loop(0, 2, near, 0)
                low = lax.rem(p, 2) * (1 - lax.div(p, 2))
                none = (1 - lax.rem(p, 2)) * (1 - lax.div(p, 2))

                def second(i, cr):
                    d = lax.rem(i, 2)
                    second_form(jnp.bitwise_xor(chip, 1 + d), lax.div(i, 2), d)
                    return cr
                lax.fori_loop(2 * (p - low), 2 * (p + 1 - none), second, 0)
                return carry
            lax.fori_loop(0, 4, step, 0)

        @pl.when(k == 3)
        def _():
            def step(i, carry):
                p = lax.rem(i, 2) * 2 + lax.div(i, 2)
                from_far(p).wait_recv()
                first_form(jnp.bitwise_xor(chip, 3), p, lax.rem(i, 2), False)
                return carry
            lax.fori_loop(0, 4, step, 0)
        turn = turn_of(0)

        def pre_pair(j, carry):
            for q in four:
                row = tile(pl.multiple_of(j * (4 * TILE), TILE) + q * TILE)
                for ri in BITS:
                    at = [u * HALF + ri * TILE + jnp.bitwise_xor(chip, k) * 2 + n0 for n0 in BITS for u in BITS]
                    at = [at[0], at[2], at[1], at[3]]
                    for i, x in zip(at, pair4(*[B[i, row, :] for i in at], turn)):
                        B[i, row, :] = x
            return carry
        lax.fori_loop(0, ROWS // (4 * TILE), pre_pair, 0)
        for ri in BITS:
            first_piece(k, ri).start()

    def gathered():
        own_second(jnp.bitwise_xor(chip, 3))

        def sent(p, carry):
            for d in BITS:
                push_own(d, p).wait_send()
            pass_on(0, p).wait_send()
            return carry
        lax.fori_loop(0, 4, sent, 0)
        for slot in BITS:
            flush(0, slot, 0, 0, 0).wait()

        def kept(t, carry):
            for form in BITS:
                keep_cost(form, lax.div(t, 4), lax.div(lax.rem(t, 4), 2), lax.rem(t, 2)).wait()
            return carry
        lax.fori_loop(0, HALF, kept, 0)
        trig_copy(1).start()
        cost_copy(0).start()

        @pl.when(role == 0)
        def _():
            save_copy(0).start()
        for k in four:
            for ri in BITS:
                first_piece(k, ri).wait()

    def body_loop(step):
        turn = turn_of(step)
        par = lax.rem(step, 2)
        stay, come = half_loop(turn, core, None), half_loop(turn, 1 - core, par)

        def part(k, carry):
            @pl.when(step == 0)
            def _():
                gather(k)
            return lax.fori_loop(0, 2, lambda ri, c: stay(ri * 4 + jnp.bitwise_xor(chip, k), c), carry)
        lax.fori_loop(0, 4, part, 0)

        @pl.when(step == 0)
        def _():
            gathered()

        @pl.when(step > 0)
        def _():
            def wait(j, carry):
                piece(par, j).wait()
                return carry
            lax.fori_loop(0, PIECES, wait, 0)
        lax.fori_loop(0, HALF // BATCH, come, 0)

    def sweep(step, unit, init, send):
        par = lax.rem(step, 2)

        def body(j, carry):
            def some(t, cr):
                row = pl.multiple_of(j * SPAN + t * (UNROLL * TILE), TILE)
                group = lax.div(row, GROUP)
                spot = group * GROUP + lax.div(row - group * GROUP, TILE)
                for k in range(UNROLL):
                    cr = unit(spot + k, row + k * TILE, cr)
                return cr
            carry = lax.fori_loop(0, SPAN // (TILE * UNROLL), some, carry)
            if send:
                @pl.when(j > 0)
                def _():
                    piece(par, j - 1).start()
            return carry
        carry = lax.fori_loop(0, PIECES, body, init)
        if send:
            piece(par, PIECES - 1).start()
        return carry

    zero = spread(0.0)

    def forward(step):
        k = step
        c0 = post_of(step - 1)
        c1 = turn_of(step)
        trig_copy(k).wait()

        @pl.when(k > 1)
        def _():
            save_copy(k - 1).wait()

        @pl.when(k == 1)
        def _():
            @pl.when(role == 0)
            def _():
                save_copy(0).wait()

        def unit(keep_before):
            def f(spot, row, carry):
                v = ({}, {})
                for groups in post_pairs:
                    both = [posted(get(ri, row), groups, c0) for ri in BITS]
                    for (i, x), (_, y) in zip(*both):
                        cs, sn = TB[0, amp_at(i), tile(row), :], TB[1, amp_at(i), tile(row), :]
                        v[0][i], v[1][i] = x * cs + y * sn, y * cs - x * sn
                        PB[pair_at(i, 0), tile(row), :] = x if keep_before else v[0][i]
                        PB[pair_at(i, 1), tile(row), :] = y if keep_before else v[1][i]
                for group in pre_groups:
                    for ri in BITS:
                        for i, x in zip(group, pair4(*[v[ri][i] for i in group], c1)):
                            B[pair_at(i, ri), tile(row), :] = x
                return carry
            return f

        for r in BITS:
            @pl.when(role == r)
            def _():
                sweep(step, unit(r == 1), 0, True)
        save_copy(k).start()

        @pl.when(k < LAYERS - 1)
        def _():
            trig_copy(k + 1).start()

    def generator(swap):
        def body(t, carry):
            for ri in BITS:
                b = t + HALF * ri
                for q in BITS:
                    for p in BITS:
                        spots = [strided(at_row(q, p, h) + k) for h in BITS for k in EIGHT]
                        g = gen_sums(lambda i: PB[b, spots[i], :])
                        for k in REGS:
                            GA[b, tile(at_row(q, p, 0) + TILE * k), :] = g(k)
                for held in BITS:
                    for h in BITS:
                        rows = [tile((at_row(e, held, h) if swap else at_row(held, e, h)) + TILE * k) for e in BITS for k in EIGHT]
                        g = gen_sums(lambda i: PB[b, rows[i], :])
                        for k in REGS:
                            GB[b, rows[k], :] = g(k)
            return carry
        lax.fori_loop(0, HALF, body, 0)

    def generated(i, ri, spot, row):
        return GA[pair_at(i, ri), strided(spot), :] + GB[pair_at(i, ri), tile(row), :]

    def beta_u(lam, psi, group, ri, spot, row):
        terms = []
        for k, i in enumerate(group):
            g = generated(i, ri, spot, row)
            terms.append(lam[k] * (g + psi[k - 1] if i & U else g - psi[k + 1]))
        return tree_sum(terms)

    def store_pre(ri, row, group, v, angles):
        for i, x in zip(group, pair4(*v, angles)):
            B[pair_at(i, ri), tile(row), :] = x

    def turn(step):
        c0 = post_of(step - 1)
        c1 = turn_of(step)
        save_copy(LAYERS - 1).wait()
        cost_copy(0).wait()

        def only_energy(spot, row, acc):
            for ri in BITS:
                v = {}
                for groups in post_pairs:
                    terms = []
                    for i, x in posted(get(ri, row), groups, c0):
                        v[i] = CB[amp_at(i), tile(row), :] * x
                        terms.append(v[i] * x)
                    acc = acc + tree_sum(terms)
                for group in pre_groups:
                    store_pre(ri, row, group, [v[i] for i in group], c1)
            return acc

        def keep(spot, row, acc):
            for ri in BITS:
                for groups in post_pairs:
                    for i, x in posted(get(ri, row), groups, c0):
                        PB[pair_at(i, ri), tile(row), :] = x
            return acc

        def with_beta(spot, row, acc):
            for ri in BITS:
                for group in pre_groups:
                    psi = [PB[pair_at(i, ri), tile(row), :] for i in group]
                    lam = [CB[amp_at(i), tile(row), :] * x for i, x in zip(group, psi)]
                    acc = acc + beta_u(lam, psi, group, ri, spot, row)
                    store_pre(ri, row, group, lam, c1)
            return acc

        @pl.when(role == 0)
        def _():
            acc_ref[0] = sweep(step, only_energy, zero, True)

        @pl.when(role == 1)
        def _():
            sweep(step, keep, 0, False)
            generator(True)
            acc_ref[2 * LAYERS] = sweep(step, with_beta, zero, True)
        load_copy(LAYERS - 1).start()
        trig_copy(LAYERS - 1).start()
        cost_copy(LAYERS - 1).start()

    def backward(step, layer, last):
        c0 = post_of(step - 1)
        c1 = None if last else turn_of(step)
        trig_copy(layer).wait()
        cost_copy(layer).wait()
        load_copy(layer).wait()

        def un_phase(i, x, y, row):
            cs, sn = TB[0, amp_at(i), tile(row), :], TB[1, amp_at(i), tile(row), :]
            return x * cs - y * sn, y * cs + x * sn

        def beta_after(spot, row, acc):
            for ri in BITS:
                g = gen_sums(lambda i: PB[pair_at(i, ri), tile(row), :])
                for groups in post_pairs:
                    lam = posted(get(ri, row), groups, c0)
                    acc = acc + tree_sum([x * (generated(i, ri, spot, row) + g(i)) for i, x in lam])
                    if not last:
                        for i, x in lam:
                            B[pair_at(i, ri), tile(row), :] = x
            return acc

        def to_before(spot, row, acc):
            for group in pre_groups:
                lam = [un_phase(i, get(0, row)(i), get(1, row)(i), row) for i in group]
                for ri in BITS:
                    store_pre(ri, row, group, [x[ri] for x in lam], c1)
            return acc

        def to_phase(spot, row, acc):
            for groups in post_pairs:
                both = [posted(get(ri, row), groups, c0) for ri in BITS]
                for (i, x), (_, y) in zip(*both):
                    for ri, z in enumerate(un_phase(i, x, y, row)):
                        B[pair_at(i, ri), tile(row), :] = z
            return acc

        def sums_before(spot, row, acc):
            acc_g, acc_b = acc
            for group in pre_groups:
                psi = [[PB[pair_at(i, ri), tile(row), :] for i in group] for ri in BITS]
                lam = [[get(ri, row)(i) for i in group] for ri in BITS]
                acc_g = acc_g + tree_sum([
                    CB[amp_at(i), tile(row), :] * (lam[0][k] * psi[1][k] - lam[1][k] * psi[0][k]) for k, i in enumerate(group)])
                if not last:
                    for ri in BITS:
                        acc_b = acc_b + beta_u(lam[ri], psi[ri], group, ri, spot, row)
                        store_pre(ri, row, group, lam[ri], c1)
            return acc_g, acc_b

        @pl.when(role == 0)
        def _():
            generator(False)
            acc_ref[1 + LAYERS + layer] = sweep(step, beta_after, zero, False)
            if not last:
                sweep(step, to_before, 0, True)

        @pl.when(role == 1)
        def _():
            if not last:
                generator(True)
            sweep(step, to_phase, 0, False)
            acc_g, acc_b = sweep(step, sums_before, (zero, zero), not last)
            acc_ref[1 + layer] = acc_g + acc_g
            if not last:
                acc_ref[LAYERS + layer] = acc_b
        if not last:
            load_copy(layer - 1).start()
            trig_copy(layer - 1).start()
            cost_copy(layer - 1).start()

    acc_ref[...] = jnp.zeros_like(acc_ref)

    def layer_loop(step, carry):
        @pl.when(lax.rem(step + LAYERS, 2 * LAYERS) > LAYERS)
        def _():
            forward(step)

        @pl.when(step == LAYERS)
        def _():
            turn(step)

        @pl.when(step > LAYERS)
        def _():
            backward(step, 2 * LAYERS - step, False)
        body_loop(step)
        return carry
    lax.fori_loop(0, 2 * LAYERS, layer_loop, 0)
    backward(2 * LAYERS, 0, True)

    all_ref[me] = jnp.sum(acc_ref[...], axis=1)
    copies = [pltpu.make_async_remote_copy(
        src_ref=all_ref.at[me], dst_ref=all_ref.at[me], send_sem=fin_send.at[k], recv_sem=fin_recv.at[k],
        device_id=peer(k), device_id_type=MESH) for k in devices]
    for cp in copies:
        cp.start()
    for cp in copies:
        cp.wait()
    row = lax.broadcasted_iota(jnp.int32, (HALF, LANES), 0)
    lane = lax.broadcasted_iota(jnp.int32, (HALF, LANES), 1)
    lines = []
    for k in BITS:
        total = (all_ref[2 * k] + all_ref[2 * k + 1]) + (all_ref[2 * k + 4] + all_ref[2 * k + 5])
        total = jnp.broadcast_to(jnp.sum(total, axis=1, keepdims=True), (HALF, LANES))
        lines.append(jnp.sum(jnp.where(row == lane + 1, total, 0.0), axis=0, keepdims=True))
        energy_ref[k, :] = total[0, :]
    grad_ref[...] = jnp.concatenate(lines, axis=0)[:, :2 * LAYERS]


def solution(mesh):
    def device_fn(cost, gamma, beta):
        any_space = pl.BlockSpec(memory_space=pl.ANY)
        smem = pl.BlockSpec(memory_space=pltpu.SMEM)
        in_vmem = pl.BlockSpec(memory_space=pltpu.VMEM)
        dma = pltpu.SemaphoreType.DMA
        vmem = pltpu.VMEM

        def padded(*shape):
            return vmem((*shape, ROWS + TILE, LANES), F32)

        def out(*shape):
            return jax.ShapeDtypeStruct(shape, F32)

        four = dma((4,))
        four_two = dma((4, 2))
        two_four = dma((2, 4))
        energy, grad, *_ = pl.pallas_call(
            main_kernel,
            out_shape=(out(2, LANES), out(2, 2 * LAYERS), out(LAYERS, *PAIRS), out(2, *AMPS), out(2, LAYERS, *AMPS)),
            in_specs=[smem, smem, any_space], out_specs=(in_vmem, in_vmem, any_space, any_space, any_space),
            scratch_shapes=[
                padded(2 * HALF), padded(2, HALF), padded(2, HALF), padded(2 * HALF), padded(HALF), padded(2 * HALF), padded(2 * HALF),
                vmem((5, 2 * LAYERS + 1, TILE, LANES), F32), vmem((HALF, TILE, LANES), F32), vmem((TILE, HALF, LANES), F32),
                dma((PIECES,)), dma((2, PIECES)), four, dma((8,)), dma((8,)),
                two_four, four, two_four, four, four_two, four_two, four_two, four_two, dma((2,)), dma((2, HALF))],
            compiler_params=pltpu.CompilerParams(collective_id=0, has_side_effects=True, vmem_limit_bytes=63 * 2 ** 20),
            name="chain",
        )(gamma, beta, cost.reshape(4, ROWS, LANES))
        return energy[:, 0], grad

    spec = P("inst", None)
    return jax.shard_map(device_fn, mesh=mesh, in_specs=(P(("inst", "qy", "qx")), spec, spec), out_specs=(P("inst"), spec), check_vma=False)
```

time: 234 us -> 226 us (0.966)
  Pallas kernels: 230 us -> 223 us
    pallas_call x1 -> x0, Pallas kernels: 49.3 us -> none  [device_fn(): pl.pallas_call(prep_kernel, out_shape=(out(2, *AMPS), out(2, 3, 2, *AMPS)...]
    pallas_call x1, Pallas kernels: 181 us -> 223 us  [device_fn(): pl.pallas_call(main_kernel, out_shape=(out(2, LANES), out(2, 2 * LAYERS),...]
where the time goes in v5:
time: 226 us
  Pallas kernels  223 us (99%)
  local copies, waits for them, and re-layouts  2.43 us (1%)
    pallas_call x1, Pallas kernels, device_fn(): pl.pallas_call(main_kernel, out_shape=(out(2, LANES), out(2, 2 * LAYERS),...  223 us

profile of v5, /device:TPU:0, one launch (start us, length us, event | category | flops | bytes accessed | tf_op | source)
XLA Modules:
  0.0 225.9 jit_solution(16531589042198376083)
XLA Ops:
  0.6 222.8 %chain.1 = (f32[2,128]{1,0:T(2,128)}, f32[2,12]{1,0:T(2,128)}, f32[6,32,512,128]{3,2,1,0:T(8,128)}, f32[2,16,512,128]{3,2,1,0:T(8,128)}, f32[2,6,16,512,128]{4,3,2,1,0:T(8,128)}) custom-call(f32[2,6]{1,0:T(2,128)} %gamma_ref.1, f32[2,6]{1,0:T(2,128)} %beta_ref.1, f32[4,512,128]{2,1,0:T(8,128)} %bitcast.1), custom_call_target="tpu_custom_call" | custom-call | tf_op jit(solution)/shard_map/chain/pallas_call | solution.py:761
  223.5 1.2 slice_reduce_fusion
  224.7 1.2 copy.6

commit v6 on v5

v6 whole, which is shorter than its diff:
```python
import functools
import jax
import jax.numpy as jnp
from jax import lax
from jax.experimental import pallas as pl
from jax.experimental.pallas import tpu as pltpu
from jax.sharding import PartitionSpec as P

F32 = jnp.float32
MESH = pl.DeviceIdType.MESH
TILE, GROUP, LANES, ROWS = 8, 64, 128, 512
HALF = 16
AMPS = (TILE, 2, ROWS, LANES)
PAIRS = (HALF, 2, ROWS, LANES)
BITS = range(2)
EIGHT = range(TILE)
REGS = range(HALF)
N0, U, N1, N2 = 1, 2, 4, 8
LAYERS = 6


def pair4(a00, a01, a10, a11, turn):
    tan, cos2, cossin = turn
    w = (a11 - a00) + tan * (a01 + a10)
    cw = cos2 * w
    sw = cossin * w
    return a11 - cw, a01 - sw, a10 - sw, a00 + cw


def rot16(load, store, turn):
    v = []
    for g in range(N1):
        v += pair4(*[load(N1 * g + k) for k in range(N1)], turn)
    for k in range(N1):
        at = [N1 * g + k for g in range(N1)]
        for i, x in zip(at, pair4(*[v[i] for i in at], turn)):
            store(i, x)


def gen_sums(load):
    four = range(N1)
    last = N1 - 1
    v, lo = [], []
    for h in four:
        v += [load(N1 * h + k) for k in four]
        lo.append((v[N1 * h + 1] + v[N1 * h + U], v[N1 * h] - v[N1 * h + last]))
    hi = [(v[N1 + k] + v[N2 + k], v[k] - v[N1 * last + k]) for k in four]

    def value(i):
        h, k = i // N1, i % N1
        x, y = lo[h][k in (1, U)], hi[k][h in (1, U)]
        if k == 0:
            return -(x + y) if h == 0 else y - x
        return x - y if h == 0 else x + y
    return value


def tree_sum(terms):
    terms = list(terms)
    while len(terms) > 1:
        rest = terms[len(terms) // 2 * 2:]
        terms = [x + y for x, y in zip(terms[::2], terms[1::2])] + rest
    return terms[0]


def tile(start):
    return pl.ds(start, TILE)


def strided(start):
    return pl.ds(start, TILE, stride=TILE)


def spread(x):
    return jnp.full((TILE, LANES), x, F32)


def poly(coefs, z):
    acc = coefs[-1]
    for c in coefs[-2::-1]:
        acc = acc * z + c
    return acc


SIN_HALF = (4.442882834149774, -7.308241154537804, 3.6062889581019757, -0.8457635954863518, 0.10920575246185597)
COS_HALF = (1.41421356206289, -6.978864110095999, 5.73988154593808, -1.8882749991429137, 0.33225188199103406, -0.03450216718833275)
PER_TURN = 0.15915494309189535


def sincos(turns):
    f = turns - jnp.round(turns)
    z = f * f
    sn = poly(SIN_HALF, z) * f
    return 1.0 - sn * sn, sn * poly(COS_HALF, z)


PIECES = 8
SPAN = ROWS // PIECES
UNROLL = 2
BATCH = 2
TAN, COS2, COSSIN, COS, SIN = range(5)


def main_kernel(gamma_ref, beta_ref, own_ref, energy_ref, grad_ref, save_ref, cost_ref, trig_ref,
                B, R, TB, PB, CB, GA, GB, ang, acc_ref, all_ref, send_sem, recv_sem, loc_sem, fin_send, fin_recv,
                near_send, pass_send, near_recv, far_recv, give_send, give_recv, first_send, first_recv, out_sem, cost_sem):
    inst = lax.axis_index("inst")
    role = lax.axis_index("qy")
    qx = lax.axis_index("qx")
    core = lax.rem(qx, 2)
    angle_set = lax.div(qx, 2)
    chip = role * 2 + angle_set
    partner = (inst, role, qx + 1 - 2 * core)

    def neighbour(d):
        return (inst, jnp.bitwise_xor(role, d), jnp.bitwise_xor(qx, 2 - 2 * d))

    me = role * 4 + qx
    rows_all = pl.ds(0, ROWS)
    four = range(4)

    def cost_at(form, blk, u, n0):
        return form * TILE + blk * 2 + u, n0

    own = pltpu.make_async_copy(own_ref, GA.at[pl.ds(chip * 2, 2), :, rows_all, :], loc_sem.at[0])
    own.start()

    devices = range(1, 8)

    def peer(k):
        return (inst, jnp.bitwise_xor(role, k // 4), jnp.bitwise_xor(qx, k % 4))

    barrier = pltpu.get_barrier_semaphore()
    for k in devices:
        pl.semaphore_signal(barrier, inc=1, device_id=peer(k), device_id_type=MESH)
    for k in range(LAYERS):
        cs, sn = sincos(spread(beta_ref[angle_set, k] * (0.5 * PER_TURN)))
        for at, sine in ((k, sn), (2 * LAYERS - 1 - k, -sn)):
            for where, value in ((TAN, sine / cs), (COS2, cs * cs), (COSSIN, cs * sine), (COS, cs), (SIN, sine)):
                ang[where, at] = value
    for where in (TAN, COS2, COSSIN, COS, SIN):
        ang[where, 2 * LAYERS] = spread(1.0 if where in (COS2, COS) else 0.0)

    inside = lax.population_count(
        lax.broadcasted_iota(jnp.int32, (TILE, LANES), 0) * LANES + lax.broadcasted_iota(jnp.int32, (TILE, LANES), 1))

    def fill(ref, b, carry):
        u, nh, n0 = lax.div(b, 8), lax.rem(lax.div(b, 2), 4), lax.rem(b, 2)
        ones = (inside + (core + u + lax.div(nh, 2) + lax.rem(nh, 2) + n0)) & 3
        amp = F32(2.0 ** -10.5)
        re = jnp.where(ones == 0, amp, jnp.where(ones == 2, -amp, 0.0))
        im = jnp.where(ones == 1, amp, jnp.where(ones == 3, -amp, 0.0))
        turns = [(re, im), (-im, re), (-re, -im), (im, -re)]
        slot = nh * 2 + n0
        for t in range(GROUP):
            x, y = turns[bin(t).count("1") % len(turns)]
            ref[slot, u, tile(TILE * t), :] = x
            ref[slot + TILE, u, tile(TILE * t), :] = y
        return carry
    lax.fori_loop(0, HALF, functools.partial(fill, B), 0)

    pl.semaphore_wait(barrier, len(devices))
    own.wait()

    def within(low, high, most, work):
        def body(i, carry):
            @pl.when(i >= low)
            def _():
                @pl.when(i < high)
                def _():
                    work(i)
            return carry

        @pl.when(low < high)
        def _():
            lax.fori_loop(0, most, body, 0)

    def half_of(p):
        return jnp.bitwise_xor(core, lax.div(p, 2))

    def push(blk, p, ssem, rsem, d):
        at = cost_at(0, blk, half_of(p), lax.rem(p, 2))
        return pltpu.make_async_remote_copy(
            src_ref=GA.at[*at, rows_all, :], dst_ref=GA.at[*at, rows_all, :], send_sem=ssem, recv_sem=rsem,
            device_id=neighbour(d), device_id_type=MESH)

    def push_own(d, p):
        return push(chip, p, near_send.at[d, p], near_recv.at[d, p], d)

    def from_near(d, p):
        return push(jnp.bitwise_xor(chip, 1 + d), p, near_send.at[d, p], near_recv.at[d, p], d)

    def pass_on(d, p):
        return push(jnp.bitwise_xor(chip, 1 + d), p, pass_send.at[p], far_recv.at[p], 1 - d)

    def from_far(p):
        return push(jnp.bitwise_xor(chip, 3), p, pass_send.at[p], far_recv.at[p], 0)

    def send_own(i, carry):
        push_own(lax.rem(i, 2), lax.div(i, 2)).start()
        return carry
    lax.fori_loop(0, 8, send_own, 0)

    def piece(par, j):
        rows = pl.ds(pl.multiple_of(j * SPAN, SPAN), SPAN)
        return pltpu.make_async_remote_copy(
            src_ref=B.at[:, 1 - core, rows, :], dst_ref=R.at[par, :, rows, :],
            send_sem=send_sem.at[j], recv_sem=recv_sem.at[par, j], device_id=partner, device_id_type=MESH)

    def full(ref):
        return ref.at[(slice(None),) * (len(ref.shape) - 2) + (rows_all,)]

    def trig_copy(k):
        return pltpu.make_async_copy(trig_ref.at[lax.rem(k, 2), lax.div(k, 2)], full(TB), loc_sem.at[0])

    def cost_copy(k):
        return pltpu.make_async_copy(cost_ref.at[lax.rem(k, 2)], full(CB), loc_sem.at[1])

    def save_copy(k):
        return pltpu.make_async_copy(full(PB), save_ref.at[k], loc_sem.at[2])

    def load_copy(k):
        return pltpu.make_async_copy(save_ref.at[k], full(PB), loc_sem.at[3])

    def low(i):
        return (i >> 2) * 2 + (i & 1)

    def up(i):
        return (i >> 1) & 1

    def pair_at(i, ri):
        return ri * TILE + low(i), up(i)

    def amp_at(i):
        return low(i), up(i)

    def turn_of(step):
        return tuple(ang[k, step] for k in (TAN, COS2, COSSIN))

    post_pairs = [tuple([n0 + n2 + b for b in (0, U, N1, U + N1)] for n2 in (0, N2)) for n0 in (0, N0)]
    pre_groups = [[n1 + n2 + b for b in (0, U, N0, U + N0)] for n1 in (0, N1) for n2 in (0, N2)]

    def post_of(step):
        return turn_of(step), ang[COS, step], ang[SIN, step]

    def posted(load, groups, angles):
        turn, c, s = angles
        parts = [pair4(*[load(i) for i in group], turn) for group in groups]
        out = []
        for i, k, x, y in zip(*groups, *parts):
            out += [(i, c * x - s * y), (k, s * x + c * y)]
        return out

    def get(ri, row):
        return lambda i: B[*pair_at(i, ri), tile(row), :]

    def at_row(n4, n3, h):
        return (n4 * 2 + n3) * LANES + h * GROUP

    def half_loop(turn, u, got):
        def put(blk, rows):
            def store(i, x):
                B[blk, u, rows[i], :] = x
            return store

        def stage1(blk, src, n4, h):
            rows = [tile(at_row(n4, n3, h) + TILE * k) for n3 in BITS for k in EIGHT]
            rot16(lambda i: B[blk, u, rows[i], :] if got is None else R[got, src, rows[i], :], put(blk, rows), turn)

        def stage2(blk, n4, n3):
            rows = [tile(at_row(n4, n3, 0) + TILE * k) for k in REGS]
            spots = [strided(at_row(n4, n3, h) + k) for h in BITS for k in EIGHT]
            v = {}
            rot16(lambda i: B[blk, u, spots[i], :], v.__setitem__, turn)
            flip = jnp.transpose(jnp.concatenate([v[i] for i in REGS], axis=0))
            rot16(lambda i: flip[TILE * i:TILE * i + TILE, :], put(blk, rows), turn)

        def stage3(blk, n3, h):
            rows = [tile(at_row(n4, n3, h) + TILE * k) for n4 in BITS for k in EIGHT]
            spots = [strided(at_row(n4, n3, h) + k) for n4 in BITS for k in EIGHT]
            rot16(lambda i: B[blk, u, spots[i], :], put(blk, rows), turn)

        def some(t, carry):
            first = t * BATCH
            parts = [(x, y) for x in BITS for y in BITS]
            for k in range(BATCH):
                for part in parts:
                    stage1(first + k, t * BATCH + k, *part)
            for k in range(BATCH):
                for part in parts:
                    stage2(first + k, *part)
            for k in range(BATCH):
                for part in parts:
                    stage3(first + k, *part)
            return carry
        return some

    def give(blk, n0):
        return pltpu.make_async_remote_copy(
            src_ref=GA.at[*cost_at(0, blk, 1 - core, n0), rows_all, :], dst_ref=GB.at[blk, n0, rows_all, :],
            send_sem=give_send.at[blk, n0], recv_sem=give_recv.at[blk, n0], device_id=partner, device_id_type=MESH)

    def table_at(slot):
        return 4 + slot * 3

    def flush(form, slot, blk, u, n0):
        return pltpu.make_async_copy(
            GB.at[pl.ds(table_at(slot), 3), :, rows_all, :], trig_ref.at[form, :, :, blk * 2 + n0, u], out_sem.at[slot])

    def keep_cost(form, blk, u, n0):
        at = blk * 2 + n0
        return pltpu.make_async_copy(
            GA.at[*cost_at(form, blk, u, n0), rows_all, :], cost_ref.at[form, at, u], cost_sem.at[form, at * 2 + u])

    def tables(form, slot, blk, u, n0):
        state = blk * 2 + n0
        chunk = GROUP

        def body(r, carry):
            rows = pl.ds(pl.multiple_of(r * chunk, chunk), chunk)
            c = GA[*cost_at(form, blk, u, n0), rows, :]
            for sub in range(LAYERS // 2):
                cs, sn = sincos((gamma_ref[angle_set, sub * 2 + form] * PER_TURN) * c)
                GB[table_at(slot) + sub, 0, rows, :] = cs
                GB[table_at(slot) + sub, 1, rows, :] = sn
                if form == 1 and sub == 0:
                    TB[0, state, u, rows, :] = cs
                    TB[1, state, u, rows, :] = sn
                if form == 0 and sub == 0:
                    re, im = B[state, u, rows, :], B[state + TILE, u, rows, :]
                    re, im = re * cs + im * sn, im * cs - re * sn
                    for ref in (B, PB):
                        ref[state, u, rows, :] = re
                        ref[state + TILE, u, rows, :] = im
            return carry
        lax.fori_loop(0, ROWS // chunk, body, 0)
        flush(form, slot, blk, u, n0).start()
        keep_cost(form, blk, u, n0).start()

    def first_form(blk, p, slot, fresh):
        u, n0 = half_of(p), lax.rem(p, 2)

        @pl.when(p > 1)
        def _():
            give(blk, n0).start()
        if fresh:
            @pl.when(p > 1)
            def _():
                flush(0, slot, blk, u, n0).wait()
        else:
            flush(0, slot, blk, u, n0).wait()
        tables(0, slot, blk, u, n0)

    def second_form(blk, p, slot):
        u, n0 = half_of(p), lax.rem(p, 2)
        dst = cost_at(1, blk, u, n0)

        def turn_over(ref, at):
            def body(q, carry):
                spots = [q * LANES + h * GROUP + k for h in BITS for k in EIGHT]
                x = jnp.transpose(jnp.concatenate([ref[*at, strided(r), :] for r in spots], axis=0))
                for i, r in enumerate(spots):
                    GA[*dst, strided(r), :] = x[TILE * i:TILE * i + TILE, :]
                return carry
            lax.fori_loop(0, 4, body, 0)

        @pl.when(p < 2)
        def _():
            turn_over(GA, cost_at(0, blk, core, n0))

        @pl.when(p > 1)
        def _():
            give(blk, n0).wait()
            turn_over(GB, (blk, n0))
        flush(1, slot, blk, u, n0).wait()
        tables(1, slot, blk, u, n0)

    def first_piece(k, ri):
        at = ri * TILE + jnp.bitwise_xor(chip, k) * 2
        return pltpu.make_async_remote_copy(
            src_ref=B.at[pl.ds(at, 2), 1 - core, rows_all, :], dst_ref=R.at[0, pl.ds(at, 2), rows_all, :],
            send_sem=first_send.at[k, ri], recv_sem=first_recv.at[k, ri], device_id=partner, device_id_type=MESH)

    def near_part(p, carry):
        def near(d, cr):
            from_near(d, p).wait_recv()

            @pl.when(lax.div(p, 2) == d)
            def _():
                pass_on(d, p).start()
            first_form(jnp.bitwise_xor(chip, 1 + d), p, d, False)
            return cr
        lax.fori_loop(0, 2, near, 0)
        odd, high = lax.rem(p, 2), lax.div(p, 2)

        def second(i):
            d = lax.rem(i, 2)
            second_form(jnp.bitwise_xor(chip, 1 + d), lax.div(i, 2), d)
        within(4 * high, 4 * high + 4 * odd * (1 - high) + 2 * high * (1 - odd), 6, second)
        return carry

    def far_part(i, carry):
        p = lax.rem(i, 2) * 2 + lax.div(i, 2)
        from_far(p).wait_recv()
        first_form(jnp.bitwise_xor(chip, 3), p, lax.rem(i, 2), False)

        @pl.when(i == 1)
        def _():
            def both(q, cr):
                second_form(jnp.bitwise_xor(chip, 3), 2 * q, q)
                return cr
            lax.fori_loop(0, 2, both, 0)
        return carry

    def own_part(p, carry):
        first_form(chip, p, lax.rem(p, 2), True)
        return carry

    def seconds(k):
        four_th = lax.div(k, 4)
        third = lax.rem(k, 2) * lax.div(k, 3)
        first = lax.rem(k, 2) - third

        def one(i):
            part = third * (1 + i) + four_th * 3
            second_form(jnp.bitwise_xor(chip, part), first * i + third * 3 + four_th * (1 + 2 * i), lax.rem(i, 2))
        within(0, 4 * first + 2 * third + 2 * four_th, 4, one)

    def gather(k):
        @pl.when(k == 0)
        def _():
            lax.fori_loop(0, 4, own_part, 0)

        @pl.when(k == 1)
        def _():
            lax.fori_loop(0, 4, near_part, 0)

        @pl.when(k == 3)
        def _():
            lax.fori_loop(0, 4, far_part, 0)
        turn = turn_of(0)

        def pre_pair(j, carry):
            for q in four:
                row = tile(pl.multiple_of(j * (4 * TILE), TILE) + q * TILE)
                for ri in BITS:
                    at = [(ri * TILE + jnp.bitwise_xor(chip, k) * 2 + n0, u) for n0 in BITS for u in BITS]
                    at = [at[0], at[2], at[1], at[3]]
                    for i, x in zip(at, pair4(*[B[*i, row, :] for i in at], turn)):
                        B[*i, row, :] = x
            return carry
        lax.fori_loop(0, ROWS // (4 * TILE), pre_pair, 0)
        for ri in BITS:
            first_piece(k, ri).start()

    def settle():
        def sent(p, carry):
            for d in BITS:
                push_own(d, p).wait_send()
            pass_on(0, p).wait_send()
            return carry
        lax.fori_loop(0, 4, sent, 0)
        for slot in BITS:
            flush(0, slot, 0, 0, 0).wait()

        def kept(t, carry):
            for form in BITS:
                keep_cost(form, lax.div(t, 4), lax.div(lax.rem(t, 4), 2), lax.rem(t, 2)).wait()
            return carry
        lax.fori_loop(0, HALF, kept, 0)

    def body_loop(step):
        turn = turn_of(step)
        par = lax.rem(step, 2)
        stay, come = half_loop(turn, core, None), half_loop(turn, 1 - core, par)

        def block_of(i):
            return lax.rem(i, 2) * 4 + jnp.bitwise_xor(chip, lax.div(i, 2))

        def part(k, carry):
            end = lax.div(k, 4)
            first = 1 - lax.div(step + 2 * LAYERS, 2 * LAYERS + 1)
            third = lax.rem(k, 2) * lax.div(k, 3)

            @pl.when(first == 1)
            def _():
                seconds(k)

                def wait(q):
                    for ri in BITS:
                        first_piece(q, ri).wait()
                own_now = lax.rem(k, 2) - third
                within(third + 3 * end, own_now + 3 * third + 4 * end, 4, wait)

                @pl.when(end - role == 1)
                def _():
                    save_copy(0).start()

            @pl.when((1 - first) * end == 1)
            def _():
                def wait(j, cr):
                    piece(par, j).wait()
                    return cr
                lax.fori_loop(0, PIECES, wait, 0)
            within(first * (2 * third + 6 * end), first * (2 * (lax.rem(k, 2) - third) + 6 * third) + 8 * end, 8, lambda i: come(block_of(i), 0))

            @pl.when(first * (1 - end) == 1)
            def _():
                gather(k)

            @pl.when(end == 0)
            def _():
                lax.fori_loop(0, 2, lambda i, c: stay(block_of(2 * k + i), c), 0)
            return carry
        lax.fori_loop(0, 5, part, 0)

    def sweep(step, unit, init, send):
        par = lax.rem(step, 2)

        def body(j, carry):
            def some(t, cr):
                row = pl.multiple_of(j * SPAN + t * (UNROLL * TILE), TILE)
                group = lax.div(row, GROUP)
                spot = group * GROUP + lax.div(row - group * GROUP, TILE)
                for k in range(UNROLL):
                    cr = unit(spot + k, row + k * TILE, cr)
                return cr
            carry = lax.fori_loop(0, SPAN // (TILE * UNROLL), some, carry)
            if send:
                piece(par, j).start()
            return carry
        return lax.fori_loop(0, PIECES, body, init)

    zero = spread(0.0)

    def forward(step):
        k = step
        c0 = post_of(step - 1)
        c1 = turn_of(step)

        @pl.when(k > 1)
        def _():
            trig_copy(k).wait()
            save_copy(k - 1).wait()

        @pl.when(k == 1)
        def _():
            @pl.when(role == 0)
            def _():
                save_copy(0).wait()

        def unit(keep_before):
            def f(spot, row, carry):
                v = ({}, {})
                for groups in post_pairs:
                    both = [posted(get(ri, row), groups, c0) for ri in BITS]
                    for (i, x), (_, y) in zip(*both):
                        cs, sn = TB[0, *amp_at(i), tile(row), :], TB[1, *amp_at(i), tile(row), :]
                        v[0][i], v[1][i] = x * cs + y * sn, y * cs - x * sn
                        PB[*pair_at(i, 0), tile(row), :] = x if keep_before else v[0][i]
                        PB[*pair_at(i, 1), tile(row), :] = y if keep_before else v[1][i]
                for group in pre_groups:
                    for ri in BITS:
                        for i, x in zip(group, pair4(*[v[ri][i] for i in group], c1)):
                            B[*pair_at(i, ri), tile(row), :] = x
                return carry
            return f

        for r in BITS:
            @pl.when(role == r)
            def _():
                sweep(step, unit(r == 1), 0, True)
        save_copy(k).start()

        @pl.when(k == 1)
        def _():
            settle()

        @pl.when(k < LAYERS - 1)
        def _():
            trig_copy(k + 1).start()

        @pl.when(k == LAYERS - 1)
        def _():
            cost_copy(0).start()

    def generator(swap):
        def body(t, carry):
            for ri in BITS:
                b = (ri * TILE + lax.rem(t, TILE), lax.div(t, TILE))
                for q in BITS:
                    for p in BITS:
                        spots = [strided(at_row(q, p, h) + k) for h in BITS for k in EIGHT]
                        g = gen_sums(lambda i: PB[*b, spots[i], :])
                        for k in REGS:
                            GA[*b, tile(at_row(q, p, 0) + TILE * k), :] = g(k)
                for held in BITS:
                    for h in BITS:
                        rows = [tile((at_row(e, held, h) if swap else at_row(held, e, h)) + TILE * k) for e in BITS for k in EIGHT]
                        g = gen_sums(lambda i: PB[*b, rows[i], :])
                        for k in REGS:
                            GB[*b, rows[k], :] = g(k)
            return carry
        lax.fori_loop(0, HALF, body, 0)

    def generated(i, ri, spot, row):
        return GA[*pair_at(i, ri), strided(spot), :] + GB[*pair_at(i, ri), tile(row), :]

    def beta_u(lam, psi, group, ri, spot, row):
        terms = []
        for k, i in enumerate(group):
            g = generated(i, ri, spot, row)
            terms.append(lam[k] * (g + psi[k - 1] if i & U else g - psi[k + 1]))
        return tree_sum(terms)

    def store_pre(ri, row, group, v, angles):
        for i, x in zip(group, pair4(*v, angles)):
            B[*pair_at(i, ri), tile(row), :] = x

    def before_turn(step):
        c0 = post_of(step - 1)
        save_copy(LAYERS - 1).wait()
        cost_copy(0).wait()

        def keep(spot, row, acc):
            for ri in BITS:
                for groups in post_pairs:
                    for i, x in posted(get(ri, row), groups, c0):
                        PB[*pair_at(i, ri), tile(row), :] = x
            return acc

        @pl.when(role == 1)
        def _():
            sweep(step, keep, 0, False)

    def before_backward(layer):
        trig_copy(layer).wait()
        cost_copy(layer).wait()

        @pl.when(layer + 1 - role > 0)
        def _():
            load_copy(layer).wait()

        @pl.when(role - layer == 1)
        def _():
            lax.fori_loop(0, HALF, functools.partial(fill, PB), 0)

    def turn(step):
        c0 = post_of(step - 1)
        c1 = turn_of(step)

        def only_energy(spot, row, acc):
            for ri in BITS:
                v = {}
                for groups in post_pairs:
                    terms = []
                    for i, x in posted(get(ri, row), groups, c0):
                        v[i] = CB[*amp_at(i), tile(row), :] * x
                        terms.append(v[i] * x)
                    acc = acc + tree_sum(terms)
                for group in pre_groups:
                    store_pre(ri, row, group, [v[i] for i in group], c1)
            return acc

        def with_beta(spot, row, acc):
            for ri in BITS:
                for group in pre_groups:
                    psi = [PB[*pair_at(i, ri), tile(row), :] for i in group]
                    lam = [CB[*amp_at(i), tile(row), :] * x for i, x in zip(group, psi)]
                    acc = acc + beta_u(lam, psi, group, ri, spot, row)
                    store_pre(ri, row, group, lam, c1)
            return acc

        @pl.when(role == 0)
        def _():
            acc_ref[0] = sweep(step, only_energy, zero, True)

        @pl.when(role == 1)
        def _():
            acc_ref[2 * LAYERS] = sweep(step, with_beta, zero, True)
        load_copy(LAYERS - 1).start()
        trig_copy(LAYERS - 1).start()
        cost_copy(LAYERS - 1).start()

    def backward(step, layer):
        c0 = post_of(step - 1)
        c1 = turn_of(step)

        def un_phase(i, x, y, row):
            cs, sn = TB[0, *amp_at(i), tile(row), :], TB[1, *amp_at(i), tile(row), :]
            return x * cs - y * sn, y * cs + x * sn

        def beta_after(spot, row, acc):
            for ri in BITS:
                g = gen_sums(lambda i: PB[*pair_at(i, ri), tile(row), :])
                for groups in post_pairs:
                    lam = posted(get(ri, row), groups, c0)
                    acc = acc + tree_sum([x * (generated(i, ri, spot, row) + g(i)) for i, x in lam])
                    for i, x in lam:
                        B[*pair_at(i, ri), tile(row), :] = x
            return acc

        def to_before(spot, row, acc):
            for group in pre_groups:
                lam = [un_phase(i, get(0, row)(i), get(1, row)(i), row) for i in group]
                for ri in BITS:
                    store_pre(ri, row, group, [x[ri] for x in lam], c1)
            return acc

        def to_phase(spot, row, acc):
            for groups in post_pairs:
                both = [posted(get(ri, row), groups, c0) for ri in BITS]
                for (i, x), (_, y) in zip(*both):
                    for ri, z in enumerate(un_phase(i, x, y, row)):
                        B[*pair_at(i, ri), tile(row), :] = z
            return acc

        def sums_before(spot, row, acc, last=False):
            acc_g, acc_b = acc
            for group in pre_groups:
                psi = [[PB[*pair_at(i, ri), tile(row), :] for i in group] for ri in BITS]
                lam = [[get(ri, row)(i) for i in group] for ri in BITS]
                acc_g = acc_g + tree_sum([
                    CB[*amp_at(i), tile(row), :] * (lam[0][k] * psi[1][k] - lam[1][k] * psi[0][k]) for k, i in enumerate(group)])
                if not last:
                    for ri in BITS:
                        acc_b = acc_b + beta_u(lam[ri], psi[ri], group, ri, spot, row)
                        store_pre(ri, row, group, lam[ri], c1)
            return acc_g, acc_b

        @pl.when(role == 0)
        def _():
            generator(False)
            acc_ref[1 + LAYERS + layer] = sweep(step, beta_after, zero, False)

            @pl.when(layer > 0)
            def _():
                sweep(step, to_before, 0, True)

        @pl.when(role == 1)
        def _():
            sweep(step, to_phase, 0, False)

            @pl.when(layer > 0)
            def _():
                acc_g, acc_b = sweep(step, sums_before, (zero, zero), True)
                acc_ref[1 + layer] = acc_g + acc_g
                acc_ref[LAYERS + layer] = acc_b

            @pl.when(layer == 0)
            def _():
                acc_g, _ = sweep(step, functools.partial(sums_before, last=True), (zero, zero), False)
                acc_ref[1] = acc_g + acc_g

        @pl.when(layer > 0)
        def _():
            @pl.when(layer - role > 0)
            def _():
                load_copy(layer - 1).start()
            trig_copy(layer - 1).start()
            cost_copy(layer - 1).start()

    acc_ref[...] = jnp.zeros_like(acc_ref)

    def layer_loop(step, carry):
        @pl.when(lax.rem(step + LAYERS, 2 * LAYERS) > LAYERS)
        def _():
            forward(step)

        @pl.when(step == LAYERS)
        def _():
            before_turn(step)

        @pl.when(step > LAYERS)
        def _():
            before_backward(2 * LAYERS - step)

        @pl.when(lax.div(step, LAYERS) * role == 1)
        def _():
            generator(True)

        @pl.when(step == LAYERS)
        def _():
            turn(step)

        @pl.when(step > LAYERS)
        def _():
            backward(step, 2 * LAYERS - step)

        @pl.when(step < 2 * LAYERS)
        def _():
            body_loop(step)
        return carry
    lax.fori_loop(0, 2 * LAYERS + 1, layer_loop, 0)

    all_ref[me] = jnp.sum(acc_ref[...], axis=1)
    copies = [pltpu.make_async_remote_copy(
        src_ref=all_ref.at[me], dst_ref=all_ref.at[me], send_sem=fin_send.at[k], recv_sem=fin_recv.at[k],
        device_id=peer(k), device_id_type=MESH) for k in devices]
    for cp in copies:
        cp.start()
    for cp in copies:
        cp.wait()
    row = lax.broadcasted_iota(jnp.int32, (HALF, LANES), 0)
    lane = lax.broadcasted_iota(jnp.int32, (HALF, LANES), 1)
    lines = []
    for k in BITS:
        total = (all_ref[2 * k] + all_ref[2 * k + 1]) + (all_ref[2 * k + 4] + all_ref[2 * k + 5])
        total = jnp.broadcast_to(jnp.sum(total, axis=1, keepdims=True), (HALF, LANES))
        lines.append(jnp.sum(jnp.where(row == lane + 1, total, 0.0), axis=0, keepdims=True))
        energy_ref[k, :] = total[0, :]
    grad_ref[...] = jnp.concatenate(lines, axis=0)[:, :2 * LAYERS]


def solution(mesh):
    def device_fn(cost, gamma, beta):
        any_space = pl.BlockSpec(memory_space=pl.ANY)
        smem = pl.BlockSpec(memory_space=pltpu.SMEM)
        in_vmem = pl.BlockSpec(memory_space=pltpu.VMEM)
        dma = pltpu.SemaphoreType.DMA
        vmem = pltpu.VMEM

        def padded(*shape):
            return vmem((*shape, ROWS + TILE, LANES), F32)

        def out(*shape):
            return jax.ShapeDtypeStruct(shape, F32)

        four = dma((4,))
        four_two = dma((4, 2))
        two_four = dma((2, 4))
        energy, grad, *_ = pl.pallas_call(
            main_kernel,
            out_shape=(out(2, LANES), out(2, 2 * LAYERS), out(LAYERS, *PAIRS), out(2, *AMPS), out(2, LAYERS // 2, 2, *AMPS)),
            in_specs=[smem, smem, any_space], out_specs=(in_vmem, in_vmem, any_space, any_space, any_space),
            scratch_shapes=[
                padded(HALF, 2), padded(2, HALF), padded(2, TILE, 2), padded(HALF, 2), padded(TILE, 2), padded(HALF, 2), padded(HALF, 2),
                vmem((5, 2 * LAYERS + 1, TILE, LANES), F32), vmem((HALF, TILE, LANES), F32), vmem((TILE, HALF, LANES), F32),
                dma((PIECES,)), dma((2, PIECES)), four, dma((8,)), dma((8,)),
                two_four, four, two_four, four, four_two, four_two, four_two, four_two, dma((2,)), dma((2, HALF))],
            compiler_params=pltpu.CompilerParams(collective_id=0, has_side_effects=True, vmem_limit_bytes=63 * 2 ** 20),
            name="chain",
        )(gamma, beta, cost.reshape(2, 2, ROWS, LANES))
        return energy[:, 0], grad

    spec = P("inst", None)
    return jax.shard_map(device_fn, mesh=mesh, in_specs=(P(("inst", "qy", "qx")), spec, spec), out_specs=(P("inst"), spec), check_vma=False)
```

time: 226 us -> 222 us (0.982)
  Pallas kernels: 223 us -> 219 us
    pallas_call x1, Pallas kernels: 223 us -> 219 us  [device_fn(): pl.pallas_call(main_kernel, out_shape=(out(2, LANES), out(2, 2 * LAYERS),...]
where the time goes in v6:
time: 222 us
  Pallas kernels  219 us (99%)
  local copies, waits for them, and re-layouts  2.43 us (1%)
    pallas_call x1, Pallas kernels, device_fn(): pl.pallas_call(main_kernel, out_shape=(out(2, LANES), out(2, 2 * LAYERS),...  219 us

profile of v6, /device:TPU:0, one launch (start us, length us, event | category | flops | bytes accessed | tf_op | source)
XLA Modules:
  0.0 221.6 jit_solution(4996878743402167016)
XLA Ops:
  0.6 218.5 %chain.1 = (f32[2,128]{1,0:T(2,128)}, f32[2,12]{1,0:T(2,128)}, f32[6,16,2,512,128]{4,3,2,1,0:T(8,128)}, f32[2,8,2,512,128]{4,3,2,1,0:T(8,128)}, f32[2,3,2,8,2,512,128]{6,5,4,3,2,1,0:T(8,128)}) custom-call(f32[2,6]{1,0:T(2,128)} %gamma_ref.1, f32[2,6]{1,0:T(2,128)} %beta_ref.1, f32[2,2,512,128]{3,2,1,0:T(8,128)} %bitcast.1), custom_call_target="tpu_custom_call" | custom-call | tf_op jit(solution)/shard_map/chain/pallas_call | solution.py:832
  219.2 1.2 slice_reduce_fusion
  220.4 1.2 copy.6

commit v7 on v6

--- a/solution.py
+++ b/solution.py
@@ -469,6 +469,21 @@
             return carry
         lax.fori_loop(0, HALF, kept, 0)
 
+    def next_generator(step):
+        layer = 2 * LAYERS - 1 - step
+
+        @pl.when(layer + 1 - role > 0)
+        def _():
+            load_copy(layer).wait()
+
+            @pl.when(role == 0)
+            def _():
+                generator(False)
+
+            @pl.when(role == 1)
+            def _():
+                generator(True)
+
     def body_loop(step):
         turn = turn_of(step)
         par = lax.rem(step, 2)
@@ -495,6 +510,10 @@
                 @pl.when(end - role == 1)
                 def _():
                     save_copy(0).start()
+
+            @pl.when(lax.div(step, LAYERS) * end == 1)
+            def _():
+                next_generator(step)
 
             @pl.when((1 - first) * end == 1)
             def _():
@@ -637,10 +656,6 @@
         trig_copy(layer).wait()
         cost_copy(layer).wait()
 
-        @pl.when(layer + 1 - role > 0)
-        def _():
-            load_copy(layer).wait()
-
         @pl.when(role - layer == 1)
         def _():
             lax.fori_loop(0, HALF, functools.partial(fill, PB), 0)
@@ -707,19 +722,16 @@
                     store_pre(ri, row, group, [x[ri] for x in lam], c1)
             return acc
 
-        def to_phase(spot, row, acc):
+        def sums_before(spot, row, acc, last=False):
+            acc_g, acc_b = acc
+            v = {}
             for groups in post_pairs:
                 both = [posted(get(ri, row), groups, c0) for ri in BITS]
                 for (i, x), (_, y) in zip(*both):
-                    for ri, z in enumerate(un_phase(i, x, y, row)):
-                        B[*pair_at(i, ri), tile(row), :] = z
-            return acc
-
-        def sums_before(spot, row, acc, last=False):
-            acc_g, acc_b = acc
+                    v[i] = un_phase(i, x, y, row)
             for group in pre_groups:
                 psi = [[PB[*pair_at(i, ri), tile(row), :] for i in group] for ri in BITS]
-                lam = [[get(ri, row)(i) for i in group] for ri in BITS]
+                lam = [[v[i][ri] for i in group] for ri in BITS]
                 acc_g = acc_g + tree_sum([
                     CB[*amp_at(i), tile(row), :] * (lam[0][k] * psi[1][k] - lam[1][k] * psi[0][k]) for k, i in enumerate(group)])
                 if not last:
@@ -730,7 +742,6 @@
 
         @pl.when(role == 0)
         def _():
-            generator(False)
             acc_ref[1 + LAYERS + layer] = sweep(step, beta_after, zero, False)
 
             @pl.when(layer > 0)
@@ -739,8 +750,6 @@
 
         @pl.when(role == 1)
         def _():
-            sweep(step, to_phase, 0, False)
-
             @pl.when(layer > 0)
             def _():
                 acc_g, acc_b = sweep(step, sums_before, (zero, zero), True)
@@ -775,12 +784,11 @@
         def _():
             before_backward(2 * LAYERS - step)
 
-        @pl.when(lax.div(step, LAYERS) * role == 1)
-        def _():
-            generator(True)
-
         @pl.when(step == LAYERS)
         def _():
+            @pl.when(role == 1)
+            def _():
+                generator(True)
             turn(step)
 
         @pl.when(step > LAYERS)

time: 222 us -> 219 us (0.986)
  Pallas kernels: 219 us -> 215 us
    pallas_call x1, Pallas kernels: 219 us -> 215 us  [device_fn(): pl.pallas_call(main_kernel, out_shape=(out(2, LANES), out(2, 2 * LAYERS),...]
where the time goes in v7:
time: 219 us; the launch traced here: 218 us
  Pallas kernels  215 us (98%)
  local copies, waits for them, and re-layouts  2.43 us (1%)
    pallas_call x1, Pallas kernels, device_fn(): pl.pallas_call(main_kernel, out_shape=(out(2, LANES), out(2, 2 * LAYERS),...  215 us

profile of v7, /device:TPU:0, one launch (start us, length us, event | category | flops | bytes accessed | tf_op | source)
XLA Modules:
  0.0 218.4 jit_solution(16295632687144811775)
XLA Ops:
  0.6 215.3 %chain.1 = (f32[2,128]{1,0:T(2,128)}, f32[2,12]{1,0:T(2,128)}, f32[6,16,2,512,128]{4,3,2,1,0:T(8,128)}, f32[2,8,2,512,128]{4,3,2,1,0:T(8,128)}, f32[2,3,2,8,2,512,128]{6,5,4,3,2,1,0:T(8,128)}) custom-call(f32[2,6]{1,0:T(2,128)} %gamma_ref.1, f32[2,6]{1,0:T(2,128)} %beta_ref.1, f32[2,2,512,128]{3,2,1,0:T(8,128)} %bitcast.1), custom_call_target="tpu_custom_call" | custom-call | tf_op jit(solution)/shard_map/chain/pallas_call | solution.py:840
  215.9 1.2 slice_reduce_fusion
  217.2 1.2 copy.6

commit v8 on v7

--- a/solution.py
+++ b/solution.py
@@ -314,7 +314,7 @@
 
     def tables(form, slot, blk, u, n0):
         state = blk * 2 + n0
-        chunk = GROUP
+        chunk = LANES
 
         def body(r, carry):
             rows = pl.ds(pl.multiple_of(r * chunk, chunk), chunk)
@@ -610,15 +610,12 @@
                 for q in BITS:
                     for p in BITS:
                         spots = [strided(at_row(q, p, h) + k) for h in BITS for k in EIGHT]
+                        rows = [tile((at_row(e, q, p) if swap else at_row(q, e, p)) + TILE * k) for e in BITS for k in EIGHT]
                         g = gen_sums(lambda i: PB[*b, spots[i], :])
+                        m = gen_sums(lambda i: PB[*b, rows[i], :])
                         for k in REGS:
                             GA[*b, tile(at_row(q, p, 0) + TILE * k), :] = g(k)
-                for held in BITS:
-                    for h in BITS:
-                        rows = [tile((at_row(e, held, h) if swap else at_row(held, e, h)) + TILE * k) for e in BITS for k in EIGHT]
-                        g = gen_sums(lambda i: PB[*b, rows[i], :])
-                        for k in REGS:
-                            GB[*b, rows[k], :] = g(k)
+                            GB[*b, rows[k], :] = m(k)
             return carry
         lax.fori_loop(0, HALF, body, 0)
 
@@ -711,13 +708,18 @@
                 for groups in post_pairs:
                     lam = posted(get(ri, row), groups, c0)
                     acc = acc + tree_sum([x * (generated(i, ri, spot, row) + g(i)) for i, x in lam])
-                    for i, x in lam:
-                        B[*pair_at(i, ri), tile(row), :] = x
             return acc
 
-        def to_before(spot, row, acc):
+        def beta_to_before(spot, row, acc):
+            v = ({}, {})
+            for ri in BITS:
+                g = gen_sums(lambda i: PB[*pair_at(i, ri), tile(row), :])
+                for groups in post_pairs:
+                    lam = posted(get(ri, row), groups, c0)
+                    v[ri].update(lam)
+                    acc = acc + tree_sum([x * (generated(i, ri, spot, row) + g(i)) for i, x in lam])
             for group in pre_groups:
-                lam = [un_phase(i, get(0, row)(i), get(1, row)(i), row) for i in group]
+                lam = [un_phase(i, v[0][i], v[1][i], row) for i in group]
                 for ri in BITS:
                     store_pre(ri, row, group, [x[ri] for x in lam], c1)
             return acc
@@ -742,11 +744,13 @@
 
         @pl.when(role == 0)
         def _():
-            acc_ref[1 + LAYERS + layer] = sweep(step, beta_after, zero, False)
-
             @pl.when(layer > 0)
             def _():
-                sweep(step, to_before, 0, True)
+                acc_ref[1 + LAYERS + layer] = sweep(step, beta_to_before, zero, True)
+
+            @pl.when(layer == 0)
+            def _():
+                acc_ref[1 + LAYERS] = sweep(step, beta_after, zero, False)
 
         @pl.when(role == 1)
         def _():
@@ -811,12 +815,13 @@
         cp.wait()
     row = lax.broadcasted_iota(jnp.int32, (HALF, LANES), 0)
     lane = lax.broadcasted_iota(jnp.int32, (HALF, LANES), 1)
-    lines = []
+    lines, energies = [], []
     for k in BITS:
         total = (all_ref[2 * k] + all_ref[2 * k + 1]) + (all_ref[2 * k + 4] + all_ref[2 * k + 5])
         total = jnp.broadcast_to(jnp.sum(total, axis=1, keepdims=True), (HALF, LANES))
         lines.append(jnp.sum(jnp.where(row == lane + 1, total, 0.0), axis=0, keepdims=True))
-        energy_ref[k, :] = total[0, :]
+        energies.append(total[:1, :])
+    energy_ref[...] = jnp.where(lane[:1] == 0, energies[0], energies[1])[:, :2]
     grad_ref[...] = jnp.concatenate(lines, axis=0)[:, :2 * LAYERS]
 
 
@@ -839,7 +844,7 @@
         two_four = dma((2, 4))
         energy, grad, *_ = pl.pallas_call(
             main_kernel,
-            out_shape=(out(2, LANES), out(2, 2 * LAYERS), out(LAYERS, *PAIRS), out(2, *AMPS), out(2, LAYERS // 2, 2, *AMPS)),
+            out_shape=(out(1, 2), out(2, 2 * LAYERS), out(LAYERS, *PAIRS), out(2, *AMPS), out(2, LAYERS // 2, 2, *AMPS)),
             in_specs=[smem, smem, any_space], out_specs=(in_vmem, in_vmem, any_space, any_space, any_space),
             scratch_shapes=[
                 padded(HALF, 2), padded(2, HALF), padded(2, TILE, 2), padded(HALF, 2), padded(TILE, 2), padded(HALF, 2), padded(HALF, 2),
@@ -849,7 +854,7 @@
             compiler_params=pltpu.CompilerParams(collective_id=0, has_side_effects=True, vmem_limit_bytes=63 * 2 ** 20),
             name="chain",
         )(gamma, beta, cost.reshape(2, 2, ROWS, LANES))
-        return energy[:, 0], grad
+        return energy.reshape(2), grad
 
     spec = P("inst", None)
     return jax.shard_map(device_fn, mesh=mesh, in_specs=(P(("inst", "qy", "qx")), spec, spec), out_specs=(P("inst"), spec), check_vma=False)

time: 219 us -> 217 us (level)
  no operation moved by 1% of the time
where the time goes in v8:
time: 217 us
  Pallas kernels  214 us (99%)
  local copies, waits for them, and re-layouts  2.32 us (1%)
    pallas_call x1, Pallas kernels, device_fn(): pl.pallas_call(main_kernel, out_shape=(out(1, 2), out(2, 2 * LAYERS), out...  214 us

profile of v8, /device:TPU:0, one launch (start us, length us, event | category | flops | bytes accessed | tf_op | source)
XLA Modules:
  0.0 216.8 jit_solution(2594780277833078817)
XLA Ops:
  0.6 213.8 %chain.1 = (f32[1,2]{1,0:T(1,128)}, f32[2,12]{1,0:T(2,128)}, f32[6,16,2,512,128]{4,3,2,1,0:T(8,128)}, f32[2,8,2,512,128]{4,3,2,1,0:T(8,128)}, f32[2,3,2,8,2,512,128]{6,5,4,3,2,1,0:T(8,128)}) custom-call(f32[2,6]{1,0:T(2,128)} %gamma_ref.1, f32[2,6]{1,0:T(2,128)} %beta_ref.1, f32[2,2,512,128]{3,2,1,0:T(8,128)} %bitcast.2), custom_call_target="tpu_custom_call" | custom-call | tf_op jit(solution)/shard_map/chain/pallas_call | solution.py:845
  214.4 1.1 copy.7
  215.6 1.2 copy.8
